TPU v7x, 512 devices: a whole 4x4x16 slice. The times are simulated.
512 devices in a mesh: pipe: 16 (over x_lo, y, core), expert: 32 (over z, x_hi).
Axes of the slice: x: 4 (x_hi: 2, x_lo: 2; x = x_hi * 2 + x_lo), y: 4, z: 16, core: 2. Of those that a mesh axis runs over, the one named last changes fastest.
Arguments:
- forward_tokens: bfloat16 [16, 768, 3584], P('pipe', 'expert'), may hold values from -6 to 6
- forward_routing: int32 [16, 768, 1], P('pipe', 'expert'), may hold values from 0 to 3; in each aligned block of 24 rows (0 to 23, 24 to 47, ..., all dimensions but the last counted through in order) at most 8 rows name the same one
- forward_gates: float32 [16, 768], P('pipe', 'expert'), may hold values from 0.25 to 2.5
- backward_tokens: bfloat16 [16, 768, 3584], P('pipe', 'expert'), may hold values from -6 to 6
- backward_routing: int32 [16, 768, 1], P('pipe', 'expert'), may hold values from 0 to 3; in each aligned block of 24 rows (0 to 23, 24 to 47, ..., all dimensions but the last counted through in order) at most 8 rows name the same one
- backward_gates: float32 [16, 768], P('pipe', 'expert'), may hold values from 0.25 to 2.5
- cotangent: bfloat16 [16, 768, 3584], P('pipe', 'expert'), may hold values from -6 to 6
- gate_matrix: bfloat16 [16, 3584, 4096], P('pipe', None, 'expert'), as said below
- up_matrix: bfloat16 [16, 3584, 4096], P('pipe', None, 'expert'), as said below
- down_matrix: bfloat16 [16, 4096, 3584], P('pipe', 'expert'), as said below
Outputs:
- forward_output: bfloat16 [16, 768, 3584], P('pipe', 'expert')
- input_gradient: bfloat16 [16, 768, 3584], P('pipe', 'expert')
- gate_gradient: bfloat16 [16, 1792, 4096], P('pipe', None, 'expert')
- up_gradient: bfloat16 [16, 1792, 4096], P('pipe', None, 'expert')
- down_gradient: bfloat16 [16, 4096, 1792], P('pipe', 'expert')
Inputs may be any that keep to these rules, and one draw needn't show every extreme that they name: `forward_routing`: in each device's 24 rows no expert is named more than 8 times. `backward_routing`: in each device's 24 rows no expert is named more than 8 times. `gate_matrix`: blocks p and 15 - p along the first dimension are equal. `up_matrix`: blocks p and 15 - p along the first dimension are equal. `down_matrix`: blocks p and 15 - p along the first dimension are equal.
All inputs are finite; a program needn't handle non-finite values.
Results may differ from a plain program's by a relative error of at most 0.0065.
Values may be sent and summed in bfloat16 or wider, within the bound.
No kernel may reach another device: no remote copies, remote signals or barrier semaphores. Data moves between devices by JAX's collectives and lax.ppermute only.
A program may use at most 64 MiB of HBM per device.

v0:
```python
import jax
import jax.numpy as jnp
from jax import lax
from jax.sharding import PartitionSpec as P

SHARING_CARDS = 8


def from_partner(value, axis, stride):
    mask = 2**stride
    pairs = [(source, source ^ mask) for source in range(lax.axis_size(axis))]
    return lax.ppermute(value, axis, pairs)


def slot_matrix(routing, experts, capacity):
    members = (routing[:, None] == jnp.arange(experts, dtype=jnp.int32)[None, :]).astype(jnp.int32)
    earlier = jnp.cumsum(members, axis=0) - members
    within = jnp.sum(earlier * members, axis=1)
    target = routing * capacity + within
    matches = target[None, :] == jnp.arange(experts * capacity, dtype=jnp.int32)[:, None]
    return matches.astype(jnp.bfloat16)


def spread_rows(matches, value_entries, experts, capacity):
    placed = jnp.dot(matches, value_entries, preferred_element_type=jnp.float32).astype(
        jnp.bfloat16
    )
    return jnp.repeat(
        placed.reshape(experts, capacity, value_entries.shape[1]), SHARING_CARDS, axis=0
    )


def collect_rows(received, matches, experts, capacity):
    summed = received.reshape(experts, SHARING_CARDS, capacity, -1).astype(jnp.float32).sum(axis=1)
    return jnp.dot(
        matches.astype(jnp.float32).T,
        summed.reshape(experts * capacity, -1),
        precision=lax.Precision.HIGHEST,
    )


def on_device(
    forward_tokens,
    forward_routing,
    forward_gates,
    backward_tokens,
    backward_routing,
    backward_gates,
    cotangent,
    gate_matrix,
    up_matrix,
    down_matrix,
):
    devices = lax.axis_size("expert")
    experts = devices // SHARING_CARDS
    tokens = forward_tokens.shape[1]
    width = forward_tokens.shape[2]
    capacity = max(tokens // 3, tokens // experts)
    gate_weights = gate_matrix[0]
    up_weights = up_matrix[0]
    down_weights = down_matrix[0]
    forward_inputs = forward_tokens[0]
    backward_inputs = backward_tokens[0]
    forward_experts = forward_routing[0, :, 0]
    backward_experts = backward_routing[0, :, 0]
    scaled = (backward_gates[0][:, None] * cotangent[0].astype(jnp.float32)).astype(jnp.bfloat16)
    forward_slots = slot_matrix(forward_experts, experts, capacity)
    backward_slots = slot_matrix(backward_experts, experts, capacity)
    forward_row_set = lax.all_to_all(
        spread_rows(forward_slots, forward_inputs, experts, capacity),
        "expert",
        split_axis=0,
        concat_axis=0,
        tiled=True,
    )
    backward_rows, scaled_rows = (
        lax.all_to_all(
            spread_rows(backward_slots, backward_inputs, experts, capacity),
            "expert",
            split_axis=0,
            concat_axis=0,
            tiled=True,
        ),
        lax.all_to_all(
            spread_rows(backward_slots, scaled, experts, capacity),
            "expert",
            split_axis=0,
            concat_axis=0,
            tiled=True,
        ),
    )
    flat_forward = forward_row_set.reshape(-1, width)
    forward_gate_pre = jnp.dot(flat_forward, gate_weights, preferred_element_type=jnp.float32)
    forward_up_pre = jnp.dot(flat_forward, up_weights, preferred_element_type=jnp.float32)
    forward_hidden = (jax.nn.silu(forward_gate_pre) * forward_up_pre).astype(jnp.bfloat16)
    forward_parts = jnp.dot(
        forward_hidden, down_weights, preferred_element_type=jnp.float32
    ).astype(jnp.bfloat16)
    forward_back = lax.all_to_all(
        forward_parts.reshape(devices, capacity, width),
        "expert",
        split_axis=0,
        concat_axis=0,
        tiled=True,
    )
    forward_result = (
        forward_gates[0][:, None] * collect_rows(forward_back, forward_slots, experts, capacity)
    ).astype(jnp.bfloat16)
    flat_backward = backward_rows.reshape(-1, width)
    flat_scaled = scaled_rows.reshape(-1, width)
    gate_pre = jnp.dot(flat_backward, gate_weights, preferred_element_type=jnp.float32)
    up_pre = jnp.dot(flat_backward, up_weights, preferred_element_type=jnp.float32)
    sigma = jax.nn.sigmoid(gate_pre)
    activated = gate_pre * sigma
    backward_hidden = (activated * up_pre).astype(jnp.bfloat16)
    contract_last = (((1,), (1,)), ((), ()))
    contract_first = (((0,), (0,)), ((), ()))
    hidden_grad = lax.dot_general(
        flat_scaled, down_weights, contract_last, preferred_element_type=jnp.float32
    )
    gate_grad = (hidden_grad * up_pre * sigma * (1.0 + gate_pre * (1.0 - sigma))).astype(
        jnp.bfloat16
    )
    up_grad = (hidden_grad * activated).astype(jnp.bfloat16)
    backward_parts = lax.dot_general(
        gate_grad, gate_weights, contract_last, preferred_element_type=jnp.float32
    ) + lax.dot_general(up_grad, up_weights, contract_last, preferred_element_type=jnp.float32)
    backward_back = lax.all_to_all(
        backward_parts.astype(jnp.bfloat16).reshape(devices, capacity, width),
        "expert",
        split_axis=0,
        concat_axis=0,
        tiled=True,
    )
    backward_result = collect_rows(backward_back, backward_slots, experts, capacity).astype(
        jnp.bfloat16
    )
    gate_partial = lax.dot_general(
        flat_backward, gate_grad, contract_first, preferred_element_type=jnp.float32
    ).astype(jnp.bfloat16)
    up_partial = lax.dot_general(
        flat_backward, up_grad, contract_first, preferred_element_type=jnp.float32
    ).astype(jnp.bfloat16)
    down_partial = lax.dot_general(
        backward_hidden, flat_scaled, contract_first, preferred_element_type=jnp.float32
    ).astype(jnp.bfloat16)
    positions = lax.axis_size("pipe")
    middle = width // 2
    upper_side = (lax.axis_index("pipe") >= positions // 2).astype(jnp.int32)
    own_start = upper_side * middle
    other_start = (1 - upper_side) * middle
    retained = (
        lax.dynamic_slice_in_dim(gate_partial, own_start, middle, 0),
        lax.dynamic_slice_in_dim(up_partial, own_start, middle, 0),
        lax.dynamic_slice_in_dim(down_partial, own_start, middle, 1),
    )
    outgoing = (
        lax.dynamic_slice_in_dim(gate_partial, other_start, middle, 0),
        lax.dynamic_slice_in_dim(up_partial, other_start, middle, 0),
        lax.dynamic_slice_in_dim(down_partial, other_start, middle, 1),
    )
    levels = positions.bit_length() - 1
    bit_order = list(range(levels))
    for level in bit_order:
        outgoing = from_partner((outgoing[0], outgoing[1], outgoing[2]), "pipe", level)
    gate_result = (retained[0].astype(jnp.float32) + outgoing[0].astype(jnp.float32)).astype(
        jnp.bfloat16
    )
    up_result = (retained[1].astype(jnp.float32) + outgoing[1].astype(jnp.float32)).astype(
        jnp.bfloat16
    )
    down_projected = (retained[2].astype(jnp.float32) + outgoing[2].astype(jnp.float32)).astype(
        jnp.bfloat16
    )
    return (
        forward_result[None],
        backward_result[None],
        gate_result[None],
        up_result[None],
        down_projected[None],
    )


def solution(mesh):
    in_specs = (
        P("pipe", "expert", None),
        P("pipe", "expert", None),
        P("pipe", "expert"),
        P("pipe", "expert", None),
        P("pipe", "expert", None),
        P("pipe", "expert"),
        P("pipe", "expert", None),
        P("pipe", None, "expert"),
        P("pipe", None, "expert"),
        P("pipe", "expert", None),
    )
    out_specs = (
        P("pipe", "expert", None),
        P("pipe", "expert", None),
        P("pipe", None, "expert"),
        P("pipe", None, "expert"),
        P("pipe", "expert", None),
    )
    return jax.shard_map(
        on_device, mesh=mesh, in_specs=in_specs, out_specs=out_specs, check_vma=False
    )
```

profile of v0, /device:TPU:1, one launch (start us, length us, event | category | flops | bytes accessed | tf_op | source)
XLA Modules:
  0.0 503.6 jit_solution(1225751292190271250)
XLA Ops:
  5.5 18.6 %all-to-all-start.3 = ((bf16[32,8,3584]{2,1,0:T(8,128)(2,1)}), bf16[32,8,3584]{2,1,0:T(8,128)(2,1)S(1)}, u32[]{:S(2)}, u32[]{:S(2)}) async-start(bf16[32,8,3584]{2,1,0:T(8,128)(2,1)} %bitcast.108), calls=%async_computation.3 | async-start | bytes 3670016 | tf_op jit(solution)/shard_map/all_to_all | solution.py:77
  24.5 85.0 %all-to-all-done.3 = bf16[32,8,3584]{2,1,0:T(8,128)(2,1)S(1)} async-done(((bf16[32,8,3584]{2,1,0:T(8,128)(2,1)}), bf16[32,8,3584]{2,1,0:T(8,128)(2,1)S(1)}, u32[]{:S(2)}, u32[]{:S(2)}) %all-to-all-start.3) | async-done | bytes 1835040 | tf_op jit(solution)/shard_map/all_to_all | solution.py:77
  110.8 8.5 %all-to-all-start.2 = ((bf16[32,8,3584]{2,1,0:T(8,128)(2,1)}), bf16[32,8,3584]{2,1,0:T(8,128)(2,1)}, u32[]{:S(2)}, u32[]{:S(2)}) async-start(bf16[32,8,3584]{2,1,0:T(8,128)(2,1)} %bitcast.107), calls=%async_computation.2 | async-start | bytes 3670016 | tf_op jit(solution)/shard_map/all_to_all | solution.py:84
  119.9 84.7 %all-to-all-done.2 = bf16[32,8,3584]{2,1,0:T(8,128)(2,1)} async-done(((bf16[32,8,3584]{2,1,0:T(8,128)(2,1)}), bf16[32,8,3584]{2,1,0:T(8,128)(2,1)}, u32[]{:S(2)}, u32[]{:S(2)}) %all-to-all-start.2) | async-done | bytes 1835040 | tf_op jit(solution)/shard_map/all_to_all | solution.py:84
  206.0 8.5 %all-to-all-start = ((bf16[32,8,3584]{2,1,0:T(8,128)(2,1)}), bf16[32,8,3584]{2,1,0:T(8,128)(2,1)}, u32[]{:S(2)}, u32[]{:S(2)}) async-start(bf16[32,8,3584]{2,1,0:T(8,128)(2,1)} %bitcast.106), calls=%async_computation | async-start | bytes 3670016 | tf_op jit(solution)/shard_map/all_to_all | solution.py:69
  222.4 77.4 %all-to-all-done = bf16[32,8,3584]{2,1,0:T(8,128)(2,1)} async-done(((bf16[32,8,3584]{2,1,0:T(8,128)(2,1)}), bf16[32,8,3584]{2,1,0:T(8,128)(2,1)}, u32[]{:S(2)}, u32[]{:S(2)}) %all-to-all-start) | async-done | bytes 1835040 | tf_op jit(solution)/shard_map/all_to_all | solution.py:69
  299.8 8.5 %all-to-all-start.4 = ((bf16[32,8,3584]{2,1,0:T(8,128)(2,1)}), bf16[32,8,3584]{2,1,0:T(8,128)(2,1)}, u32[]{:S(2)}, u32[]{:S(2)}) async-start(bf16[32,8,3584]{2,1,0:T(8,128)(2,1)} %fusion.2), calls=%async_computation.4 | async-start | bytes 3670016 | tf_op jit(solution)/shard_map/all_to_all | solution.py:128
  310.7 4.2 fusion.1
  314.8 78.7 %all-to-all-done.4 = bf16[32,8,3584]{2,1,0:T(8,128)(2,1)} async-done(((bf16[32,8,3584]{2,1,0:T(8,128)(2,1)}), bf16[32,8,3584]{2,1,0:T(8,128)(2,1)}, u32[]{:S(2)}, u32[]{:S(2)}) %all-to-all-start.4) | async-done | bytes 1835040 | tf_op jit(solution)/shard_map/all_to_all | solution.py:128
  393.6 8.5 %all-to-all-start.1 = ((bf16[32,8,3584]{2,1,0:T(8,128)(2,1)}), bf16[32,8,3584]{2,1,0:T(8,128)(2,1)}, u32[]{:S(2)}, u32[]{:S(2)}) async-start(bf16[32,8,3584]{2,1,0:T(8,128)(2,1)} %fusion.1), calls=%async_computation.1 | async-start | bytes 3670016 | tf_op jit(solution)/shard_map/all_to_all | solution.py:99
  402.8 3.3 collective-permute-start.4
  413.4 3.2 collective-permute-start.5
  418.7 3.2 collective-permute-start.9
  421.9 5.6 %collective-permute-done.5 = bf16[1792,128]{1,0:T(8,128)(2,1)S(1)} collective-permute-done((bf16[1792,128]{1,0:T(8,128)(2,1)S(1)}, bf16[1792,128]{1,0:T(8,128)(2,1)S(1)}, u32[]{:S(2)}, u32[]{:S(2)}) %collective-permute-start.5) | collective-permute-done | bytes 458784 | tf_op jit(solution)/shard_map/ppermute | solution.py:12
  427.5 4.8 collective-permute-start.6
  432.4 5.0 collective-permute-done.1
  437.4 4.8 collective-permute-start.2
  442.2 5.0 collective-permute-done.9
  447.2 4.8 collective-permute-start.10
  452.0 7.5 %collective-permute-done.6 = bf16[1792,128]{1,0:T(8,128)(2,1)} collective-permute-done((bf16[1792,128]{1,0:T(8,128)(2,1)S(1)}, bf16[1792,128]{1,0:T(8,128)(2,1)}, u32[]{:S(2)}, u32[]{:S(2)}) %collective-permute-start.6) | collective-permute-done | bytes 458784 | tf_op jit(solution)/shard_map/ppermute | solution.py:12
  461.7 7.6 %collective-permute-done.2 = bf16[1792,128]{1,0:T(8,128)(2,1)} collective-permute-done((bf16[1792,128]{1,0:T(8,128)(2,1)}, bf16[1792,128]{1,0:T(8,128)(2,1)}, u32[]{:S(2)}, u32[]{:S(2)}) %collective-permute-start.2) | collective-permute-done | bytes 458784 | tf_op jit(solution)/shard_map/ppermute | solution.py:12
  471.5 7.6 %collective-permute-done.10 = bf16[128,1792]{1,0:T(8,128)(2,1)} collective-permute-done((bf16[128,1792]{1,0:T(8,128)(2,1)}, bf16[128,1792]{1,0:T(8,128)(2,1)}, u32[]{:S(2)}, u32[]{:S(2)}) %collective-permute-start.10) | collective-permute-done | bytes 458784 | tf_op jit(solution)/shard_map/ppermute | solution.py:12
  482.3 5.1 %collective-permute-done.3 = bf16[1792,128]{1,0:T(8,128)(2,1)S(1)} collective-permute-done((bf16[1792,128]{1,0:T(8,128)(2,1)}, bf16[1792,128]{1,0:T(8,128)(2,1)S(1)}, u32[]{:S(2)}, u32[]{:S(2)}) %collective-permute-start.3) | collective-permute-done | bytes 458784 | tf_op jit(solution)/shard_map/ppermute | solution.py:12
  489.3 7.8 %collective-permute-done.11 = bf16[128,1792]{1,0:T(8,128)(2,1)S(1)} collective-permute-done((bf16[128,1792]{1,0:T(8,128)(2,1)}, bf16[128,1792]{1,0:T(8,128)(2,1)S(1)}, u32[]{:S(2)}, u32[]{:S(2)}) %collective-permute-start.11) | collective-permute-done | bytes 458784 | tf_op jit(solution)/shard_map/ppermute | solution.py:12
  (66 shorter events, 44.6 us)
Async XLA Ops:
  0.6 215.7 %copy-start = (bf16[1,3584,128]{2,1,0:T(8,128)(2,1)S(1)}, bf16[1,3584,128]{2,1,0:T(8,128)(2,1)}, u32[]{:S(2)}) copy-start(bf16[1,3584,128]{2,1,0:T(8,128)(2,1)} %param.18) | copy-start | bytes 2752516
  5.5 18.6 %copy-start.6 = (bf16[1,24,3584]{2,1,0:T(8,128)(2,1)S(1)}, bf16[1,24,3584]{2,1,0:T(8,128)(2,1)}, u32[]{:S(2)}) copy-start(bf16[1,24,3584]{2,1,0:T(8,128)(2,1)} %param.16) | copy-start | bytes 516100
  5.5 18.6 %copy-start.9 = (f32[1,24]{1,0:T(1,128)S(1)}, f32[1,24]{1,0:T(1,128)}, u32[]{:S(2)}) copy-start(f32[1,24]{1,0:T(1,128)} %param.15) | copy-start | bytes 292
  5.5 103.9 %all-to-all-start.3 = ((bf16[32,8,3584]{2,1,0:T(8,128)(2,1)}), bf16[32,8,3584]{2,1,0:T(8,128)(2,1)S(1)}, u32[]{:S(2)}, u32[]{:S(2)}) async-start(bf16[32,8,3584]{2,1,0:T(8,128)(2,1)} %bitcast.108), calls=%async_computation.3 | async-start | bytes 3670016 | tf_op jit(solution)/shard_map/all_to_all | solution.py:77
  110.8 8.5 %copy-start.8 = (s32[1,24,1]{1,2,0:T(1,128)S(1)}, s32[1,24,1]{1,2,0:T(1,128)}, u32[]{:S(2)}) copy-start(s32[1,24,1]{1,2,0:T(1,128)} %param.11) | copy-start | bytes 292
  110.8 8.9 %copy-start.7 = (bf16[1,24,3584]{2,1,0:T(8,128)(2,1)S(1)}, bf16[1,24,3584]{2,1,0:T(8,128)(2,1)}, u32[]{:S(2)}) copy-start(bf16[1,24,3584]{2,1,0:T(8,128)(2,1)} %param.10) | copy-start | bytes 516100
  110.8 93.8 %all-to-all-start.2 = ((bf16[32,8,3584]{2,1,0:T(8,128)(2,1)}), bf16[32,8,3584]{2,1,0:T(8,128)(2,1)}, u32[]{:S(2)}, u32[]{:S(2)}) async-start(bf16[32,8,3584]{2,1,0:T(8,128)(2,1)} %bitcast.107), calls=%async_computation.2 | async-start | bytes 3670016 | tf_op jit(solution)/shard_map/all_to_all | solution.py:84
  206.0 93.8 %all-to-all-start = ((bf16[32,8,3584]{2,1,0:T(8,128)(2,1)}), bf16[32,8,3584]{2,1,0:T(8,128)(2,1)}, u32[]{:S(2)}, u32[]{:S(2)}) async-start(bf16[32,8,3584]{2,1,0:T(8,128)(2,1)} %bitcast.106), calls=%async_computation | async-start | bytes 3670016 | tf_op jit(solution)/shard_map/all_to_all | solution.py:69
  299.8 93.8 %all-to-all-start.4 = ((bf16[32,8,3584]{2,1,0:T(8,128)(2,1)}), bf16[32,8,3584]{2,1,0:T(8,128)(2,1)}, u32[]{:S(2)}, u32[]{:S(2)}) async-start(bf16[32,8,3584]{2,1,0:T(8,128)(2,1)} %fusion.2), calls=%async_computation.4 | async-start | bytes 3670016 | tf_op jit(solution)/shard_map/all_to_all | solution.py:128
  393.6 107.2 %all-to-all-start.1 = ((bf16[32,8,3584]{2,1,0:T(8,128)(2,1)}), bf16[32,8,3584]{2,1,0:T(8,128)(2,1)}, u32[]{:S(2)}, u32[]{:S(2)}) async-start(bf16[32,8,3584]{2,1,0:T(8,128)(2,1)} %fusion.1), calls=%async_computation.1 | async-start | bytes 3670016 | tf_op jit(solution)/shard_map/all_to_all | solution.py:99
  402.8 10.6 %collective-permute-start.4 = (bf16[1792,128]{1,0:T(8,128)(2,1)S(1)}, bf16[1792,128]{1,0:T(8,128)(2,1)S(1)}, u32[]{:S(2)}, u32[]{:S(2)}) collective-permute-start(bf16[1792,128]{1,0:T(8,128)(2,1)S(1)} %constant_dynamic-slice_fusion), channel_id=1, source_target_pairs={{0,32},{32,0},{64,96},{96,64},{128,160},{160,128},{192,224},{224,1... | collective-permute-start | bytes 1376264 | tf_op jit(solution)/shard_map/ppermute | solution.py:12
  406.8 4.1 copy-start.4
  406.9 74.5 %copy-start.3 = (bf16[3584,128]{1,0:T(8,128)(2,1)S(1)}, bf16[3584,128]{1,0:T(8,128)(2,1)}, u32[]{:S(2)}) copy-start(bf16[3584,128]{1,0:T(8,128)(2,1)} %copy-done.2) | copy-start | bytes 2752516
  406.9 9.7 %collective-permute-start = (bf16[1792,128]{1,0:T(8,128)(2,1)S(1)}, bf16[1792,128]{1,0:T(8,128)(2,1)S(1)}, u32[]{:S(2)}, u32[]{:S(2)}) collective-permute-start(bf16[1792,128]{1,0:T(8,128)(2,1)S(1)} %constant_dynamic-slice_fusion.1), channel_id=1, source_target_pairs={{0,32},{32,0},{64,96},{96,64},{128,160},{160,128},{192,224},{224,1... | collective-permute-start | bytes 1376264 | tf_op jit(solution)/shard_map/ppermute | solution.py:12
  411.0 7.7 %collective-permute-start.8 = (bf16[128,1792]{1,0:T(8,128)(2,1)S(1)}, bf16[128,1792]{1,0:T(8,128)(2,1)S(1)}, u32[]{:S(2)}, u32[]{:S(2)}) collective-permute-start(bf16[128,1792]{1,0:T(8,128)(2,1)S(1)} %constant_dynamic-slice_fusion.2), channel_id=1, source_target_pairs={{0,32},{32,0},{64,96},{96,64},{128,160},{160,128},{192,224},{224,1... | collective-permute-start | bytes 1376264 | tf_op jit(solution)/shard_map/ppermute | solution.py:12
  413.4 14.1 %collective-permute-start.5 = (bf16[1792,128]{1,0:T(8,128)(2,1)S(1)}, bf16[1792,128]{1,0:T(8,128)(2,1)S(1)}, u32[]{:S(2)}, u32[]{:S(2)}) collective-permute-start(bf16[1792,128]{1,0:T(8,128)(2,1)S(1)} %collective-permute-done.4), channel_id=1, source_target_pairs={{0,64},{32,96},{64,0},{96,32},{128,192},{160,224},{192,128},{224,1... | collective-permute-start | bytes 1376264 | tf_op jit(solution)/shard_map/ppermute | solution.py:12
  416.6 20.8 %collective-permute-start.1 = (bf16[1792,128]{1,0:T(8,128)(2,1)S(1)}, bf16[1792,128]{1,0:T(8,128)(2,1)}, u32[]{:S(2)}, u32[]{:S(2)}) collective-permute-start(bf16[1792,128]{1,0:T(8,128)(2,1)S(1)} %collective-permute-done), channel_id=1, source_target_pairs={{0,64},{32,96},{64,0},{96,32},{128,192},{160,224},{192,128},{224,1... | collective-permute-start | bytes 1376264 | tf_op jit(solution)/shard_map/ppermute | solution.py:12
  418.7 28.5 %collective-permute-start.9 = (bf16[128,1792]{1,0:T(8,128)(2,1)S(1)}, bf16[128,1792]{1,0:T(8,128)(2,1)}, u32[]{:S(2)}, u32[]{:S(2)}) collective-permute-start(bf16[128,1792]{1,0:T(8,128)(2,1)S(1)} %collective-permute-done.8), channel_id=1, source_target_pairs={{0,64},{32,96},{64,0},{96,32},{128,192},{160,224},{192,128},{224,1... | collective-permute-start | bytes 1376264 | tf_op jit(solution)/shard_map/ppermute | solution.py:12
  427.5 31.9 %collective-permute-start.6 = (bf16[1792,128]{1,0:T(8,128)(2,1)S(1)}, bf16[1792,128]{1,0:T(8,128)(2,1)}, u32[]{:S(2)}, u32[]{:S(2)}) collective-permute-start(bf16[1792,128]{1,0:T(8,128)(2,1)S(1)} %collective-permute-done.5), channel_id=1, source_target_pairs={{0,128},{32,160},{64,192},{96,224},{128,0},{160,32},{192,64},{224,... | collective-permute-start | bytes 1376264 | tf_op jit(solution)/shard_map/ppermute | solution.py:12
  437.4 31.9 %collective-permute-start.2 = (bf16[1792,128]{1,0:T(8,128)(2,1)}, bf16[1792,128]{1,0:T(8,128)(2,1)}, u32[]{:S(2)}, u32[]{:S(2)}) collective-permute-start(bf16[1792,128]{1,0:T(8,128)(2,1)} %collective-permute-done.1), channel_id=1, source_target_pairs={{0,128},{32,160},{64,192},{96,224},{128,0},{160,32},{192,64},{224,... | collective-permute-start | bytes 1376264 | tf_op jit(solution)/shard_map/ppermute | solution.py:12
  447.2 31.9 %collective-permute-start.10 = (bf16[128,1792]{1,0:T(8,128)(2,1)}, bf16[128,1792]{1,0:T(8,128)(2,1)}, u32[]{:S(2)}, u32[]{:S(2)}) collective-permute-start(bf16[128,1792]{1,0:T(8,128)(2,1)} %collective-permute-done.9), channel_id=1, source_target_pairs={{0,128},{32,160},{64,192},{96,224},{128,0},{160,32},{192,64},{224,... | collective-permute-start | bytes 1376264 | tf_op jit(solution)/shard_map/ppermute | solution.py:12
  459.5 21.9 %collective-permute-start.7 = (bf16[1792,128]{1,0:T(8,128)(2,1)}, bf16[1792,128]{1,0:T(8,128)(2,1)S(1)}, u32[]{:S(2)}, u32[]{:S(2)}) collective-permute-start(bf16[1792,128]{1,0:T(8,128)(2,1)} %collective-permute-done.6), channel_id=1, source_target_pairs={{0,256},{32,288},{64,320},{96,352},{128,384},{160,416},{192,448},{... | collective-permute-start | bytes 1376264 | tf_op jit(solution)/shard_map/ppermute | solution.py:12
  469.3 18.0 %collective-permute-start.3 = (bf16[1792,128]{1,0:T(8,128)(2,1)}, bf16[1792,128]{1,0:T(8,128)(2,1)S(1)}, u32[]{:S(2)}, u32[]{:S(2)}) collective-permute-start(bf16[1792,128]{1,0:T(8,128)(2,1)} %collective-permute-done.2), channel_id=1, source_target_pairs={{0,256},{32,288},{64,320},{96,352},{128,384},{160,416},{192,448},{... | collective-permute-start | bytes 1376264 | tf_op jit(solution)/shard_map/ppermute | solution.py:12
  479.2 17.9 %collective-permute-start.11 = (bf16[128,1792]{1,0:T(8,128)(2,1)}, bf16[128,1792]{1,0:T(8,128)(2,1)S(1)}, u32[]{:S(2)}, u32[]{:S(2)}) collective-permute-start(bf16[128,1792]{1,0:T(8,128)(2,1)} %collective-permute-done.10), channel_id=1, source_target_pairs={{0,256},{32,288},{64,320},{96,352},{128,384},{160,416},{192,448},{... | collective-permute-start | bytes 1376264 | tf_op jit(solution)/shard_map/ppermute | solution.py:12
  (4 other events, 10.3 us)
where the time goes:
time: 506 us; the launch traced here: 504 us
  waiting for transfers between devices  377 us (75%)
  starting transfers between devices  89.9 us (18%)
  matrix products  20.7 us (4%)
  other arithmetic  9.93 us (2%)
    all_to_all x1, waiting for transfers between devices, on_device(): lax.all_to_all(spread_rows(backward_slots, backward_inputs, experts, capa...  85 us
    all_to_all x1, waiting for transfers between devices, on_device(): lax.all_to_all(spread_rows(backward_slots, scaled, experts, capacity), 'e...  84.7 us
    all_to_all x1, waiting for transfers between devices, on_device(): lax.all_to_all(backward_parts.astype(jnp.bfloat16).reshape(devices, capac...  78.7 us
    all_to_all x1, waiting for transfers between devices, on_device(): lax.all_to_all(spread_rows(forward_slots, forward_inputs, experts, capaci...  77.4 us
    ppermute x12, waiting for transfers between devices, from_partner(): return lax.ppermute(value, axis, pairs)  51.2 us
    ppermute x12, starting transfers between devices, from_partner(): return lax.ppermute(value, axis, pairs)  37.3 us
    all_to_all x1, starting transfers between devices, on_device(): lax.all_to_all(spread_rows(backward_slots, backward_inputs, experts, capa...  18.6 us
  transfers between devices with their start and end apart: 17, of which 12 were waited for; matrix products, arithmetic and copies ran while one was open for 5% of the time, Pallas kernels for 0%

commit v1 on v0

v1 whole, which is shorter than its diff:
```python
import jax
import jax.numpy as jnp
from jax import lax
from jax.sharding import PartitionSpec as P

SHARING_CARDS = 8
CONTRACT_LAST = (((1,), (1,)), ((), ()))
CONTRACT_FIRST = (((0,), (0,)), ((), ()))


def swap(value, axis, mask):
    pairs = [(source, source ^ mask) for source in range(lax.axis_size(axis))]
    return lax.ppermute(value, axis, pairs)


def mirror(value):
    positions = lax.axis_size("pipe")
    pairs = [(source, positions - 1 - source) for source in range(positions)]
    return lax.ppermute(value, "pipe", pairs)


def after(value, *others):
    return lax.optimization_barrier((value, *others))[0]


def dot(left, right, dims=(((1,), (0,)), ((), ()))):
    return lax.dot_general(left, right, dims, preferred_element_type=jnp.float32)


def slot_matrix(labels, experts, capacity):
    members = (labels[:, None] == jnp.arange(experts, dtype=jnp.int32)[None, :]).astype(jnp.int32)
    earlier = jnp.cumsum(members, axis=0) - members
    within = jnp.sum(earlier * members, axis=1)
    target = labels * capacity + within
    matches = target[None, :] == jnp.arange(experts * capacity, dtype=jnp.int32)[:, None]
    return matches.astype(jnp.bfloat16)


def on_device(
    forward_tokens,
    forward_routing,
    forward_gates,
    backward_tokens,
    backward_routing,
    backward_gates,
    cotangent,
    gate_matrix,
    up_matrix,
    down_matrix,
):
    devices = lax.axis_size("expert")
    experts = devices // SHARING_CARDS
    lines = SHARING_CARDS // 2
    tokens = forward_tokens.shape[1]
    width = forward_tokens.shape[2]
    capacity = max(tokens // 3, tokens // experts)
    own_group = lax.axis_index("expert") // SHARING_CARDS
    line_groups = [
        [SHARING_CARDS * a + 2 * j + h for j in range(lines)] for a in range(experts) for h in range(2)
    ]
    gate_weights = gate_matrix[0]
    up_weights = up_matrix[0]
    down_weights = down_matrix[0]
    scaled = (backward_gates[0][:, None] * cotangent[0].astype(jnp.float32)).astype(jnp.bfloat16)
    forward_slots = slot_matrix(forward_routing[0, :, 0] ^ own_group, experts, capacity)
    backward_slots = slot_matrix(backward_routing[0, :, 0] ^ own_group, experts, capacity)

    tall = experts * capacity
    placed = [
        dot(slots, rows).astype(jnp.bfloat16)
        for slots, rows in (
            (backward_slots, backward_tokens[0]),
            (backward_slots, scaled),
            (forward_slots, forward_tokens[0]),
        )
    ]
    blocks = jnp.stack([block.reshape(experts, capacity, width) for block in placed], axis=1)
    arrived = [blocks[0]] + [swap(blocks[k], "expert", SHARING_CARDS * k) for k in range(1, experts)]

    def line_gather(value):
        return lax.all_gather(value, "expert", axis_index_groups=line_groups, tiled=True)

    held = [jnp.concatenate([block[i] for block in arrived], axis=0) for i in range(3)]
    rows_own = line_gather(held[0])
    rows_other = swap(rows_own, "expert", 1)
    grads_own = line_gather(after(held[1], rows_own))
    grads_other = swap(grads_own, "expert", 1)
    ahead_own = line_gather(after(held[2], grads_own))
    ahead_other = swap(ahead_own, "expert", 1)

    def line_sum(kept, received):
        total = (kept + received.astype(jnp.float32)).astype(jnp.bfloat16)
        parts = lax.all_to_all(
            total.reshape(lines, tall, width),
            "expert",
            split_axis=0,
            concat_axis=0,
            axis_index_groups=line_groups,
            tiled=True,
        )
        return parts.astype(jnp.float32).sum(axis=0).astype(jnp.bfloat16)

    def give_back(summed, slots):
        stacked = summed.reshape(experts, capacity, width)
        back = [stacked[0]] + [
            swap(stacked[k], "expert", SHARING_CARDS * k) for k in range(1, experts)
        ]
        return dot(slots, jnp.concatenate(back, axis=0), CONTRACT_FIRST)

    def backward_half(rows, grads):
        gate_pre = dot(rows, gate_weights)
        up_pre = dot(rows, up_weights)
        sigma = jax.nn.sigmoid(gate_pre)
        activated = gate_pre * sigma
        hidden = (activated * up_pre).astype(jnp.bfloat16)
        hidden_grad = dot(grads, down_weights, CONTRACT_LAST)
        gate_grad = (hidden_grad * up_pre * sigma * (1.0 + gate_pre * (1.0 - sigma))).astype(
            jnp.bfloat16
        )
        up_grad = (hidden_grad * activated).astype(jnp.bfloat16)
        return hidden, gate_grad, up_grad

    def backward_parts(gate_grad, up_grad):
        return dot(gate_grad, gate_weights, CONTRACT_LAST) + dot(
            up_grad, up_weights, CONTRACT_LAST
        )

    def forward_parts(rows):
        gate_pre = dot(rows, gate_weights)
        up_pre = dot(rows, up_weights)
        hidden = (jax.nn.silu(gate_pre) * up_pre).astype(jnp.bfloat16)
        return dot(hidden, down_weights)

    other = backward_half(rows_other, grads_other)
    backward_sent = swap(backward_parts(*other[1:]).astype(jnp.bfloat16), "expert", 1)
    own = backward_half(rows_own, grads_own)
    backward_kept = backward_parts(*own[1:])

    middle = width // 2
    upper_side = (lax.axis_index("pipe") >= lax.axis_size("pipe") // 2).astype(jnp.int32)

    def partial_of(start):
        def columns(value):
            return lax.dynamic_slice_in_dim(value, start, middle, 1)

        y_own, y_other = columns(rows_own), columns(rows_other)
        g_own, g_other = columns(grads_own), columns(grads_other)
        gate = dot(y_own, own[1], CONTRACT_FIRST) + dot(y_other, other[1], CONTRACT_FIRST)
        up = dot(y_own, own[2], CONTRACT_FIRST) + dot(y_other, other[2], CONTRACT_FIRST)
        down = dot(own[0], g_own, CONTRACT_FIRST) + dot(other[0], g_other, CONTRACT_FIRST)
        return [value.astype(jnp.bfloat16) for value in (gate, up, down)]

    outgoing = [mirror(value) for value in partial_of((1 - upper_side) * middle)]
    retained = partial_of(upper_side * middle)

    forward_sent = swap(forward_parts(ahead_other).astype(jnp.bfloat16), "expert", 1)
    forward_kept = forward_parts(ahead_own)

    backward_total = line_sum(backward_kept, backward_sent)
    backward_result = give_back(backward_total, backward_slots).astype(jnp.bfloat16)
    forward_total = line_sum(forward_kept, forward_sent)
    forward_result = (
        forward_gates[0][:, None] * give_back(forward_total, forward_slots)
    ).astype(jnp.bfloat16)

    gradients = [
        (kept.astype(jnp.float32) + came.astype(jnp.float32)).astype(jnp.bfloat16)[None]
        for kept, came in zip(retained, outgoing)
    ]
    return forward_result[None], backward_result[None], *gradients


def solution(mesh):
    in_specs = (
        P("pipe", "expert", None),
        P("pipe", "expert", None),
        P("pipe", "expert"),
        P("pipe", "expert", None),
        P("pipe", "expert", None),
        P("pipe", "expert"),
        P("pipe", "expert", None),
        P("pipe", None, "expert"),
        P("pipe", None, "expert"),
        P("pipe", "expert", None),
    )
    out_specs = (
        P("pipe", "expert", None),
        P("pipe", "expert", None),
        P("pipe", None, "expert"),
        P("pipe", None, "expert"),
        P("pipe", "expert", None),
    )
    return jax.shard_map(
        on_device, mesh=mesh, in_specs=in_specs, out_specs=out_specs, check_vma=False
    )
```

time: 506 us -> 297 us (0.59)
  waiting for transfers between devices: 377 us -> 102 us
  blocking collectives: 0 us -> 51.1 us
  starting transfers between devices: 89.9 us -> 105 us
  matrix products: 20.7 us -> 29.9 us
  other arithmetic: 9.93 us -> 3.03 us
    all_to_all x5 -> x2, waiting for transfers between devices: 326 us -> 0.01 us  [line_sum(): lax.all_to_all(total.reshape(lines, tall, width), 'expert', split_axis=0,...]
    ppermute x12 -> x17, starting transfers between devices: 37.3 us -> 96.1 us  [the longest x14 77.3 us: swap(): return lax.ppermute(value, axis, pairs)]
    all_gather x0 -> x3, blocking collectives: none -> 51.1 us  [line_gather(): lax.all_gather(value, 'expert', axis_index_groups=line_groups, tiled=True)]
    ppermute x12 -> x17, waiting for transfers between devices: 51.2 us -> 101 us  [the longest x14 83.3 us: swap(): return lax.ppermute(value, axis, pairs)]
    all_to_all x5 -> x2, starting transfers between devices: 52.6 us -> 8.47 us  [line_sum(): lax.all_to_all(total.reshape(lines, tall, width), 'expert', split_axis=0,...]
    dot_general x15 -> x31, matrix products: 20.7 us -> 29.9 us  [dot(): lax.dot_general(left, right, dims, preferred_element_type=jnp.float32)]
  transfers between devices with their start and end apart: 17 -> 19, of which waited for: 12 -> 12; matrix products, arithmetic and copies ran while one was open for 5% -> 9% of each run, Pallas kernels for 0% -> 0%
where the time goes in v1:
time: 297 us; the launch traced here: 292 us
  starting transfers between devices  105 us (35%)
  waiting for transfers between devices  102 us (34%)
  blocking collectives  51.1 us (17%)
  matrix products  29.9 us (10%)
  other arithmetic  3.03 us (1%)
    ppermute x14, waiting for transfers between devices, swap(): return lax.ppermute(value, axis, pairs)  83.3 us
    ppermute x14, starting transfers between devices, swap(): return lax.ppermute(value, axis, pairs)  77.3 us
    all_gather x3, blocking collectives, line_gather(): lax.all_gather(value, 'expert', axis_index_groups=line_groups, tiled=True)  51.1 us
    dot_general x31, matrix products, dot(): lax.dot_general(left, right, dims, preferred_element_type=jnp.float32)  29.9 us
    ppermute x3, starting transfers between devices, mirror(): return lax.ppermute(value, 'pipe', pairs)  18.8 us
    ppermute x3, waiting for transfers between devices, mirror(): return lax.ppermute(value, 'pipe', pairs)  18.1 us
    all_to_all x2, starting transfers between devices, line_sum(): lax.all_to_all(total.reshape(lines, tall, width), 'expert', split_axis=0,...  8.47 us
  transfers between devices with their start and end apart: 19, of which 12 were waited for; matrix products, arithmetic and copies ran while one was open for 9% of the time, Pallas kernels for 0%

profile of v1, /device:TPU:1, one launch (start us, length us, event | category | flops | bytes accessed | tf_op | source)
XLA Modules:
  0.0 292.3 jit_solution(80304574798528672)
XLA Ops:
  5.6 9.6 %collective-permute-start = (bf16[3,8,3584]{2,1,0:T(8,128)(2,1)S(1)}, bf16[3,8,3584]{2,1,0:T(8,128)(2,1)S(1)}, u32[]{:S(2)}, u32[]{:S(2)}) collective-permute-start(bf16[3,8,3584]{2,1,0:T(8,128)(2,1)S(1)} %get-tuple-element.9), channel_id=1, source_target_pairs={{0,8},{1,9},{2,10},{3,11},{4,12},{5,13},{6,14},{7,15},{8,0},{9,1},... | collective-permute-start | bytes 516104 | tf_op jit(solution)/shard_map/ppermute | solution.py:13
  15.2 10.6 %collective-permute-start.1 = (bf16[3,8,3584]{2,1,0:T(8,128)(2,1)S(1)}, bf16[3,8,3584]{2,1,0:T(8,128)(2,1)S(1)}, u32[]{:S(2)}, u32[]{:S(2)}) collective-permute-start(bf16[3,8,3584]{2,1,0:T(8,128)(2,1)S(1)} %get-tuple-element.10), channel_id=1, source_target_pairs={{0,16},{1,17},{2,18},{3,19},{4,20},{5,21},{6,22},{7,23},{8,24},{9,... | collective-permute-start | bytes 516104 | tf_op jit(solution)/shard_map/ppermute | solution.py:13
  32.0 23.5 %collective-permute-done.2 = bf16[3,8,3584]{2,1,0:T(8,128)(2,1)S(1)} collective-permute-done((bf16[3,8,3584]{2,1,0:T(8,128)(2,1)S(1)}, bf16[3,8,3584]{2,1,0:T(8,128)(2,1)S(1)}, u32[]{:S(2)}, u32[]{:S(2)}) %collective-permute-start.2) | collective-permute-done | bytes 172064 | tf_op jit(solution)/shard_map/ppermute | solution.py:13
  55.5 17.3 %all_gather.9 = bf16[128,3584]{1,0:T(8,128)(2,1)S(1)} all-gather(bf16[32,3584]{1,0:T(8,128)(2,1)S(1)} %pad_maximum_fusion.2), channel_id=1, replica_groups={{0,2,4,6},{1,3,5,7},{8,10,12,14},{9,11,13,15},{16,18,20,22},{17,19,21,2..., dimensions={0}, use_global_device_ids=true | all-gather | bytes 1146880 | tf_op jit(solution)/shard_map/all_gather | solution.py:81
  72.8 17.2 %all_gather.10 = bf16[128,3584]{1,0:T(8,128)(2,1)S(1)} all-gather(bf16[32,3584]{1,0:T(8,128)(2,1)S(1)} %pad_maximum_fusion.1), channel_id=1, replica_groups={{0,2,4,6},{1,3,5,7},{8,10,12,14},{9,11,13,15},{16,18,20,22},{17,19,21,2..., dimensions={0}, use_global_device_ids=true | all-gather | bytes 1146880 | tf_op jit(solution)/shard_map/all_gather | solution.py:81
  92.7 4.3 %collective-permute-start.9 = (bf16[128,3584]{1,0:T(8,128)(2,1)S(1)}, bf16[128,3584]{1,0:T(8,128)(2,1)S(1)}, u32[]{:S(2)}, u32[]{:S(2)}) collective-permute-start(bf16[128,3584]{1,0:T(8,128)(2,1)S(1)} %all_gather.9), channel_id=1, source_target_pairs={{0,1},{1,0},{2,3},{3,2},{4,5},{5,4},{6,7},{7,6},{8,9},{9,8},{10,11... | collective-permute-start | bytes 2752520 | tf_op jit(solution)/shard_map/ppermute | solution.py:13
  97.0 16.5 %all_gather.11 = bf16[128,3584]{1,0:T(8,128)(2,1)} all-gather(bf16[32,3584]{1,0:T(8,128)(2,1)S(1)} %pad_maximum_fusion), channel_id=1, replica_groups={{0,2,4,6},{1,3,5,7},{8,10,12,14},{9,11,13,15},{16,18,20,22},{17,19,21,2..., dimensions={0}, use_global_device_ids=true | all-gather | bytes 1146880 | tf_op jit(solution)/shard_map/all_gather | solution.py:81
  114.0 15.7 %collective-permute-done.9 = bf16[128,3584]{1,0:T(8,128)(2,1)S(1)} collective-permute-done((bf16[128,3584]{1,0:T(8,128)(2,1)S(1)}, bf16[128,3584]{1,0:T(8,128)(2,1)S(1)}, u32[]{:S(2)}, u32[]{:S(2)}) %collective-permute-start.9) | collective-permute-done | bytes 917536 | tf_op jit(solution)/shard_map/ppermute | solution.py:13
  133.9 4.9 %collective-permute-start.3 = (bf16[128,3584]{1,0:T(8,128)(2,1)}, bf16[128,3584]{1,0:T(8,128)(2,1)}, u32[]{:S(2)}, u32[]{:S(2)}) collective-permute-start(bf16[128,3584]{1,0:T(8,128)(2,1)} %all_gather.11), channel_id=1, source_target_pairs={{0,1},{1,0},{2,3},{3,2},{4,5},{5,4},{6,7},{7,6},{8,9},{9,8},{10,11... | collective-permute-start | bytes 2752520 | tf_op jit(solution)/shard_map/ppermute | solution.py:13
  139.9 10.5 %collective-permute-done.10 = bf16[128,3584]{1,0:T(8,128)(2,1)S(1)} collective-permute-done((bf16[128,3584]{1,0:T(8,128)(2,1)S(1)}, bf16[128,3584]{1,0:T(8,128)(2,1)S(1)}, u32[]{:S(2)}, u32[]{:S(2)}) %collective-permute-start.10) | collective-permute-done | bytes 917536 | tf_op jit(solution)/shard_map/ppermute | solution.py:13
  151.8 4.2 %all-to-all-start.1 = ((bf16[4,32,3584]{2,1,0:T(8,128)(2,1)}), bf16[4,32,3584]{2,1,0:T(8,128)(2,1)}, u32[]{:S(2)}, u32[]{:S(2)}) async-start(bf16[4,32,3584]{2,1,0:T(8,128)(2,1)} %bitcast.132), calls=%async_computation.1 | async-start | bytes 1835008 | tf_op jit(solution)/shard_map/all_to_all | solution.py:93
  156.1 14.2 %collective-permute-done.3 = bf16[128,3584]{1,0:T(8,128)(2,1)} collective-permute-done((bf16[128,3584]{1,0:T(8,128)(2,1)}, bf16[128,3584]{1,0:T(8,128)(2,1)}, u32[]{:S(2)}, u32[]{:S(2)}) %collective-permute-start.3) | collective-permute-done | bytes 917536 | tf_op jit(solution)/shard_map/ppermute | solution.py:13
  183.4 10.0 %collective-permute-done.4 = bf16[128,3584]{1,0:T(8,128)(2,1)} collective-permute-done((bf16[128,3584]{1,0:T(8,128)(2,1)}, bf16[128,3584]{1,0:T(8,128)(2,1)}, u32[]{:S(2)}, u32[]{:S(2)}) %collective-permute-start.4) | collective-permute-done | bytes 917536 | tf_op jit(solution)/shard_map/ppermute | solution.py:13
  196.8 4.3 %all-to-all-start = ((bf16[4,32,3584]{2,1,0:T(8,128)(2,1)}), bf16[4,32,3584]{2,1,0:T(8,128)(2,1)S(1)}, u32[]{:S(2)}, u32[]{:S(2)}) async-start(bf16[4,32,3584]{2,1,0:T(8,128)(2,1)} %bitcast.131), calls=%async_computation | async-start | bytes 1835008 | tf_op jit(solution)/shard_map/all_to_all | solution.py:93
  202.9 11.0 %collective-permute-start.16 = (bf16[128,1792]{1,0:T(8,128)(2,1)S(1)}, bf16[128,1792]{1,0:T(8,128)(2,1)S(1)}, u32[]{:S(2)}, u32[]{:S(2)}) collective-permute-start(bf16[128,1792]{1,0:T(8,128)(2,1)S(1)} %fusion.18), channel_id=1, source_target_pairs={{0,480},{32,448},{64,416},{96,384},{128,352},{160,320},{192,288},{... | collective-permute-start | bytes 1376264 | tf_op jit(solution)/shard_map/ppermute | solution.py:19
  216.6 5.8 %collective-permute-start.14 = (bf16[1792,128]{1,0:T(8,128)(2,1)S(1)}, bf16[1792,128]{1,0:T(8,128)(2,1)S(1)}, u32[]{:S(2)}, u32[]{:S(2)}) collective-permute-start(bf16[1792,128]{1,0:T(8,128)(2,1)S(1)} %fusion.8), channel_id=1, source_target_pairs={{0,480},{32,448},{64,416},{96,384},{128,352},{160,320},{192,288},{... | collective-permute-start | bytes 1376264 | tf_op jit(solution)/shard_map/ppermute | solution.py:19
  225.3 8.7 %collective-permute-done.15 = bf16[1792,128]{1,0:T(8,128)(2,1)S(1)} collective-permute-done((bf16[1792,128]{1,0:T(8,128)(2,1)S(1)}, bf16[1792,128]{1,0:T(8,128)(2,1)S(1)}, u32[]{:S(2)}, u32[]{:S(2)}) %collective-permute-start.15) | collective-permute-done | bytes 458784 | tf_op jit(solution)/shard_map/ppermute | solution.py:19
  235.1 8.0 %collective-permute-done.14 = bf16[1792,128]{1,0:T(8,128)(2,1)S(1)} collective-permute-done((bf16[1792,128]{1,0:T(8,128)(2,1)S(1)}, bf16[1792,128]{1,0:T(8,128)(2,1)S(1)}, u32[]{:S(2)}, u32[]{:S(2)}) %collective-permute-start.14) | collective-permute-done | bytes 458784 | tf_op jit(solution)/shard_map/ppermute | solution.py:19
  245.5 14.2 %collective-permute-start.11 = (bf16[8,3584]{1,0:T(8,128)(2,1)S(1)}, bf16[8,3584]{1,0:T(8,128)(2,1)S(1)}, u32[]{:S(2)}, u32[]{:S(2)}) collective-permute-start(bf16[8,3584]{1,0:T(8,128)(2,1)S(1)} %get-tuple-element.15), channel_id=1, source_target_pairs={{0,8},{1,9},{2,10},{3,11},{4,12},{5,13},{6,14},{7,15},{8,0},{9,1},... | collective-permute-start | bytes 172040 | tf_op jit(solution)/shard_map/ppermute | solution.py:13
  259.8 4.8 %collective-permute-start.12 = (bf16[8,3584]{1,0:T(8,128)(2,1)S(1)}, bf16[8,3584]{1,0:T(8,128)(2,1)S(1)}, u32[]{:S(2)}, u32[]{:S(2)}) collective-permute-start(bf16[8,3584]{1,0:T(8,128)(2,1)S(1)} %get-tuple-element.14), channel_id=1, source_target_pairs={{0,16},{1,17},{2,18},{3,19},{4,20},{5,21},{6,22},{7,23},{8,24},{9,... | collective-permute-start | bytes 172040 | tf_op jit(solution)/shard_map/ppermute | solution.py:13
  264.6 4.1 %collective-permute-start.13 = (bf16[8,3584]{1,0:T(8,128)(2,1)S(1)}, bf16[8,3584]{1,0:T(8,128)(2,1)S(1)}, u32[]{:S(2)}, u32[]{:S(2)}) collective-permute-start(bf16[8,3584]{1,0:T(8,128)(2,1)S(1)} %get-tuple-element.13), channel_id=1, source_target_pairs={{0,24},{1,25},{2,26},{3,27},{4,28},{5,29},{6,30},{7,31},{8,16},{9,... | collective-permute-start | bytes 172040 | tf_op jit(solution)/shard_map/ppermute | solution.py:13
  268.9 7.3 %collective-permute-start.5 = (bf16[8,3584]{1,0:T(8,128)(2,1)S(1)}, bf16[8,3584]{1,0:T(8,128)(2,1)S(1)}, u32[]{:S(2)}, u32[]{:S(2)}) collective-permute-start(bf16[8,3584]{1,0:T(8,128)(2,1)S(1)} %get-tuple-element.19), channel_id=1, source_target_pairs={{0,8},{1,9},{2,10},{3,11},{4,12},{5,13},{6,14},{7,15},{8,0},{9,1},... | collective-permute-start | bytes 172040 | tf_op jit(solution)/shard_map/ppermute | solution.py:13
  276.2 4.8 %collective-permute-start.6 = (bf16[8,3584]{1,0:T(8,128)(2,1)S(1)}, bf16[8,3584]{1,0:T(8,128)(2,1)S(1)}, u32[]{:S(2)}, u32[]{:S(2)}) collective-permute-start(bf16[8,3584]{1,0:T(8,128)(2,1)S(1)} %get-tuple-element.18), channel_id=1, source_target_pairs={{0,16},{1,17},{2,18},{3,19},{4,20},{5,21},{6,22},{7,23},{8,24},{9,... | collective-permute-start | bytes 172040 | tf_op jit(solution)/shard_map/ppermute | solution.py:13
  281.0 4.1 %collective-permute-start.7 = (bf16[8,3584]{1,0:T(8,128)(2,1)S(1)}, bf16[8,3584]{1,0:T(8,128)(2,1)S(1)}, u32[]{:S(2)}, u32[]{:S(2)}) collective-permute-start(bf16[8,3584]{1,0:T(8,128)(2,1)S(1)} %get-tuple-element.17), channel_id=1, source_target_pairs={{0,24},{1,25},{2,26},{3,27},{4,28},{5,29},{6,30},{7,31},{8,16},{9,... | collective-permute-start | bytes 172040 | tf_op jit(solution)/shard_map/ppermute | solution.py:13
  (97 shorter events, 55.5 us)
Async XLA Ops:
  0.6 129.5 %copy-start = (bf16[1,3584,128]{2,1,0:T(8,128)(2,1)S(1)}, bf16[1,3584,128]{2,1,0:T(8,128)(2,1)}, u32[]{:S(2)}) copy-start(bf16[1,3584,128]{2,1,0:T(8,128)(2,1)} %param.18) | copy-start | bytes 2752516
  5.6 24.1 %collective-permute-start = (bf16[3,8,3584]{2,1,0:T(8,128)(2,1)S(1)}, bf16[3,8,3584]{2,1,0:T(8,128)(2,1)S(1)}, u32[]{:S(2)}, u32[]{:S(2)}) collective-permute-start(bf16[3,8,3584]{2,1,0:T(8,128)(2,1)S(1)} %get-tuple-element.9), channel_id=1, source_target_pairs={{0,8},{1,9},{2,10},{3,11},{4,12},{5,13},{6,14},{7,15},{8,0},{9,1},... | collective-permute-start | bytes 516104 | tf_op jit(solution)/shard_map/ppermute | solution.py:13
  15.2 16.7 %collective-permute-start.1 = (bf16[3,8,3584]{2,1,0:T(8,128)(2,1)S(1)}, bf16[3,8,3584]{2,1,0:T(8,128)(2,1)S(1)}, u32[]{:S(2)}, u32[]{:S(2)}) collective-permute-start(bf16[3,8,3584]{2,1,0:T(8,128)(2,1)S(1)} %get-tuple-element.10), channel_id=1, source_target_pairs={{0,16},{1,17},{2,18},{3,19},{4,20},{5,21},{6,22},{7,23},{8,24},{9,... | collective-permute-start | bytes 516104 | tf_op jit(solution)/shard_map/ppermute | solution.py:13
  25.9 29.6 %collective-permute-start.2 = (bf16[3,8,3584]{2,1,0:T(8,128)(2,1)S(1)}, bf16[3,8,3584]{2,1,0:T(8,128)(2,1)S(1)}, u32[]{:S(2)}, u32[]{:S(2)}) collective-permute-start(bf16[3,8,3584]{2,1,0:T(8,128)(2,1)S(1)} %get-tuple-element.11), channel_id=1, source_target_pairs={{0,24},{1,25},{2,26},{3,27},{4,28},{5,29},{6,30},{7,31},{8,16},{9,... | collective-permute-start | bytes 516104 | tf_op jit(solution)/shard_map/ppermute | solution.py:13
  72.8 40.8 %copy-start.2 = (bf16[1,128,3584]{2,1,0:T(8,128)(2,1)S(1)}, bf16[1,128,3584]{2,1,0:T(8,128)(2,1)}, u32[]{:S(2)}) copy-start(bf16[1,128,3584]{2,1,0:T(8,128)(2,1)} %param.19) | copy-start | bytes 2752516
  90.1 43.4 %copy-start.5 = (bf16[128,3584]{1,0:T(8,128)(2,1)}, bf16[128,3584]{1,0:T(8,128)(2,1)S(1)}, u32[]{:S(2)}) copy-start(bf16[128,3584]{1,0:T(8,128)(2,1)S(1)} %all_gather.10) | copy-start | bytes 2752516
  90.1 39.7 %copy-start.1 = (bf16[1,3584,128]{2,1,0:T(8,128)(2,1)S(1)}, bf16[1,3584,128]{2,1,0:T(8,128)(2,1)}, u32[]{:S(2)}) copy-start(bf16[1,3584,128]{2,1,0:T(8,128)(2,1)} %param.17) | copy-start | bytes 2752516
  90.1 23.5 %collective-permute-start.8 = (bf16[128,3584]{1,0:T(8,128)(2,1)S(1)}, bf16[128,3584]{1,0:T(8,128)(2,1)S(1)}, u32[]{:S(2)}, u32[]{:S(2)}) collective-permute-start(bf16[128,3584]{1,0:T(8,128)(2,1)S(1)} %all_gather.10), channel_id=1, source_target_pairs={{0,1},{1,0},{2,3},{3,2},{4,5},{5,4},{6,7},{7,6},{8,9},{9,8},{10,11... | collective-permute-start | bytes 2752520 | tf_op jit(solution)/shard_map/ppermute | solution.py:13
  92.7 37.0 %collective-permute-start.9 = (bf16[128,3584]{1,0:T(8,128)(2,1)S(1)}, bf16[128,3584]{1,0:T(8,128)(2,1)S(1)}, u32[]{:S(2)}, u32[]{:S(2)}) collective-permute-start(bf16[128,3584]{1,0:T(8,128)(2,1)S(1)} %all_gather.9), channel_id=1, source_target_pairs={{0,1},{1,0},{2,3},{3,2},{4,5},{5,4},{6,7},{7,6},{8,9},{9,8},{10,11... | collective-permute-start | bytes 2752520 | tf_op jit(solution)/shard_map/ppermute | solution.py:13
  131.5 19.0 %collective-permute-start.10 = (bf16[128,3584]{1,0:T(8,128)(2,1)S(1)}, bf16[128,3584]{1,0:T(8,128)(2,1)S(1)}, u32[]{:S(2)}, u32[]{:S(2)}) collective-permute-start(bf16[128,3584]{1,0:T(8,128)(2,1)S(1)} %fusion), channel_id=1, source_target_pairs={{0,1},{1,0},{2,3},{3,2},{4,5},{5,4},{6,7},{7,6},{8,9},{9,8},{10,11... | collective-permute-start | bytes 2752520 | tf_op jit(solution)/shard_map/ppermute | solution.py:13
  133.9 36.4 %collective-permute-start.3 = (bf16[128,3584]{1,0:T(8,128)(2,1)}, bf16[128,3584]{1,0:T(8,128)(2,1)}, u32[]{:S(2)}, u32[]{:S(2)}) collective-permute-start(bf16[128,3584]{1,0:T(8,128)(2,1)} %all_gather.11), channel_id=1, source_target_pairs={{0,1},{1,0},{2,3},{3,2},{4,5},{5,4},{6,7},{7,6},{8,9},{9,8},{10,11... | collective-permute-start | bytes 2752520 | tf_op jit(solution)/shard_map/ppermute | solution.py:13
  151.8 45.0 %all-to-all-start.1 = ((bf16[4,32,3584]{2,1,0:T(8,128)(2,1)}), bf16[4,32,3584]{2,1,0:T(8,128)(2,1)}, u32[]{:S(2)}, u32[]{:S(2)}) async-start(bf16[4,32,3584]{2,1,0:T(8,128)(2,1)} %bitcast.132), calls=%async_computation.1 | async-start | bytes 1835008 | tf_op jit(solution)/shard_map/all_to_all | solution.py:93
  174.9 18.5 %collective-permute-start.4 = (bf16[128,3584]{1,0:T(8,128)(2,1)}, bf16[128,3584]{1,0:T(8,128)(2,1)}, u32[]{:S(2)}, u32[]{:S(2)}) collective-permute-start(bf16[128,3584]{1,0:T(8,128)(2,1)} %convolution_convert_fusion), channel_id=1, source_target_pairs={{0,1},{1,0},{2,3},{3,2},{4,5},{5,4},{6,7},{7,6},{8,9},{9,8},{10,11... | collective-permute-start | bytes 2752520 | tf_op jit(solution)/shard_map/ppermute | solution.py:13
  196.8 71.9 %all-to-all-start = ((bf16[4,32,3584]{2,1,0:T(8,128)(2,1)}), bf16[4,32,3584]{2,1,0:T(8,128)(2,1)S(1)}, u32[]{:S(2)}, u32[]{:S(2)}) async-start(bf16[4,32,3584]{2,1,0:T(8,128)(2,1)} %bitcast.131), calls=%async_computation | async-start | bytes 1835008 | tf_op jit(solution)/shard_map/all_to_all | solution.py:93
  202.9 21.3 %collective-permute-start.16 = (bf16[128,1792]{1,0:T(8,128)(2,1)S(1)}, bf16[128,1792]{1,0:T(8,128)(2,1)S(1)}, u32[]{:S(2)}, u32[]{:S(2)}) collective-permute-start(bf16[128,1792]{1,0:T(8,128)(2,1)S(1)} %fusion.18), channel_id=1, source_target_pairs={{0,480},{32,448},{64,416},{96,384},{128,352},{160,320},{192,288},{... | collective-permute-start | bytes 1376264 | tf_op jit(solution)/shard_map/ppermute | solution.py:19
  214.2 19.8 %collective-permute-start.15 = (bf16[1792,128]{1,0:T(8,128)(2,1)S(1)}, bf16[1792,128]{1,0:T(8,128)(2,1)S(1)}, u32[]{:S(2)}, u32[]{:S(2)}) collective-permute-start(bf16[1792,128]{1,0:T(8,128)(2,1)S(1)} %fusion.13), channel_id=1, source_target_pairs={{0,480},{32,448},{64,416},{96,384},{128,352},{160,320},{192,288},{... | collective-permute-start | bytes 1376264 | tf_op jit(solution)/shard_map/ppermute | solution.py:19
  216.6 26.4 %collective-permute-start.14 = (bf16[1792,128]{1,0:T(8,128)(2,1)S(1)}, bf16[1792,128]{1,0:T(8,128)(2,1)S(1)}, u32[]{:S(2)}, u32[]{:S(2)}) collective-permute-start(bf16[1792,128]{1,0:T(8,128)(2,1)S(1)} %fusion.8), channel_id=1, source_target_pairs={{0,480},{32,448},{64,416},{96,384},{128,352},{160,320},{192,288},{... | collective-permute-start | bytes 1376264 | tf_op jit(solution)/shard_map/ppermute | solution.py:19
  244.1 47.3 %copy-start.12 = (f32[1,24]{1,0:T(1,128)S(1)}, f32[1,24]{1,0:T(1,128)}, u32[]{:S(2)}) copy-start(f32[1,24]{1,0:T(1,128)} %param.12) | copy-start | bytes 292
  245.5 35.5 %collective-permute-start.11 = (bf16[8,3584]{1,0:T(8,128)(2,1)S(1)}, bf16[8,3584]{1,0:T(8,128)(2,1)S(1)}, u32[]{:S(2)}, u32[]{:S(2)}) collective-permute-start(bf16[8,3584]{1,0:T(8,128)(2,1)S(1)} %get-tuple-element.15), channel_id=1, source_target_pairs={{0,8},{1,9},{2,10},{3,11},{4,12},{5,13},{6,14},{7,15},{8,0},{9,1},... | collective-permute-start | bytes 172040 | tf_op jit(solution)/shard_map/ppermute | solution.py:13
  259.8 25.4 %collective-permute-start.12 = (bf16[8,3584]{1,0:T(8,128)(2,1)S(1)}, bf16[8,3584]{1,0:T(8,128)(2,1)S(1)}, u32[]{:S(2)}, u32[]{:S(2)}) collective-permute-start(bf16[8,3584]{1,0:T(8,128)(2,1)S(1)} %get-tuple-element.14), channel_id=1, source_target_pairs={{0,16},{1,17},{2,18},{3,19},{4,20},{5,21},{6,22},{7,23},{8,24},{9,... | collective-permute-start | bytes 172040 | tf_op jit(solution)/shard_map/ppermute | solution.py:13
  264.6 20.6 %collective-permute-start.13 = (bf16[8,3584]{1,0:T(8,128)(2,1)S(1)}, bf16[8,3584]{1,0:T(8,128)(2,1)S(1)}, u32[]{:S(2)}, u32[]{:S(2)}) collective-permute-start(bf16[8,3584]{1,0:T(8,128)(2,1)S(1)} %get-tuple-element.13), channel_id=1, source_target_pairs={{0,24},{1,25},{2,26},{3,27},{4,28},{5,29},{6,30},{7,31},{8,16},{9,... | collective-permute-start | bytes 172040 | tf_op jit(solution)/shard_map/ppermute | solution.py:13
  268.9 17.2 %collective-permute-start.5 = (bf16[8,3584]{1,0:T(8,128)(2,1)S(1)}, bf16[8,3584]{1,0:T(8,128)(2,1)S(1)}, u32[]{:S(2)}, u32[]{:S(2)}) collective-permute-start(bf16[8,3584]{1,0:T(8,128)(2,1)S(1)} %get-tuple-element.19), channel_id=1, source_target_pairs={{0,8},{1,9},{2,10},{3,11},{4,12},{5,13},{6,14},{7,15},{8,0},{9,1},... | collective-permute-start | bytes 172040 | tf_op jit(solution)/shard_map/ppermute | solution.py:13
  276.2 13.8 %collective-permute-start.6 = (bf16[8,3584]{1,0:T(8,128)(2,1)S(1)}, bf16[8,3584]{1,0:T(8,128)(2,1)S(1)}, u32[]{:S(2)}, u32[]{:S(2)}) collective-permute-start(bf16[8,3584]{1,0:T(8,128)(2,1)S(1)} %get-tuple-element.18), channel_id=1, source_target_pairs={{0,16},{1,17},{2,18},{3,19},{4,20},{5,21},{6,22},{7,23},{8,24},{9,... | collective-permute-start | bytes 172040 | tf_op jit(solution)/shard_map/ppermute | solution.py:13
  281.0 10.4 %collective-permute-start.7 = (bf16[8,3584]{1,0:T(8,128)(2,1)S(1)}, bf16[8,3584]{1,0:T(8,128)(2,1)S(1)}, u32[]{:S(2)}, u32[]{:S(2)}) collective-permute-start(bf16[8,3584]{1,0:T(8,128)(2,1)S(1)} %get-tuple-element.17), channel_id=1, source_target_pairs={{0,24},{1,25},{2,26},{3,27},{4,28},{5,29},{6,30},{7,31},{8,16},{9,... | collective-permute-start | bytes 172040 | tf_op jit(solution)/shard_map/ppermute | solution.py:13
  (8 other events, 60.7 us)

commit v2 on v1

--- a/solution.py
+++ b/solution.py
@@ -61,51 +61,74 @@
     gate_weights = gate_matrix[0]
     up_weights = up_matrix[0]
     down_weights = down_matrix[0]
+    partner_gate, partner_up, partner_down = [
+        swap(value, "expert", 1) for value in (gate_weights, up_weights, down_weights)
+    ]
     scaled = (backward_gates[0][:, None] * cotangent[0].astype(jnp.float32)).astype(jnp.bfloat16)
-    forward_slots = slot_matrix(forward_routing[0, :, 0] ^ own_group, experts, capacity)
-    backward_slots = slot_matrix(backward_routing[0, :, 0] ^ own_group, experts, capacity)
+    order = sorted(range(experts), key=lambda step: (step != 0, step != 2, step))
+
+    def slots_of(routing):
+        step = routing[0, :, 0] ^ own_group
+        place = sum((step == order[j]) * j for j in range(1, experts)).astype(jnp.int32)
+        return slot_matrix(place, experts, capacity)
+
+    forward_slots = slots_of(forward_routing)
+    backward_slots = slots_of(backward_routing)
 
     tall = experts * capacity
-    placed = [
-        dot(slots, rows).astype(jnp.bfloat16)
-        for slots, rows in (
-            (backward_slots, backward_tokens[0]),
-            (backward_slots, scaled),
-            (forward_slots, forward_tokens[0]),
-        )
-    ]
-    blocks = jnp.stack([block.reshape(experts, capacity, width) for block in placed], axis=1)
-    arrived = [blocks[0]] + [swap(blocks[k], "expert", SHARING_CARDS * k) for k in range(1, experts)]
+
+    def send_out(*row_sets):
+        blocks = jnp.stack(
+            [
+                dot(slots, rows).astype(jnp.bfloat16).reshape(experts, capacity, width)
+                for slots, rows in row_sets
+            ],
+            axis=1,
+        )
+        arrived = [
+            swap(blocks[j], "expert", SHARING_CARDS * order[j]) if j else blocks[j]
+            for j in range(experts)
+        ]
+        arrived[1:] = after(arrived[1:], partner_gate, partner_up)
+        return [
+            jnp.concatenate([block[i] for block in arrived], axis=0) for i in range(len(row_sets))
+        ]
 
     def line_gather(value):
         return lax.all_gather(value, "expert", axis_index_groups=line_groups, tiled=True)
 
-    held = [jnp.concatenate([block[i] for block in arrived], axis=0) for i in range(3)]
-    rows_own = line_gather(held[0])
+    rows_held, grads_held, ahead_held = send_out(
+        (backward_slots, backward_tokens[0]), (backward_slots, scaled), (forward_slots, forward_tokens[0])
+    )
+    rows_own = line_gather(rows_held)
     rows_other = swap(rows_own, "expert", 1)
-    grads_own = line_gather(after(held[1], rows_own))
-    grads_other = swap(grads_own, "expert", 1)
-    ahead_own = line_gather(after(held[2], grads_own))
-    ahead_other = swap(ahead_own, "expert", 1)
-
-    def line_sum(kept, received):
-        total = (kept + received.astype(jnp.float32)).astype(jnp.bfloat16)
+    grads_own = line_gather(after(grads_held, rows_own, partner_down))
+    grads_other = swap(after(grads_own, rows_other), "expert", 1)
+    ahead = line_gather(after(ahead_held, grads_own, rows_other))
+    ahead = after(ahead, grads_other)
+
+    def line_sum(values):
         parts = lax.all_to_all(
-            total.reshape(lines, tall, width),
+            values,
             "expert",
             split_axis=0,
             concat_axis=0,
             axis_index_groups=line_groups,
             tiled=True,
         )
-        return parts.astype(jnp.float32).sum(axis=0).astype(jnp.bfloat16)
-
-    def give_back(summed, slots):
-        stacked = summed.reshape(experts, capacity, width)
-        back = [stacked[0]] + [
-            swap(stacked[k], "expert", SHARING_CARDS * k) for k in range(1, experts)
+        return parts.astype(jnp.float32).sum(axis=0)
+
+    def give_back(*summed):
+        blocks = jnp.stack(
+            [value.astype(jnp.bfloat16).reshape(experts, capacity, width) for value in summed], axis=1
+        )
+        return [
+            swap(blocks[j], "expert", SHARING_CARDS * order[j]) if j else blocks[j]
+            for j in range(experts)
         ]
-        return dot(slots, jnp.concatenate(back, axis=0), CONTRACT_FIRST)
+
+    def joined(back, i):
+        return jnp.concatenate([block[i] for block in back], axis=0)
 
     def backward_half(rows, grads):
         gate_pre = dot(rows, gate_weights)
@@ -125,16 +148,27 @@
             up_grad, up_weights, CONTRACT_LAST
         )
 
-    def forward_parts(rows):
-        gate_pre = dot(rows, gate_weights)
-        up_pre = dot(rows, up_weights)
+    def forward_slice(gate_slice, up_slice, down_slice):
+        gate_pre = dot(ahead, gate_slice)
+        up_pre = dot(ahead, up_slice)
         hidden = (jax.nn.silu(gate_pre) * up_pre).astype(jnp.bfloat16)
-        return dot(hidden, down_weights)
-
+        return dot(hidden, down_slice)
+
+    forward_parts = forward_slice(gate_weights, up_weights, down_weights) + forward_slice(
+        partner_gate, partner_up, partner_down
+    )
+    forward_total = line_sum(forward_parts.astype(jnp.bfloat16).reshape(lines, tall, width))
+
+    grads_other = after(grads_other, forward_parts)
     other = backward_half(rows_other, grads_other)
-    backward_sent = swap(backward_parts(*other[1:]).astype(jnp.bfloat16), "expert", 1)
+    backward_leaving = backward_parts(*other[1:]).astype(jnp.bfloat16)
+    backward_sent = swap(backward_leaving, "expert", 1)
+
     own = backward_half(rows_own, grads_own)
     backward_kept = backward_parts(*own[1:])
+    backward_sent = after(backward_sent, forward_total)
+    backward_pair = (backward_kept + backward_sent.astype(jnp.float32)).astype(jnp.bfloat16)
+    backward_total = line_sum(backward_pair.reshape(lines, tall, width))
 
     middle = width // 2
     upper_side = (lax.axis_index("pipe") >= lax.axis_size("pipe") // 2).astype(jnp.int32)
@@ -147,27 +181,28 @@
         g_own, g_other = columns(grads_own), columns(grads_other)
         gate = dot(y_own, own[1], CONTRACT_FIRST) + dot(y_other, other[1], CONTRACT_FIRST)
         up = dot(y_own, own[2], CONTRACT_FIRST) + dot(y_other, other[2], CONTRACT_FIRST)
-        down = dot(own[0], g_own, CONTRACT_FIRST) + dot(other[0], g_other, CONTRACT_FIRST)
-        return [value.astype(jnp.bfloat16) for value in (gate, up, down)]
-
-    outgoing = [mirror(value) for value in partial_of((1 - upper_side) * middle)]
+        down = dot(g_own, own[0], CONTRACT_FIRST) + dot(g_other, other[0], CONTRACT_FIRST)
+        return jnp.stack([value.astype(jnp.bfloat16) for value in (gate, up, down)])
+
+    outgoing = mirror(after(partial_of((1 - upper_side) * middle), backward_pair))
     retained = partial_of(upper_side * middle)
 
-    forward_sent = swap(forward_parts(ahead_other).astype(jnp.bfloat16), "expert", 1)
-    forward_kept = forward_parts(ahead_own)
-
-    backward_total = line_sum(backward_kept, backward_sent)
-    backward_result = give_back(backward_total, backward_slots).astype(jnp.bfloat16)
-    forward_total = line_sum(forward_kept, forward_sent)
+    back = give_back(forward_total, backward_total)
+    forward_back, backward_back = joined(back, 0), joined(back, 1)
     forward_result = (
-        forward_gates[0][:, None] * give_back(forward_total, forward_slots)
+        forward_gates[0][:, None] * dot(forward_slots, forward_back, CONTRACT_FIRST)
     ).astype(jnp.bfloat16)
-
-    gradients = [
-        (kept.astype(jnp.float32) + came.astype(jnp.float32)).astype(jnp.bfloat16)[None]
-        for kept, came in zip(retained, outgoing)
-    ]
-    return forward_result[None], backward_result[None], *gradients
+    backward_result = dot(backward_slots, backward_back, CONTRACT_FIRST).astype(jnp.bfloat16)
+
+    outgoing = after(outgoing, back[1])
+    gradients = (retained.astype(jnp.float32) + outgoing.astype(jnp.float32)).astype(jnp.bfloat16)
+    return (
+        forward_result[None],
+        backward_result[None],
+        gradients[0][None],
+        gradients[1][None],
+        gradients[2].T[None],
+    )
 
 
 def solution(mesh):

time: 297 us -> 230 us (0.77); the launches traced: 292 us -> 229 us
  waiting for transfers between devices: 102 us -> 42.3 us
  starting transfers between devices: 105 us -> 82.5 us
  other arithmetic: 3.03 us -> 11.2 us
  local copies, waits for them, and re-layouts: 1.08 us -> 8.23 us
  blocking collectives: 51.1 us -> 57.4 us
  matrix products: 29.9 us -> 25.8 us
    ppermute x14 -> x12, waiting for transfers between devices: 83.3 us -> 25.8 us  [swap(): return lax.ppermute(value, axis, pairs)]
    ppermute x14 -> x12, starting transfers between devices: 77.3 us -> 61.6 us  [swap(): return lax.ppermute(value, axis, pairs)]
    ppermute x3 -> x1, waiting for transfers between devices: 18.1 us -> 6.75 us  [mirror(): return lax.ppermute(value, 'pipe', pairs)]
    all_to_all x2, waiting for transfers between devices: 0.01 us -> 9.73 us  [line_sum(): lax.all_to_all(values, 'expert', split_axis=0, concat_axis=0, axis_index_...]
    ppermute x3 -> x1, starting transfers between devices: 18.8 us -> 11.7 us  [mirror(): return lax.ppermute(value, 'pipe', pairs)]
    all_gather x3, blocking collectives: 51.1 us -> 57.4 us  [line_gather(): lax.all_gather(value, 'expert', axis_index_groups=line_groups, tiled=True)]
    convert_element_type x0 -> x2, other arithmetic: none -> 4.53 us  [the longest x1 2.83 us: on_device(): (backward_kept + backward_sent.astype(jnp.float32)).astype(jnp.bfloat16)]
    unnamed x26 -> x43, local copies, waits for them, and re-layouts: 0.99 us -> 5.49 us
  transfers between devices with their start and end apart: 19 -> 15, of which waited for: 12 -> 6; matrix products, arithmetic and copies ran while one was open for 9% -> 12% of each run, Pallas kernels for 0% -> 0%
where the time goes in v2:
time: 230 us; the launch traced here: 229 us
  starting transfers between devices  82.5 us (36%)
  blocking collectives  57.4 us (25%)
  waiting for transfers between devices  42.3 us (18%)
  matrix products  25.8 us (11%)
  other arithmetic  11.2 us (5%)
  local copies, waits for them, and re-layouts  8.23 us (4%)
    ppermute x12, starting transfers between devices, swap(): return lax.ppermute(value, axis, pairs)  61.6 us
    all_gather x3, blocking collectives, line_gather(): lax.all_gather(value, 'expert', axis_index_groups=line_groups, tiled=True)  57.4 us
    dot_general x31, matrix products, dot(): lax.dot_general(left, right, dims, preferred_element_type=jnp.float32)  25.8 us
    ppermute x12, waiting for transfers between devices, swap(): return lax.ppermute(value, axis, pairs)  25.8 us
    ppermute x1, starting transfers between devices, mirror(): return lax.ppermute(value, 'pipe', pairs)  11.7 us
    all_to_all x2, waiting for transfers between devices, line_sum(): lax.all_to_all(values, 'expert', split_axis=0, concat_axis=0, axis_index_...  9.73 us
    all_to_all x2, starting transfers between devices, line_sum(): lax.all_to_all(values, 'expert', split_axis=0, concat_axis=0, axis_index_...  9.27 us
    ppermute x1, waiting for transfers between devices, mirror(): return lax.ppermute(value, 'pipe', pairs)  6.75 us
  transfers between devices with their start and end apart: 15, of which 6 were waited for; matrix products, arithmetic and copies ran while one was open for 12% of the time, Pallas kernels for 0%

profile of v2, /device:TPU:1, one launch (start us, length us, event | category | flops | bytes accessed | tf_op | source)
XLA Modules:
  0.0 228.6 jit_solution(960925748002397192)
XLA Ops:
  0.7 5.6 %collective-permute-start.3 = (bf16[3584,128]{1,0:T(8,128)(2,1)}, bf16[3584,128]{1,0:T(8,128)(2,1)S(1)}, u32[]{:S(2)}, u32[]{:S(2)}) collective-permute-start(bf16[3584,128]{1,0:T(8,128)(2,1)} %bitcast.160), channel_id=1, source_target_pairs={{0,1},{1,0},{2,3},{3,2},{4,5},{5,4},{6,7},{7,6},{8,9},{9,8},{10,11... | collective-permute-start | bytes 2752520 | tf_op jit(solution)/shard_map/ppermute | solution.py:13
  12.2 15.7 %collective-permute-start = (bf16[3,8,3584]{2,1,0:T(8,128)(2,1)S(1)}, bf16[3,8,3584]{2,1,0:T(8,128)(2,1)S(1)}, u32[]{:S(2)}, u32[]{:S(2)}) collective-permute-start(bf16[3,8,3584]{2,1,0:T(8,128)(2,1)S(1)} %get-tuple-element.37), channel_id=1, source_target_pairs={{0,16},{1,17},{2,18},{3,19},{4,20},{5,21},{6,22},{7,23},{8,24},{9,... | collective-permute-start | bytes 516104 | tf_op jit(solution)/shard_map/ppermute | solution.py:13
  27.8 4.0 %collective-permute-start.1 = (bf16[3,8,3584]{2,1,0:T(8,128)(2,1)S(1)}, bf16[3,8,3584]{2,1,0:T(8,128)(2,1)S(1)}, u32[]{:S(2)}, u32[]{:S(2)}) collective-permute-start(bf16[3,8,3584]{2,1,0:T(8,128)(2,1)S(1)} %get-tuple-element.36), channel_id=1, source_target_pairs={{0,8},{1,9},{2,10},{3,11},{4,12},{5,13},{6,14},{7,15},{8,0},{9,1},... | collective-permute-start | bytes 516104 | tf_op jit(solution)/shard_map/ppermute | solution.py:13
  33.8 4.7 %collective-permute-start.5 = (bf16[128,3584]{1,0:T(8,128)(2,1)S(1)}, bf16[128,3584]{1,0:T(8,128)(2,1)S(1)}, u32[]{:S(2)}, u32[]{:S(2)}) collective-permute-start(bf16[128,3584]{1,0:T(8,128)(2,1)S(1)} %bitcast.161), channel_id=1, source_target_pairs={{0,1},{1,0},{2,3},{3,2},{4,5},{5,4},{6,7},{7,6},{8,9},{9,8},{10,11... | collective-permute-start | bytes 2752520 | tf_op jit(solution)/shard_map/ppermute | solution.py:13
  38.5 16.9 %collective-permute-done.1 = bf16[3,8,3584]{2,1,0:T(8,128)(2,1)S(1)} collective-permute-done((bf16[3,8,3584]{2,1,0:T(8,128)(2,1)S(1)}, bf16[3,8,3584]{2,1,0:T(8,128)(2,1)S(1)}, u32[]{:S(2)}, u32[]{:S(2)}) %collective-permute-start.1) | collective-permute-done | bytes 172064 | tf_op jit(solution)/shard_map/ppermute | solution.py:13
  56.6 20.2 %all_gather.9 = bf16[128,3584]{1,0:T(8,128)(2,1)S(1)} all-gather(bf16[32,3584]{1,0:T(8,128)(2,1)S(1)} %pad_maximum_fusion.3), channel_id=1, replica_groups={{0,2,4,6},{1,3,5,7},{8,10,12,14},{9,11,13,15},{16,18,20,22},{17,19,21,2..., dimensions={0}, use_global_device_ids=true | all-gather | bytes 1146880 | tf_op jit(solution)/shard_map/all_gather | solution.py:98
  76.8 4.0 %collective-permute-start.6 = (bf16[128,3584]{1,0:T(8,128)(2,1)S(1)}, bf16[128,3584]{1,0:T(8,128)(2,1)S(1)}, u32[]{:S(2)}, u32[]{:S(2)}) collective-permute-start(bf16[128,3584]{1,0:T(8,128)(2,1)S(1)} %all_gather.9), channel_id=1, source_target_pairs={{0,1},{1,0},{2,3},{3,2},{4,5},{5,4},{6,7},{7,6},{8,9},{9,8},{10,11... | collective-permute-start | bytes 2752520 | tf_op jit(solution)/shard_map/ppermute | solution.py:13
  80.8 18.4 %all_gather.10 = bf16[128,3584]{1,0:T(8,128)(2,1)S(1)} all-gather(bf16[32,3584]{1,0:T(8,128)(2,1)S(1)} %pad_maximum_fusion.2), channel_id=1, replica_groups={{0,2,4,6},{1,3,5,7},{8,10,12,14},{9,11,13,15},{16,18,20,22},{17,19,21,2..., dimensions={0}, use_global_device_ids=true | all-gather | bytes 1146880 | tf_op jit(solution)/shard_map/all_gather | solution.py:98
  99.2 3.3 %collective-permute-start.7 = (bf16[128,3584]{1,0:T(8,128)(2,1)S(1)}, bf16[128,3584]{1,0:T(8,128)(2,1)S(1)}, u32[]{:S(2)}, u32[]{:S(2)}) collective-permute-start(bf16[128,3584]{1,0:T(8,128)(2,1)S(1)} %all_gather.10), channel_id=1, source_target_pairs={{0,1},{1,0},{2,3},{3,2},{4,5},{5,4},{6,7},{7,6},{8,9},{9,8},{10,11... | collective-permute-start | bytes 2752520 | tf_op jit(solution)/shard_map/ppermute | solution.py:13
  102.6 18.9 %all_gather.11 = bf16[128,3584]{1,0:T(8,128)(2,1)S(1)} all-gather(bf16[32,3584]{1,0:T(8,128)(2,1)S(1)} %pad_maximum_fusion.1), channel_id=1, replica_groups={{0,2,4,6},{1,3,5,7},{8,10,12,14},{9,11,13,15},{16,18,20,22},{17,19,21,2..., dimensions={0}, use_global_device_ids=true | all-gather | bytes 1146880 | tf_op jit(solution)/shard_map/all_gather | solution.py:98
  123.8 3.4 %fusion.58 = f32[128,3584]{1,0:T(8,128)} fusion(f32[128,128]{1,0:T(8,128)S(1)} %fusion.113, bf16[1,128,3584]{2,1,0:T(8,128)(2,1)} %param.19, bf16[128,3584]{1,0:T(8,128)(2,1)} %copy-done.3, bf16[1,3584,128]{2,1,0:T(8,128)(2,1)S(1)} %copy-done.1), kind=kOutput, calls=%fused_computation.112 | convolution fusion | flops 234979328 | bytes 4653056 | tf_op jit(solution)/shard_map/dot_general | solution.py:27
  129.1 4.0 %convolution_add_fusion.2 = bf16[128,3584]{1,0:T(8,128)(2,1)} fusion(f32[128,3584]{1,0:T(8,128)} %fusion.58, bf16[128,3584]{1,0:T(8,128)(2,1)} %copy-done.19, f32[128,128]{1,0:T(8,128)S(1)} %fusion.119, bf16[128,3584]{1,0:T(8,128)(2,1)} %copy-done.3, bf16[3584,128]{1,0:T(8,128)(2,1)} %copy-done.18), kind=kOutput, calls=%fused_computation.2 | convolution fusion | flops 235896832 | bytes 5570560 | tf_op jit(solution)/shard_map/dot_general | solution.py:27
  133.1 5.0 %all-to-all-start = ((bf16[4,32,3584]{2,1,0:T(8,128)(2,1)}), bf16[4,32,3584]{2,1,0:T(8,128)(2,1)}, u32[]{:S(2)}, u32[]{:S(2)}) async-start(bf16[4,32,3584]{2,1,0:T(8,128)(2,1)} %bitcast.162), calls=%async_computation | async-start | bytes 1835008 | tf_op jit(solution)/shard_map/all_to_all | solution.py:111
  142.6 4.4 %collective-permute-start.8 = (bf16[128,3584]{1,0:T(8,128)(2,1)}, bf16[128,3584]{1,0:T(8,128)(2,1)}, u32[]{:S(2)}, u32[]{:S(2)}) collective-permute-start(bf16[128,3584]{1,0:T(8,128)(2,1)} %fusion), channel_id=1, source_target_pairs={{0,1},{1,0},{2,3},{3,2},{4,5},{5,4},{6,7},{7,6},{8,9},{9,8},{10,11... | collective-permute-start | bytes 2752520 | tf_op jit(solution)/shard_map/ppermute | solution.py:13
  149.5 8.6 %all-to-all-done = bf16[4,32,3584]{2,1,0:T(8,128)(2,1)} async-done(((bf16[4,32,3584]{2,1,0:T(8,128)(2,1)}), bf16[4,32,3584]{2,1,0:T(8,128)(2,1)}, u32[]{:S(2)}, u32[]{:S(2)}) %all-to-all-start) | async-done | bytes 917536 | tf_op jit(solution)/shard_map/all_to_all | solution.py:111
  160.2 3.0 %collective-permute-done.8 = bf16[128,3584]{1,0:T(8,128)(2,1)} collective-permute-done((bf16[128,3584]{1,0:T(8,128)(2,1)}, bf16[128,3584]{1,0:T(8,128)(2,1)}, u32[]{:S(2)}, u32[]{:S(2)}) %collective-permute-start.8) | collective-permute-done | bytes 917536 | tf_op jit(solution)/shard_map/ppermute | solution.py:13
  163.2 2.8 %add_convert_fusion.1 = bf16[128,3584]{1,0:T(8,128)(2,1)} fusion(f32[128,3584]{1,0:T(8,128)} %convolution_add_fusion.1, bf16[128,3584]{1,0:T(8,128)(2,1)} %collective-permute-done.8), kind=kLoop, calls=%fused_computation.31 | loop fusion | flops 1376256 | bytes 3670016 | tf_op jit(solution)/shard_map/convert_element_type | solution.py:170
  166.0 4.3 %all-to-all-start.1 = ((bf16[4,32,3584]{2,1,0:T(8,128)(2,1)}), bf16[4,32,3584]{2,1,0:T(8,128)(2,1)S(1)}, u32[]{:S(2)}, u32[]{:S(2)}) async-start(bf16[4,32,3584]{2,1,0:T(8,128)(2,1)} %bitcast.29), calls=%async_computation.1 | async-start | bytes 1835008 | tf_op jit(solution)/shard_map/all_to_all | solution.py:111
  174.4 11.7 %collective-permute-start.12 = (bf16[3,1792,128]{2,1,0:T(8,128)(2,1)}, bf16[3,1792,128]{2,1,0:T(8,128)(2,1)}, u32[]{:S(2)}, u32[]{:S(2)}) collective-permute-start(bf16[3,1792,128]{2,1,0:T(8,128)(2,1)} %pad_maximum_fusion), channel_id=1, source_target_pairs={{0,480},{32,448},{64,416},{96,384},{128,352},{160,320},{192,288},{... | collective-permute-start | bytes 4128776 | tf_op jit(solution)/shard_map/ppermute | solution.py:19
  192.2 10.1 %collective-permute-start.9 = (bf16[2,8,3584]{2,1,0:T(8,128)(2,1)S(1)}, bf16[2,8,3584]{2,1,0:T(8,128)(2,1)S(1)}, u32[]{:S(2)}, u32[]{:S(2)}) collective-permute-start(bf16[2,8,3584]{2,1,0:T(8,128)(2,1)S(1)} %get-tuple-element.38), channel_id=1, source_target_pairs={{0,16},{1,17},{2,18},{3,19},{4,20},{5,21},{6,22},{7,23},{8,24},{9,... | collective-permute-start | bytes 344072 | tf_op jit(solution)/shard_map/ppermute | solution.py:13
  204.4 3.1 %collective-permute-start.10 = (bf16[2,8,3584]{2,1,0:T(8,128)(2,1)S(1)}, bf16[2,8,3584]{2,1,0:T(8,128)(2,1)S(1)}, u32[]{:S(2)}, u32[]{:S(2)}) collective-permute-start(bf16[2,8,3584]{2,1,0:T(8,128)(2,1)S(1)} %get-tuple-element.39), channel_id=1, source_target_pairs={{0,8},{1,9},{2,10},{3,11},{4,12},{5,13},{6,14},{7,15},{8,0},{9,1},... | collective-permute-start | bytes 344072 | tf_op jit(solution)/shard_map/ppermute | solution.py:13
  207.5 2.9 %collective-permute-start.11 = (bf16[2,8,3584]{2,1,0:T(8,128)(2,1)S(1)}, bf16[2,8,3584]{2,1,0:T(8,128)(2,1)S(1)}, u32[]{:S(2)}, u32[]{:S(2)}) collective-permute-start(bf16[2,8,3584]{2,1,0:T(8,128)(2,1)S(1)} %get-tuple-element.40), channel_id=1, source_target_pairs={{0,24},{1,25},{2,26},{3,27},{4,28},{5,29},{6,30},{7,31},{8,16},{9,... | collective-permute-start | bytes 344072 | tf_op jit(solution)/shard_map/ppermute | solution.py:13
  210.4 6.8 %collective-permute-done.12 = bf16[3,1792,128]{2,1,0:T(8,128)(2,1)} collective-permute-done((bf16[3,1792,128]{2,1,0:T(8,128)(2,1)}, bf16[3,1792,128]{2,1,0:T(8,128)(2,1)}, u32[]{:S(2)}, u32[]{:S(2)}) %collective-permute-start.12) | collective-permute-done | bytes 1376288 | tf_op jit(solution)/shard_map/ppermute | solution.py:19
  218.9 5.9 %collective-permute-done.10 = bf16[2,8,3584]{2,1,0:T(8,128)(2,1)S(1)} collective-permute-done((bf16[2,8,3584]{2,1,0:T(8,128)(2,1)S(1)}, bf16[2,8,3584]{2,1,0:T(8,128)(2,1)S(1)}, u32[]{:S(2)}, u32[]{:S(2)}) %collective-permute-start.10) | collective-permute-done | bytes 114720 | tf_op jit(solution)/shard_map/ppermute | solution.py:13
  (114 shorter events, 40.0 us)
Async XLA Ops:
  0.6 8.9 %copy-start = (bf16[1,24,3584]{2,1,0:T(8,128)(2,1)S(1)}, bf16[1,24,3584]{2,1,0:T(8,128)(2,1)}, u32[]{:S(2)}) copy-start(bf16[1,24,3584]{2,1,0:T(8,128)(2,1)} %param.13) | copy-start | bytes 516100
  0.6 33.1 %copy-start.10 = (bf16[1,128,3584]{2,1,0:T(8,128)(2,1)S(1)}, bf16[1,128,3584]{2,1,0:T(8,128)(2,1)}, u32[]{:S(2)}) copy-start(bf16[1,128,3584]{2,1,0:T(8,128)(2,1)} %param.19) | copy-start | bytes 2752516
  0.7 54.7 %collective-permute-start.3 = (bf16[3584,128]{1,0:T(8,128)(2,1)}, bf16[3584,128]{1,0:T(8,128)(2,1)S(1)}, u32[]{:S(2)}, u32[]{:S(2)}) collective-permute-start(bf16[3584,128]{1,0:T(8,128)(2,1)} %bitcast.160), channel_id=1, source_target_pairs={{0,1},{1,0},{2,3},{3,2},{4,5},{5,4},{6,7},{7,6},{8,9},{9,8},{10,11... | collective-permute-start | bytes 2752520 | tf_op jit(solution)/shard_map/ppermute | solution.py:13
  6.3 49.1 %collective-permute-start.4 = (bf16[3584,128]{1,0:T(8,128)(2,1)}, bf16[3584,128]{1,0:T(8,128)(2,1)S(1)}, u32[]{:S(2)}, u32[]{:S(2)}) collective-permute-start(bf16[3584,128]{1,0:T(8,128)(2,1)} %bitcast.159), channel_id=1, source_target_pairs={{0,1},{1,0},{2,3},{3,2},{4,5},{5,4},{6,7},{7,6},{8,9},{9,8},{10,11... | collective-permute-start | bytes 2752520 | tf_op jit(solution)/shard_map/ppermute | solution.py:13
  12.2 21.6 %collective-permute-start = (bf16[3,8,3584]{2,1,0:T(8,128)(2,1)S(1)}, bf16[3,8,3584]{2,1,0:T(8,128)(2,1)S(1)}, u32[]{:S(2)}, u32[]{:S(2)}) collective-permute-start(bf16[3,8,3584]{2,1,0:T(8,128)(2,1)S(1)} %get-tuple-element.37), channel_id=1, source_target_pairs={{0,16},{1,17},{2,18},{3,19},{4,20},{5,21},{6,22},{7,23},{8,24},{9,... | collective-permute-start | bytes 516104 | tf_op jit(solution)/shard_map/ppermute | solution.py:13
  27.8 27.5 %collective-permute-start.1 = (bf16[3,8,3584]{2,1,0:T(8,128)(2,1)S(1)}, bf16[3,8,3584]{2,1,0:T(8,128)(2,1)S(1)}, u32[]{:S(2)}, u32[]{:S(2)}) collective-permute-start(bf16[3,8,3584]{2,1,0:T(8,128)(2,1)S(1)} %get-tuple-element.36), channel_id=1, source_target_pairs={{0,8},{1,9},{2,10},{3,11},{4,12},{5,13},{6,14},{7,15},{8,0},{9,1},... | collective-permute-start | bytes 516104 | tf_op jit(solution)/shard_map/ppermute | solution.py:13
  31.8 23.5 %collective-permute-start.2 = (bf16[3,8,3584]{2,1,0:T(8,128)(2,1)S(1)}, bf16[3,8,3584]{2,1,0:T(8,128)(2,1)S(1)}, u32[]{:S(2)}, u32[]{:S(2)}) collective-permute-start(bf16[3,8,3584]{2,1,0:T(8,128)(2,1)S(1)} %get-tuple-element.35), channel_id=1, source_target_pairs={{0,24},{1,25},{2,26},{3,27},{4,28},{5,29},{6,30},{7,31},{8,16},{9,... | collective-permute-start | bytes 516104 | tf_op jit(solution)/shard_map/ppermute | solution.py:13
  33.8 47.0 %collective-permute-start.5 = (bf16[128,3584]{1,0:T(8,128)(2,1)S(1)}, bf16[128,3584]{1,0:T(8,128)(2,1)S(1)}, u32[]{:S(2)}, u32[]{:S(2)}) collective-permute-start(bf16[128,3584]{1,0:T(8,128)(2,1)S(1)} %bitcast.161), channel_id=1, source_target_pairs={{0,1},{1,0},{2,3},{3,2},{4,5},{5,4},{6,7},{7,6},{8,9},{9,8},{10,11... | collective-permute-start | bytes 2752520 | tf_op jit(solution)/shard_map/ppermute | solution.py:13
  76.8 46.6 %copy-start.2 = (bf16[1,3584,128]{2,1,0:T(8,128)(2,1)S(1)}, bf16[1,3584,128]{2,1,0:T(8,128)(2,1)}, u32[]{:S(2)}) copy-start(bf16[1,3584,128]{2,1,0:T(8,128)(2,1)} %param.17) | copy-start | bytes 2752516
  76.8 22.4 %collective-permute-start.6 = (bf16[128,3584]{1,0:T(8,128)(2,1)S(1)}, bf16[128,3584]{1,0:T(8,128)(2,1)S(1)}, u32[]{:S(2)}, u32[]{:S(2)}) collective-permute-start(bf16[128,3584]{1,0:T(8,128)(2,1)S(1)} %all_gather.9), channel_id=1, source_target_pairs={{0,1},{1,0},{2,3},{3,2},{4,5},{5,4},{6,7},{7,6},{8,9},{9,8},{10,11... | collective-permute-start | bytes 2752520 | tf_op jit(solution)/shard_map/ppermute | solution.py:13
  80.8 18.4 %copy-start.19 = (bf16[128,3584]{1,0:T(8,128)(2,1)}, bf16[128,3584]{1,0:T(8,128)(2,1)S(1)}, u32[]{:S(2)}) copy-start(bf16[128,3584]{1,0:T(8,128)(2,1)S(1)} %collective-permute-done.5) | copy-start | bytes 2752516
  99.2 3.3 %copy-start.7 = (bf16[128,3584]{1,0:T(8,128)(2,1)}, bf16[128,3584]{1,0:T(8,128)(2,1)S(1)}, u32[]{:S(2)}) copy-start(bf16[128,3584]{1,0:T(8,128)(2,1)S(1)} %all_gather.10) | copy-start | bytes 2752516
  99.2 24.6 %copy-start.1 = (bf16[1,3584,128]{2,1,0:T(8,128)(2,1)S(1)}, bf16[1,3584,128]{2,1,0:T(8,128)(2,1)}, u32[]{:S(2)}) copy-start(bf16[1,3584,128]{2,1,0:T(8,128)(2,1)} %param.18) | copy-start | bytes 2752516
  99.2 22.2 %collective-permute-start.7 = (bf16[128,3584]{1,0:T(8,128)(2,1)S(1)}, bf16[128,3584]{1,0:T(8,128)(2,1)S(1)}, u32[]{:S(2)}, u32[]{:S(2)}) collective-permute-start(bf16[128,3584]{1,0:T(8,128)(2,1)S(1)} %all_gather.10), channel_id=1, source_target_pairs={{0,1},{1,0},{2,3},{3,2},{4,5},{5,4},{6,7},{7,6},{8,9},{9,8},{10,11... | collective-permute-start | bytes 2752520 | tf_op jit(solution)/shard_map/ppermute | solution.py:13
  133.1 25.0 %all-to-all-start = ((bf16[4,32,3584]{2,1,0:T(8,128)(2,1)}), bf16[4,32,3584]{2,1,0:T(8,128)(2,1)}, u32[]{:S(2)}, u32[]{:S(2)}) async-start(bf16[4,32,3584]{2,1,0:T(8,128)(2,1)} %bitcast.162), calls=%async_computation | async-start | bytes 1835008 | tf_op jit(solution)/shard_map/all_to_all | solution.py:111
  141.2 5.8 %copy-start.8 = (bf16[128,3584]{1,0:T(8,128)(2,1)S(1)}, bf16[128,3584]{1,0:T(8,128)(2,1)}, u32[]{:S(2)}) copy-start(bf16[128,3584]{1,0:T(8,128)(2,1)} %copy-done.7) | copy-start | bytes 2752516
  142.6 20.5 %collective-permute-start.8 = (bf16[128,3584]{1,0:T(8,128)(2,1)}, bf16[128,3584]{1,0:T(8,128)(2,1)}, u32[]{:S(2)}, u32[]{:S(2)}) collective-permute-start(bf16[128,3584]{1,0:T(8,128)(2,1)} %fusion), channel_id=1, source_target_pairs={{0,1},{1,0},{2,3},{3,2},{4,5},{5,4},{6,7},{7,6},{8,9},{9,8},{10,11... | collective-permute-start | bytes 2752520 | tf_op jit(solution)/shard_map/ppermute | solution.py:13
  166.0 24.3 %all-to-all-start.1 = ((bf16[4,32,3584]{2,1,0:T(8,128)(2,1)}), bf16[4,32,3584]{2,1,0:T(8,128)(2,1)S(1)}, u32[]{:S(2)}, u32[]{:S(2)}) async-start(bf16[4,32,3584]{2,1,0:T(8,128)(2,1)} %bitcast.29), calls=%async_computation.1 | async-start | bytes 1835008 | tf_op jit(solution)/shard_map/all_to_all | solution.py:111
  174.4 42.7 %collective-permute-start.12 = (bf16[3,1792,128]{2,1,0:T(8,128)(2,1)}, bf16[3,1792,128]{2,1,0:T(8,128)(2,1)}, u32[]{:S(2)}, u32[]{:S(2)}) collective-permute-start(bf16[3,1792,128]{2,1,0:T(8,128)(2,1)} %pad_maximum_fusion), channel_id=1, source_target_pairs={{0,480},{32,448},{64,416},{96,384},{128,352},{160,320},{192,288},{... | collective-permute-start | bytes 4128776 | tf_op jit(solution)/shard_map/ppermute | solution.py:19
  188.1 14.3 %copy-start.12 = (f32[1792,128]{1,0:T(8,128)S(1)}, f32[1792,128]{1,0:T(8,128)}, u32[]{:S(2)}) copy-start(f32[1792,128]{1,0:T(8,128)} %fusion.30) | copy-start | bytes 2752516
  191.2 26.0 %copy-start.16 = (bf16[1,1792,128]{2,1,0:T(8,128)(2,1)S(1)}, bf16[1,1792,128]{2,1,0:T(8,128)(2,1)}, u32[]{:S(2)}) copy-start(bf16[1,1792,128]{2,1,0:T(8,128)(2,1)} %fusion.15) | copy-start | bytes 1376260
  192.2 24.9 %collective-permute-start.9 = (bf16[2,8,3584]{2,1,0:T(8,128)(2,1)S(1)}, bf16[2,8,3584]{2,1,0:T(8,128)(2,1)S(1)}, u32[]{:S(2)}, u32[]{:S(2)}) collective-permute-start(bf16[2,8,3584]{2,1,0:T(8,128)(2,1)S(1)} %get-tuple-element.38), channel_id=1, source_target_pairs={{0,16},{1,17},{2,18},{3,19},{4,20},{5,21},{6,22},{7,23},{8,24},{9,... | collective-permute-start | bytes 344072 | tf_op jit(solution)/shard_map/ppermute | solution.py:13
  204.4 20.4 %collective-permute-start.10 = (bf16[2,8,3584]{2,1,0:T(8,128)(2,1)S(1)}, bf16[2,8,3584]{2,1,0:T(8,128)(2,1)S(1)}, u32[]{:S(2)}, u32[]{:S(2)}) collective-permute-start(bf16[2,8,3584]{2,1,0:T(8,128)(2,1)S(1)} %get-tuple-element.39), channel_id=1, source_target_pairs={{0,8},{1,9},{2,10},{3,11},{4,12},{5,13},{6,14},{7,15},{8,0},{9,1},... | collective-permute-start | bytes 344072 | tf_op jit(solution)/shard_map/ppermute | solution.py:13
  207.5 19.3 %collective-permute-start.11 = (bf16[2,8,3584]{2,1,0:T(8,128)(2,1)S(1)}, bf16[2,8,3584]{2,1,0:T(8,128)(2,1)S(1)}, u32[]{:S(2)}, u32[]{:S(2)}) collective-permute-start(bf16[2,8,3584]{2,1,0:T(8,128)(2,1)S(1)} %get-tuple-element.40), channel_id=1, source_target_pairs={{0,24},{1,25},{2,26},{3,27},{4,28},{5,29},{6,30},{7,31},{8,16},{9,... | collective-permute-start | bytes 344072 | tf_op jit(solution)/shard_map/ppermute | solution.py:13
  (12 other events, 18.0 us)

commit v3 on v2

--- a/solution.py
+++ b/solution.py
@@ -1,6 +1,8 @@
 import jax
 import jax.numpy as jnp
 from jax import lax
+from jax.experimental import pallas as pl
+from jax.experimental.pallas import tpu as pltpu
 from jax.sharding import PartitionSpec as P
 
 SHARING_CARDS = 8
@@ -34,6 +36,76 @@
     target = labels * capacity + within
     matches = target[None, :] == jnp.arange(experts * capacity, dtype=jnp.int32)[:, None]
     return matches.astype(jnp.bfloat16)
+
+
+def forward_kernel(x_ref, gate_a, up_a, down_a, gate_b, up_b, down_b, out_ref):
+    x = x_ref[...]
+    hidden = []
+    for gate_ref, up_ref in ((gate_a, up_a), (gate_b, up_b)):
+        gate_pre = jnp.dot(x, gate_ref[...], preferred_element_type=jnp.float32)
+        up_pre = jnp.dot(x, up_ref[...], preferred_element_type=jnp.float32)
+        hidden.append((gate_pre / (1.0 + jnp.exp(-gate_pre)) * up_pre).astype(jnp.bfloat16))
+    step = 512
+    for start in range(0, out_ref.shape[1], step):
+        cut = slice(start, start + step)
+        total = jnp.dot(hidden[0], down_a[:, cut], preferred_element_type=jnp.float32)
+        total += jnp.dot(hidden[1], down_b[:, cut], preferred_element_type=jnp.float32)
+        out_ref[:, cut] = total.astype(jnp.bfloat16)
+
+
+def forward_block(x, own, partner):
+    rows, width = x.shape
+    units = own[0].shape[1]
+    return pl.pallas_call(
+        forward_kernel,
+        out_shape=jax.ShapeDtypeStruct(x.shape, jnp.bfloat16),
+        in_specs=[pl.BlockSpec(memory_space=pltpu.VMEM)] * 7,
+        out_specs=pl.BlockSpec(memory_space=pltpu.VMEM),
+        cost_estimate=pl.CostEstimate(
+            flops=12 * rows * width * units,
+            bytes_accessed=2 * (2 * rows * width + 6 * width * units),
+            transcendentals=2 * rows * units,
+        ),
+        compiler_params=pltpu.CompilerParams(vmem_limit_bytes=24 * 2**20),
+    )(x, *own, *partner)
+
+
+def backward_kernel(x_ref, g_ref, gate_ref, up_ref, down_ref, parts_ref, gate_grad_ref, up_grad_ref, hidden_ref):
+    x = x_ref[...]
+    gate_pre = jnp.dot(x, gate_ref[...], preferred_element_type=jnp.float32)
+    up_pre = jnp.dot(x, up_ref[...], preferred_element_type=jnp.float32)
+    hidden_grad = dot(g_ref[...], down_ref[...], CONTRACT_LAST)
+    sigma = 1.0 / (1.0 + jnp.exp(-gate_pre))
+    activated = gate_pre * sigma
+    hidden_ref[...] = (activated * up_pre).astype(jnp.bfloat16)
+    gate_grad = (hidden_grad * up_pre * sigma * (1.0 + gate_pre * (1.0 - sigma))).astype(jnp.bfloat16)
+    up_grad = (hidden_grad * activated).astype(jnp.bfloat16)
+    gate_grad_ref[...] = gate_grad
+    up_grad_ref[...] = up_grad
+    step = 512
+    for start in range(0, x_ref.shape[1], step):
+        cut = slice(start, start + step)
+        total = dot(gate_grad, gate_ref[cut, :], CONTRACT_LAST)
+        total += dot(up_grad, up_ref[cut, :], CONTRACT_LAST)
+        parts_ref[:, cut] = total.astype(parts_ref.dtype)
+
+
+def backward_block(x, g, gate, up, down, parts_type):
+    rows, width = x.shape
+    units = gate.shape[1]
+    small = jax.ShapeDtypeStruct((rows, units), jnp.bfloat16)
+    return pl.pallas_call(
+        backward_kernel,
+        out_shape=[jax.ShapeDtypeStruct(x.shape, parts_type), small, small, small],
+        in_specs=[pl.BlockSpec(memory_space=pltpu.VMEM)] * 5,
+        out_specs=[pl.BlockSpec(memory_space=pltpu.VMEM)] * 4,
+        cost_estimate=pl.CostEstimate(
+            flops=10 * rows * width * units,
+            bytes_accessed=2 * (4 * rows * width + 3 * width * units),
+            transcendentals=rows * units,
+        ),
+        compiler_params=pltpu.CompilerParams(vmem_limit_bytes=24 * 2**20),
+    )(x, g, gate, up, down)
 
 
 def on_device(
@@ -89,7 +161,7 @@
             swap(blocks[j], "expert", SHARING_CARDS * order[j]) if j else blocks[j]
             for j in range(experts)
         ]
-        arrived[1:] = after(arrived[1:], partner_gate, partner_up)
+        arrived[1:] = after(arrived[1:], partner_gate)
         return [
             jnp.concatenate([block[i] for block in arrived], axis=0) for i in range(len(row_sets))
         ]
@@ -102,7 +174,7 @@
     )
     rows_own = line_gather(rows_held)
     rows_other = swap(rows_own, "expert", 1)
-    grads_own = line_gather(after(grads_held, rows_own, partner_down))
+    grads_own = line_gather(after(grads_held, rows_own, partner_up, partner_down))
     grads_other = swap(after(grads_own, rows_other), "expert", 1)
     ahead = line_gather(after(ahead_held, grads_own, rows_other))
     ahead = after(ahead, grads_other)
@@ -130,42 +202,16 @@
     def joined(back, i):
         return jnp.concatenate([block[i] for block in back], axis=0)
 
-    def backward_half(rows, grads):
-        gate_pre = dot(rows, gate_weights)
-        up_pre = dot(rows, up_weights)
-        sigma = jax.nn.sigmoid(gate_pre)
-        activated = gate_pre * sigma
-        hidden = (activated * up_pre).astype(jnp.bfloat16)
-        hidden_grad = dot(grads, down_weights, CONTRACT_LAST)
-        gate_grad = (hidden_grad * up_pre * sigma * (1.0 + gate_pre * (1.0 - sigma))).astype(
-            jnp.bfloat16
-        )
-        up_grad = (hidden_grad * activated).astype(jnp.bfloat16)
-        return hidden, gate_grad, up_grad
-
-    def backward_parts(gate_grad, up_grad):
-        return dot(gate_grad, gate_weights, CONTRACT_LAST) + dot(
-            up_grad, up_weights, CONTRACT_LAST
-        )
-
-    def forward_slice(gate_slice, up_slice, down_slice):
-        gate_pre = dot(ahead, gate_slice)
-        up_pre = dot(ahead, up_slice)
-        hidden = (jax.nn.silu(gate_pre) * up_pre).astype(jnp.bfloat16)
-        return dot(hidden, down_slice)
-
-    forward_parts = forward_slice(gate_weights, up_weights, down_weights) + forward_slice(
-        partner_gate, partner_up, partner_down
-    )
-    forward_total = line_sum(forward_parts.astype(jnp.bfloat16).reshape(lines, tall, width))
-
+    forward_parts = forward_block(
+        ahead, (gate_weights, up_weights, down_weights), (partner_gate, partner_up, partner_down)
+    )
+    forward_total = line_sum(forward_parts.reshape(lines, tall, width))
     grads_other = after(grads_other, forward_parts)
-    other = backward_half(rows_other, grads_other)
-    backward_leaving = backward_parts(*other[1:]).astype(jnp.bfloat16)
+    weights = (gate_weights, up_weights, down_weights)
+    backward_leaving, *other = backward_block(rows_other, grads_other, *weights, jnp.bfloat16)
     backward_sent = swap(backward_leaving, "expert", 1)
 
-    own = backward_half(rows_own, grads_own)
-    backward_kept = backward_parts(*own[1:])
+    backward_kept, *own = backward_block(rows_own, grads_own, *weights, jnp.float32)
     backward_sent = after(backward_sent, forward_total)
     backward_pair = (backward_kept + backward_sent.astype(jnp.float32)).astype(jnp.bfloat16)
     backward_total = line_sum(backward_pair.reshape(lines, tall, width))
@@ -179,29 +225,34 @@
 
         y_own, y_other = columns(rows_own), columns(rows_other)
         g_own, g_other = columns(grads_own), columns(grads_other)
-        gate = dot(y_own, own[1], CONTRACT_FIRST) + dot(y_other, other[1], CONTRACT_FIRST)
-        up = dot(y_own, own[2], CONTRACT_FIRST) + dot(y_other, other[2], CONTRACT_FIRST)
-        down = dot(g_own, own[0], CONTRACT_FIRST) + dot(g_other, other[0], CONTRACT_FIRST)
-        return jnp.stack([value.astype(jnp.bfloat16) for value in (gate, up, down)])
-
-    outgoing = mirror(after(partial_of((1 - upper_side) * middle), backward_pair))
+        gate = dot(y_own, own[0], CONTRACT_FIRST) + dot(y_other, other[0], CONTRACT_FIRST)
+        up = dot(y_own, own[1], CONTRACT_FIRST) + dot(y_other, other[1], CONTRACT_FIRST)
+        down = dot(g_own, own[2], CONTRACT_FIRST) + dot(g_other, other[2], CONTRACT_FIRST)
+        return [value.astype(jnp.bfloat16) for value in (gate, up, down)]
+
+    leaving = jnp.stack(partial_of((1 - upper_side) * middle))
+    outgoing = mirror(after(leaving, backward_pair))
     retained = partial_of(upper_side * middle)
 
     back = give_back(forward_total, backward_total)
     forward_back, backward_back = joined(back, 0), joined(back, 1)
+    outgoing = after(outgoing, back[1])
+    gate_result, up_result, down_result = [
+        (kept.astype(jnp.float32) + outgoing[i].astype(jnp.float32)).astype(jnp.bfloat16)
+        for i, kept in enumerate(retained)
+    ]
+    forward_back, backward_back = after([forward_back, backward_back], gate_result, up_result, down_result)
     forward_result = (
         forward_gates[0][:, None] * dot(forward_slots, forward_back, CONTRACT_FIRST)
     ).astype(jnp.bfloat16)
     backward_result = dot(backward_slots, backward_back, CONTRACT_FIRST).astype(jnp.bfloat16)
 
-    outgoing = after(outgoing, back[1])
-    gradients = (retained.astype(jnp.float32) + outgoing.astype(jnp.float32)).astype(jnp.bfloat16)
     return (
         forward_result[None],
         backward_result[None],
-        gradients[0][None],
-        gradients[1][None],
-        gradients[2].T[None],
+        gate_result[None],
+        up_result[None],
+        down_result.T[None],
     )
 
 

time: 230 us -> 229 us (level)
  matrix products: 25.8 us -> 14.8 us
  waiting for transfers between devices: 42.3 us -> 53.3 us
  Pallas kernels: 0 us -> 9.92 us
  starting transfers between devices: 82.5 us -> 77 us
  blocking collectives: 57.4 us -> 53.6 us
  other arithmetic: 11.2 us -> 8.22 us
    dot_general x31 -> x17, matrix products: 25.8 us -> 14.8 us  [dot(): lax.dot_general(left, right, dims, preferred_element_type=jnp.float32)]
    pallas_call x0 -> x3, Pallas kernels: none -> 9.92 us  [the longest x2 7.06 us: backward_block(): pl.pallas_call(backward_kernel, out_shape=[jax.ShapeDtypeStruct(x.shape,...]
    ppermute x12, waiting for transfers between devices: 25.8 us -> 34.4 us  [swap(): return lax.ppermute(value, axis, pairs)]
    ppermute x12, starting transfers between devices: 61.6 us -> 56.4 us  [swap(): return lax.ppermute(value, axis, pairs)]
    unnamed x43 -> x41, local copies, waits for them, and re-layouts: 5.49 us -> 9.94 us
    all_gather x3, blocking collectives: 57.4 us -> 53.6 us  [line_gather(): lax.all_gather(value, 'expert', axis_index_groups=line_groups, tiled=True)]
    ppermute x1, waiting for transfers between devices: 6.75 us -> 10.4 us  [mirror(): return lax.ppermute(value, 'pipe', pairs)]
  transfers between devices with their start and end apart: 15 -> 15, of which waited for: 6 -> 10; matrix products, arithmetic and copies ran while one was open for 12% -> 6% of each run, Pallas kernels for 0% -> 3%
where the time goes in v3:
time: 229 us; the launch traced here: 228 us
  starting transfers between devices  77 us (34%)
  blocking collectives  53.6 us (23%)
  waiting for transfers between devices  53.3 us (23%)
  matrix products  14.8 us (6%)
  local copies, waits for them, and re-layouts  10 us (4%)
  Pallas kernels  9.92 us (4%)
  other arithmetic  8.22 us (4%)
    ppermute x12, starting transfers between devices, swap(): return lax.ppermute(value, axis, pairs)  56.4 us
    all_gather x3, blocking collectives, line_gather(): lax.all_gather(value, 'expert', axis_index_groups=line_groups, tiled=True)  53.6 us
    ppermute x12, waiting for transfers between devices, swap(): return lax.ppermute(value, axis, pairs)  34.4 us
    dot_general x17, matrix products, dot(): lax.dot_general(left, right, dims, preferred_element_type=jnp.float32)  14.8 us
    ppermute x1, starting transfers between devices, mirror(): return lax.ppermute(value, 'pipe', pairs)  11.4 us
    ppermute x1, waiting for transfers between devices, mirror(): return lax.ppermute(value, 'pipe', pairs)  10.4 us
    unnamed x41, local copies, waits for them, and re-layouts  9.94 us
    all_to_all x2, starting transfers between devices, line_sum(): lax.all_to_all(values, 'expert', split_axis=0, concat_axis=0, axis_index_...  9.18 us
  transfers between devices with their start and end apart: 15, of which 10 were waited for; matrix products, arithmetic and copies ran while one was open for 6% of the time, Pallas kernels for 3%

profile of v3, /device:TPU:1, one launch (start us, length us, event | category | flops | bytes accessed | tf_op | source)
XLA Modules:
  0.0 228.0 jit_solution(5225843107261587195)
XLA Ops:
  0.7 5.6 %collective-permute-start.3 = (bf16[3584,128]{1,0:T(8,128)(2,1)}, bf16[3584,128]{1,0:T(8,128)(2,1)S(1)}, u32[]{:S(2)}, u32[]{:S(2)}) collective-permute-start(bf16[3584,128]{1,0:T(8,128)(2,1)} %bitcast.110), channel_id=1, source_target_pairs={{0,1},{1,0},{2,3},{3,2},{4,5},{5,4},{6,7},{7,6},{8,9},{9,8},{10,11... | collective-permute-start | bytes 2752520 | tf_op jit(solution)/shard_map/ppermute | solution.py:15
  10.2 12.5 %collective-permute-start.2 = (bf16[3,8,3584]{2,1,0:T(8,128)(2,1)S(1)}, bf16[3,8,3584]{2,1,0:T(8,128)(2,1)S(1)}, u32[]{:S(2)}, u32[]{:S(2)}) collective-permute-start(bf16[3,8,3584]{2,1,0:T(8,128)(2,1)S(1)} %get-tuple-element.52), channel_id=1, source_target_pairs={{0,24},{1,25},{2,26},{3,27},{4,28},{5,29},{6,30},{7,31},{8,16},{9,... | collective-permute-start | bytes 516104 | tf_op jit(solution)/shard_map/ppermute | solution.py:15
  22.7 5.2 %collective-permute-start.1 = (bf16[3,8,3584]{2,1,0:T(8,128)(2,1)S(1)}, bf16[3,8,3584]{2,1,0:T(8,128)(2,1)S(1)}, u32[]{:S(2)}, u32[]{:S(2)}) collective-permute-start(bf16[3,8,3584]{2,1,0:T(8,128)(2,1)S(1)} %get-tuple-element.53), channel_id=1, source_target_pairs={{0,8},{1,9},{2,10},{3,11},{4,12},{5,13},{6,14},{7,15},{8,0},{9,1},... | collective-permute-start | bytes 516104 | tf_op jit(solution)/shard_map/ppermute | solution.py:15
  27.9 3.7 %collective-permute-start = (bf16[3,8,3584]{2,1,0:T(8,128)(2,1)S(1)}, bf16[3,8,3584]{2,1,0:T(8,128)(2,1)S(1)}, u32[]{:S(2)}, u32[]{:S(2)}) collective-permute-start(bf16[3,8,3584]{2,1,0:T(8,128)(2,1)S(1)} %get-tuple-element.54), channel_id=1, source_target_pairs={{0,16},{1,17},{2,18},{3,19},{4,20},{5,21},{6,22},{7,23},{8,24},{9,... | collective-permute-start | bytes 516104 | tf_op jit(solution)/shard_map/ppermute | solution.py:15
  33.8 6.4 %collective-permute-done.2 = bf16[3,8,3584]{2,1,0:T(8,128)(2,1)S(1)} collective-permute-done((bf16[3,8,3584]{2,1,0:T(8,128)(2,1)S(1)}, bf16[3,8,3584]{2,1,0:T(8,128)(2,1)S(1)}, u32[]{:S(2)}, u32[]{:S(2)}) %collective-permute-start.2) | collective-permute-done | bytes 172064 | tf_op jit(solution)/shard_map/ppermute | solution.py:15
  42.3 2.4 %collective-permute-done.1 = bf16[3,8,3584]{2,1,0:T(8,128)(2,1)S(1)} collective-permute-done((bf16[3,8,3584]{2,1,0:T(8,128)(2,1)S(1)}, bf16[3,8,3584]{2,1,0:T(8,128)(2,1)S(1)}, u32[]{:S(2)}, u32[]{:S(2)}) %collective-permute-start.1) | collective-permute-done | bytes 172064 | tf_op jit(solution)/shard_map/ppermute | solution.py:15
  44.7 12.6 %collective-permute-done = bf16[3,8,3584]{2,1,0:T(8,128)(2,1)S(1)} collective-permute-done((bf16[3,8,3584]{2,1,0:T(8,128)(2,1)S(1)}, bf16[3,8,3584]{2,1,0:T(8,128)(2,1)S(1)}, u32[]{:S(2)}, u32[]{:S(2)}) %collective-permute-start) | collective-permute-done | bytes 172064 | tf_op jit(solution)/shard_map/ppermute | solution.py:15
  58.3 18.9 %all_gather.9.x_ref = bf16[128,3584]{1,0:T(8,128)(2,1)S(1)} all-gather(bf16[32,3584]{1,0:T(8,128)(2,1)S(1)} %pad_maximum_fusion.3), channel_id=1, replica_groups={{0,2,4,6},{1,3,5,7},{8,10,12,14},{9,11,13,15},{16,18,20,22},{17,19,21,2..., dimensions={0}, use_global_device_ids=true | all-gather | bytes 1146880 | tf_op jit(solution)/shard_map/all_gather | solution.py:170
  79.4 17.7 %all_gather.10.g_ref = bf16[128,3584]{1,0:T(8,128)(2,1)S(1)} all-gather(bf16[32,3584]{1,0:T(8,128)(2,1)S(1)} %pad_maximum_fusion.2), channel_id=1, replica_groups={{0,2,4,6},{1,3,5,7},{8,10,12,14},{9,11,13,15},{16,18,20,22},{17,19,21,2..., dimensions={0}, use_global_device_ids=true | all-gather | bytes 1146880 | tf_op jit(solution)/shard_map/all_gather | solution.py:170
  100.1 2.5 %collective-permute-start.7 = (bf16[128,3584]{1,0:T(8,128)(2,1)S(1)}, bf16[128,3584]{1,0:T(8,128)(2,1)S(1)}, u32[]{:S(2)}, u32[]{:S(2)}) collective-permute-start(bf16[128,3584]{1,0:T(8,128)(2,1)S(1)} %all_gather.10.g_ref), channel_id=1, source_target_pairs={{0,1},{1,0},{2,3},{3,2},{4,5},{5,4},{6,7},{7,6},{8,9},{9,8},{10,11... | collective-permute-start | bytes 2752520 | tf_op jit(solution)/shard_map/ppermute | solution.py:15
  103.6 16.9 %all_gather.11.x_ref = bf16[128,3584]{1,0:T(8,128)(2,1)S(1)} all-gather(bf16[32,3584]{1,0:T(8,128)(2,1)S(1)} %pad_maximum_fusion.1), channel_id=1, replica_groups={{0,2,4,6},{1,3,5,7},{8,10,12,14},{9,11,13,15},{16,18,20,22},{17,19,21,2..., dimensions={0}, use_global_device_ids=true | all-gather | bytes 1146880 | tf_op jit(solution)/shard_map/all_gather | solution.py:170
  122.1 2.9 %shard_map.137 = bf16[128,3584]{1,0:T(8,128)(2,1)S(1)} custom-call(bf16[128,3584]{1,0:T(8,128)(2,1)S(1)} %all_gather.11.x_ref, bf16[3584,128]{1,0:T(8,128)(2,1)S(1)} %bitcast.111, bf16[3584,128]{1,0:T(8,128)(2,1)S(1)} %bitcast.115, bf16[128,3584]{1,0:T(8,128)(2,1)} %bitcast.24.down_a.down_ref, bf16[3584,128]{1,0:T(8,128)(2,1)S(1)} %copy-done.16, ...), custom_call_target="tpu_custom_call" | custom-call | flops 704643072 | bytes 7340032 | tf_op jit(solution)/shard_map/pallas_call | solution.py:59
  126.0 4.9 %all-to-all-start = ((bf16[4,32,3584]{2,1,0:T(8,128)(2,1)}), bf16[4,32,3584]{2,1,0:T(8,128)(2,1)}, u32[]{:S(2)}, u32[]{:S(2)}) async-start(bf16[4,32,3584]{2,1,0:T(8,128)(2,1)} %bitcast.118), calls=%async_computation | async-start | bytes 1835008 | tf_op jit(solution)/shard_map/all_to_all | solution.py:183
  133.2 4.0 %shard_map.139 = (bf16[128,3584]{1,0:T(8,128)(2,1)}, bf16[128,128]{1,0:T(8,128)(2,1)S(1)}, bf16[128,128]{1,0:T(8,128)(2,1)S(1)}, bf16[128,128]{1,0:T(8,128)(2,1)S(1)}) custom-call(bf16[128,3584]{1,0:T(8,128)(2,1)S(1)} %copy-done.4, bf16[128,3584]{1,0:T(8,128)(2,1)S(1)} %copy-done.11, bf16[3584,128]{1,0:T(8,128)(2,1)S(1)} %bitcast.112, ...), custom_call_target="tpu_custom_call" | custom-call | flops 587202560 | bytes 6422528 | tf_op jit(solution)/shard_map/pallas_call | solution.py:97
  137.2 3.7 %collective-permute-start.8 = (bf16[128,3584]{1,0:T(8,128)(2,1)}, bf16[128,3584]{1,0:T(8,128)(2,1)}, u32[]{:S(2)}, u32[]{:S(2)}) collective-permute-start(bf16[128,3584]{1,0:T(8,128)(2,1)} %get-tuple-element.35), channel_id=1, source_target_pairs={{0,1},{1,0},{2,3},{3,2},{4,5},{5,4},{6,7},{7,6},{8,9},{9,8},{10,11... | collective-permute-start | bytes 2752520 | tf_op jit(solution)/shard_map/ppermute | solution.py:15
  141.0 3.0 %shard_map.138 = (f32[128,3584]{1,0:T(8,128)S(1)}, bf16[128,128]{1,0:T(8,128)(2,1)S(1)}, bf16[128,128]{1,0:T(8,128)(2,1)S(1)}, bf16[128,128]{1,0:T(8,128)(2,1)S(1)}) custom-call(bf16[128,3584]{1,0:T(8,128)(2,1)S(1)} %all_gather.9.x_ref, bf16[128,3584]{1,0:T(8,128)(2,1)S(1)} %copy-done.7, bf16[3584,128]{1,0:T(8,128)(2,1)S(1)} %bitcast.113, ...), custom_call_target="tpu_custom_call" | custom-call | flops 587202560 | bytes 6422528 | tf_op jit(solution)/shard_map/pallas_call | solution.py:97
  145.3 6.1 %all-to-all-done = bf16[4,32,3584]{2,1,0:T(8,128)(2,1)} async-done(((bf16[4,32,3584]{2,1,0:T(8,128)(2,1)}), bf16[4,32,3584]{2,1,0:T(8,128)(2,1)}, u32[]{:S(2)}, u32[]{:S(2)}) %all-to-all-start) | async-done | bytes 917536 | tf_op jit(solution)/shard_map/all_to_all | solution.py:183
  152.7 5.1 %collective-permute-done.8 = bf16[128,3584]{1,0:T(8,128)(2,1)} collective-permute-done((bf16[128,3584]{1,0:T(8,128)(2,1)}, bf16[128,3584]{1,0:T(8,128)(2,1)}, u32[]{:S(2)}, u32[]{:S(2)}) %collective-permute-start.8) | collective-permute-done | bytes 917536 | tf_op jit(solution)/shard_map/ppermute | solution.py:15
  157.8 2.8 %add_convert_fusion = bf16[128,3584]{1,0:T(8,128)(2,1)} fusion(f32[128,3584]{1,0:T(8,128)} %copy-done.14, bf16[128,3584]{1,0:T(8,128)(2,1)} %collective-permute-done.8), kind=kLoop, calls=%fused_computation.32 | loop fusion | flops 1376256 | bytes 3670016 | tf_op jit(solution)/shard_map/convert_element_type | solution.py:216
  160.6 4.3 %all-to-all-start.1 = ((bf16[4,32,3584]{2,1,0:T(8,128)(2,1)}), bf16[4,32,3584]{2,1,0:T(8,128)(2,1)}, u32[]{:S(2)}, u32[]{:S(2)}) async-start(bf16[4,32,3584]{2,1,0:T(8,128)(2,1)} %bitcast.28), calls=%async_computation.1 | async-start | bytes 1835008 | tf_op jit(solution)/shard_map/all_to_all | solution.py:183
  171.2 11.4 %collective-permute-start.12 = (bf16[3,1792,128]{2,1,0:T(8,128)(2,1)}, bf16[3,1792,128]{2,1,0:T(8,128)(2,1)}, u32[]{:S(2)}, u32[]{:S(2)}) collective-permute-start(bf16[3,1792,128]{2,1,0:T(8,128)(2,1)} %pad_maximum_fusion), channel_id=1, source_target_pairs={{0,480},{32,448},{64,416},{96,384},{128,352},{160,320},{192,288},{... | collective-permute-start | bytes 4128776 | tf_op jit(solution)/shard_map/ppermute | solution.py:21
  186.3 12.6 %collective-permute-start.9 = (bf16[2,8,3584]{2,1,0:T(8,128)(2,1)S(1)}, bf16[2,8,3584]{2,1,0:T(8,128)(2,1)S(1)}, u32[]{:S(2)}, u32[]{:S(2)}) collective-permute-start(bf16[2,8,3584]{2,1,0:T(8,128)(2,1)S(1)} %get-tuple-element.55), channel_id=1, source_target_pairs={{0,16},{1,17},{2,18},{3,19},{4,20},{5,21},{6,22},{7,23},{8,24},{9,... | collective-permute-start | bytes 344072 | tf_op jit(solution)/shard_map/ppermute | solution.py:15
  203.5 10.4 %collective-permute-done.12 = bf16[3,1792,128]{2,1,0:T(8,128)(2,1)} collective-permute-done((bf16[3,1792,128]{2,1,0:T(8,128)(2,1)}, bf16[3,1792,128]{2,1,0:T(8,128)(2,1)}, u32[]{:S(2)}, u32[]{:S(2)}) %collective-permute-start.12) | collective-permute-done | bytes 1376288 | tf_op jit(solution)/shard_map/ppermute | solution.py:21
  213.9 5.3 %collective-permute-done.10 = bf16[2,8,3584]{2,1,0:T(8,128)(2,1)S(1)} collective-permute-done((bf16[2,8,3584]{2,1,0:T(8,128)(2,1)S(1)}, bf16[2,8,3584]{2,1,0:T(8,128)(2,1)S(1)}, u32[]{:S(2)}, u32[]{:S(2)}) %collective-permute-start.10) | collective-permute-done | bytes 114720 | tf_op jit(solution)/shard_map/ppermute | solution.py:15
  (101 shorter events, 45.7 us)
Async XLA Ops:
  0.6 7.0 %copy-start = (bf16[1,24,3584]{2,1,0:T(8,128)(2,1)S(1)}, bf16[1,24,3584]{2,1,0:T(8,128)(2,1)}, u32[]{:S(2)}) copy-start(bf16[1,24,3584]{2,1,0:T(8,128)(2,1)} %param.13) | copy-start | bytes 516100
  0.6 31.0 %copy-start.2 = (bf16[1,3584,128]{2,1,0:T(8,128)(2,1)S(1)}, bf16[1,3584,128]{2,1,0:T(8,128)(2,1)}, u32[]{:S(2)}) copy-start(bf16[1,3584,128]{2,1,0:T(8,128)(2,1)} %param.18) | copy-start | bytes 2752516
  0.7 56.7 %collective-permute-start.3 = (bf16[3584,128]{1,0:T(8,128)(2,1)}, bf16[3584,128]{1,0:T(8,128)(2,1)S(1)}, u32[]{:S(2)}, u32[]{:S(2)}) collective-permute-start(bf16[3584,128]{1,0:T(8,128)(2,1)} %bitcast.110), channel_id=1, source_target_pairs={{0,1},{1,0},{2,3},{3,2},{4,5},{5,4},{6,7},{7,6},{8,9},{9,8},{10,11... | collective-permute-start | bytes 2752520 | tf_op jit(solution)/shard_map/ppermute | solution.py:15
  10.2 29.9 %collective-permute-start.2 = (bf16[3,8,3584]{2,1,0:T(8,128)(2,1)S(1)}, bf16[3,8,3584]{2,1,0:T(8,128)(2,1)S(1)}, u32[]{:S(2)}, u32[]{:S(2)}) collective-permute-start(bf16[3,8,3584]{2,1,0:T(8,128)(2,1)S(1)} %get-tuple-element.52), channel_id=1, source_target_pairs={{0,24},{1,25},{2,26},{3,27},{4,28},{5,29},{6,30},{7,31},{8,16},{9,... | collective-permute-start | bytes 516104 | tf_op jit(solution)/shard_map/ppermute | solution.py:15
  22.7 22.0 %collective-permute-start.1 = (bf16[3,8,3584]{2,1,0:T(8,128)(2,1)S(1)}, bf16[3,8,3584]{2,1,0:T(8,128)(2,1)S(1)}, u32[]{:S(2)}, u32[]{:S(2)}) collective-permute-start(bf16[3,8,3584]{2,1,0:T(8,128)(2,1)S(1)} %get-tuple-element.53), channel_id=1, source_target_pairs={{0,8},{1,9},{2,10},{3,11},{4,12},{5,13},{6,14},{7,15},{8,0},{9,1},... | collective-permute-start | bytes 516104 | tf_op jit(solution)/shard_map/ppermute | solution.py:15
  27.9 29.5 %collective-permute-start = (bf16[3,8,3584]{2,1,0:T(8,128)(2,1)S(1)}, bf16[3,8,3584]{2,1,0:T(8,128)(2,1)S(1)}, u32[]{:S(2)}, u32[]{:S(2)}) collective-permute-start(bf16[3,8,3584]{2,1,0:T(8,128)(2,1)S(1)} %get-tuple-element.54), channel_id=1, source_target_pairs={{0,16},{1,17},{2,18},{3,19},{4,20},{5,21},{6,22},{7,23},{8,24},{9,... | collective-permute-start | bytes 516104 | tf_op jit(solution)/shard_map/ppermute | solution.py:15
  31.6 47.8 %collective-permute-start.4 = (bf16[3584,128]{1,0:T(8,128)(2,1)S(1)}, bf16[3584,128]{1,0:T(8,128)(2,1)S(1)}, u32[]{:S(2)}, u32[]{:S(2)}) collective-permute-start(bf16[3584,128]{1,0:T(8,128)(2,1)S(1)} %bitcast.114), channel_id=1, source_target_pairs={{0,1},{1,0},{2,3},{3,2},{4,5},{5,4},{6,7},{7,6},{8,9},{9,8},{10,11... | collective-permute-start | bytes 2752520 | tf_op jit(solution)/shard_map/ppermute | solution.py:15
  40.1 39.3 %collective-permute-start.5 = (bf16[128,3584]{1,0:T(8,128)(2,1)}, bf16[128,3584]{1,0:T(8,128)(2,1)S(1)}, u32[]{:S(2)}, u32[]{:S(2)}) collective-permute-start(bf16[128,3584]{1,0:T(8,128)(2,1)} %bitcast.24.down_a.down_ref), channel_id=1, source_target_pairs={{0,1},{1,0},{2,3},{3,2},{4,5},{5,4},{6,7},{7,6},{8,9},{9,8},{10,11... | collective-permute-start | bytes 2752520 | tf_op jit(solution)/shard_map/ppermute | solution.py:15
  77.2 21.9 %collective-permute-start.6 = (bf16[128,3584]{1,0:T(8,128)(2,1)S(1)}, bf16[128,3584]{1,0:T(8,128)(2,1)S(1)}, u32[]{:S(2)}, u32[]{:S(2)}) collective-permute-start(bf16[128,3584]{1,0:T(8,128)(2,1)S(1)} %all_gather.9.x_ref), channel_id=1, source_target_pairs={{0,1},{1,0},{2,3},{3,2},{4,5},{5,4},{6,7},{7,6},{8,9},{9,8},{10,11... | collective-permute-start | bytes 2752520 | tf_op jit(solution)/shard_map/ppermute | solution.py:15
  79.4 42.7 %copy-start.1 = (bf16[1,3584,128]{2,1,0:T(8,128)(2,1)S(1)}, bf16[1,3584,128]{2,1,0:T(8,128)(2,1)}, u32[]{:S(2)}) copy-start(bf16[1,3584,128]{2,1,0:T(8,128)(2,1)} %param.17) | copy-start | bytes 2752516
  79.4 42.7 %copy-start.16 = (bf16[3584,128]{1,0:T(8,128)(2,1)S(1)}, bf16[3584,128]{1,0:T(8,128)(2,1)}, u32[]{:S(2)}) copy-start(bf16[3584,128]{1,0:T(8,128)(2,1)} %copy-done.15) | copy-start | bytes 2752516
  100.1 21.0 %collective-permute-start.7 = (bf16[128,3584]{1,0:T(8,128)(2,1)S(1)}, bf16[128,3584]{1,0:T(8,128)(2,1)S(1)}, u32[]{:S(2)}, u32[]{:S(2)}) collective-permute-start(bf16[128,3584]{1,0:T(8,128)(2,1)S(1)} %all_gather.10.g_ref), channel_id=1, source_target_pairs={{0,1},{1,0},{2,3},{3,2},{4,5},{5,4},{6,7},{7,6},{8,9},{9,8},{10,11... | collective-permute-start | bytes 2752520 | tf_op jit(solution)/shard_map/ppermute | solution.py:15
  126.0 25.5 %all-to-all-start = ((bf16[4,32,3584]{2,1,0:T(8,128)(2,1)}), bf16[4,32,3584]{2,1,0:T(8,128)(2,1)}, u32[]{:S(2)}, u32[]{:S(2)}) async-start(bf16[4,32,3584]{2,1,0:T(8,128)(2,1)} %bitcast.118), calls=%async_computation | async-start | bytes 1835008 | tf_op jit(solution)/shard_map/all_to_all | solution.py:183
  133.2 7.8 %copy-start.7 = (bf16[128,3584]{1,0:T(8,128)(2,1)S(1)}, bf16[128,3584]{1,0:T(8,128)(2,1)}, u32[]{:S(2)}) copy-start(bf16[128,3584]{1,0:T(8,128)(2,1)} %copy-done.6) | copy-start | bytes 2752516
  137.2 20.6 %collective-permute-start.8 = (bf16[128,3584]{1,0:T(8,128)(2,1)}, bf16[128,3584]{1,0:T(8,128)(2,1)}, u32[]{:S(2)}, u32[]{:S(2)}) collective-permute-start(bf16[128,3584]{1,0:T(8,128)(2,1)} %get-tuple-element.35), channel_id=1, source_target_pairs={{0,1},{1,0},{2,3},{3,2},{4,5},{5,4},{6,7},{7,6},{8,9},{9,8},{10,11... | collective-permute-start | bytes 2752520 | tf_op jit(solution)/shard_map/ppermute | solution.py:15
  160.6 24.3 %all-to-all-start.1 = ((bf16[4,32,3584]{2,1,0:T(8,128)(2,1)}), bf16[4,32,3584]{2,1,0:T(8,128)(2,1)}, u32[]{:S(2)}, u32[]{:S(2)}) async-start(bf16[4,32,3584]{2,1,0:T(8,128)(2,1)} %bitcast.28), calls=%async_computation.1 | async-start | bytes 1835008 | tf_op jit(solution)/shard_map/all_to_all | solution.py:183
  166.5 1.6 copy-start.8
  171.2 42.7 %collective-permute-start.12 = (bf16[3,1792,128]{2,1,0:T(8,128)(2,1)}, bf16[3,1792,128]{2,1,0:T(8,128)(2,1)}, u32[]{:S(2)}, u32[]{:S(2)}) collective-permute-start(bf16[3,1792,128]{2,1,0:T(8,128)(2,1)} %pad_maximum_fusion), channel_id=1, source_target_pairs={{0,480},{32,448},{64,416},{96,384},{128,352},{160,320},{192,288},{... | collective-permute-start | bytes 4128776 | tf_op jit(solution)/shard_map/ppermute | solution.py:21
  186.3 33.0 %copy-start.13 = (bf16[128,3584]{1,0:T(8,128)(2,1)S(1)}, bf16[128,3584]{1,0:T(8,128)(2,1)}, u32[]{:S(2)}) copy-start(bf16[128,3584]{1,0:T(8,128)(2,1)} %copy-done.10) | copy-start | bytes 2752516
  186.3 17.1 %collective-permute-start.9 = (bf16[2,8,3584]{2,1,0:T(8,128)(2,1)S(1)}, bf16[2,8,3584]{2,1,0:T(8,128)(2,1)S(1)}, u32[]{:S(2)}, u32[]{:S(2)}) collective-permute-start(bf16[2,8,3584]{2,1,0:T(8,128)(2,1)S(1)} %get-tuple-element.55), channel_id=1, source_target_pairs={{0,16},{1,17},{2,18},{3,19},{4,20},{5,21},{6,22},{7,23},{8,24},{9,... | collective-permute-start | bytes 344072 | tf_op jit(solution)/shard_map/ppermute | solution.py:15
  199.3 19.9 %collective-permute-start.10 = (bf16[2,8,3584]{2,1,0:T(8,128)(2,1)S(1)}, bf16[2,8,3584]{2,1,0:T(8,128)(2,1)S(1)}, u32[]{:S(2)}, u32[]{:S(2)}) collective-permute-start(bf16[2,8,3584]{2,1,0:T(8,128)(2,1)S(1)} %get-tuple-element.56), channel_id=1, source_target_pairs={{0,8},{1,9},{2,10},{3,11},{4,12},{5,13},{6,14},{7,15},{8,0},{9,1},... | collective-permute-start | bytes 344072 | tf_op jit(solution)/shard_map/ppermute | solution.py:15
  201.5 19.2 %collective-permute-start.11 = (bf16[2,8,3584]{2,1,0:T(8,128)(2,1)S(1)}, bf16[2,8,3584]{2,1,0:T(8,128)(2,1)S(1)}, u32[]{:S(2)}, u32[]{:S(2)}) collective-permute-start(bf16[2,8,3584]{2,1,0:T(8,128)(2,1)S(1)} %get-tuple-element.57), channel_id=1, source_target_pairs={{0,24},{1,25},{2,26},{3,27},{4,28},{5,29},{6,30},{7,31},{8,16},{9,... | collective-permute-start | bytes 344072 | tf_op jit(solution)/shard_map/ppermute | solution.py:15
  220.8 2.2 copy-start.17
  223.0 4.0 %copy-start.19 = (f32[1,24]{1,0:T(1,128)S(1)}, f32[1,24]{1,0:T(1,128)}, u32[]{:S(2)}) copy-start(f32[1,24]{1,0:T(1,128)} %param.12) | copy-start | bytes 292
  (11 other events, 12.4 us)

commit v4 on v2

--- a/solution.py
+++ b/solution.py
@@ -1,6 +1,8 @@
 import jax
 import jax.numpy as jnp
 from jax import lax
+from jax.experimental import pallas as pl
+from jax.experimental.pallas import tpu as pltpu
 from jax.sharding import PartitionSpec as P
 
 SHARING_CARDS = 8
@@ -34,6 +36,38 @@
     target = labels * capacity + within
     matches = target[None, :] == jnp.arange(experts * capacity, dtype=jnp.int32)[:, None]
     return matches.astype(jnp.bfloat16)
+
+
+def forward_kernel(x_ref, gate_a, up_a, down_a, gate_b, up_b, down_b, out_ref):
+    x = x_ref[...]
+    hidden = []
+    for gate_ref, up_ref in ((gate_a, up_a), (gate_b, up_b)):
+        gate_pre = jnp.dot(x, gate_ref[...], preferred_element_type=jnp.float32)
+        up_pre = jnp.dot(x, up_ref[...], preferred_element_type=jnp.float32)
+        hidden.append((gate_pre / (1.0 + jnp.exp(-gate_pre)) * up_pre).astype(jnp.bfloat16))
+    step = 512
+    for start in range(0, out_ref.shape[1], step):
+        cut = slice(start, start + step)
+        total = jnp.dot(hidden[0], down_a[:, cut], preferred_element_type=jnp.float32)
+        total += jnp.dot(hidden[1], down_b[:, cut], preferred_element_type=jnp.float32)
+        out_ref[:, cut] = total.astype(jnp.bfloat16)
+
+
+def forward_block(x, own, partner):
+    rows, width = x.shape
+    units = own[0].shape[1]
+    return pl.pallas_call(
+        forward_kernel,
+        out_shape=jax.ShapeDtypeStruct(x.shape, jnp.bfloat16),
+        in_specs=[pl.BlockSpec(memory_space=pltpu.VMEM)] * 7,
+        out_specs=pl.BlockSpec(memory_space=pltpu.VMEM),
+        cost_estimate=pl.CostEstimate(
+            flops=12 * rows * width * units,
+            bytes_accessed=2 * (2 * rows * width + 6 * width * units),
+            transcendentals=2 * rows * units,
+        ),
+        compiler_params=pltpu.CompilerParams(vmem_limit_bytes=24 * 2**20),
+    )(x, *own, *partner)
 
 
 def on_device(
@@ -89,7 +123,7 @@
             swap(blocks[j], "expert", SHARING_CARDS * order[j]) if j else blocks[j]
             for j in range(experts)
         ]
-        arrived[1:] = after(arrived[1:], partner_gate, partner_up)
+        arrived[1:] = after(arrived[1:], partner_gate)
         return [
             jnp.concatenate([block[i] for block in arrived], axis=0) for i in range(len(row_sets))
         ]
@@ -102,7 +136,7 @@
     )
     rows_own = line_gather(rows_held)
     rows_other = swap(rows_own, "expert", 1)
-    grads_own = line_gather(after(grads_held, rows_own, partner_down))
+    grads_own = line_gather(after(grads_held, rows_own, partner_up, partner_down))
     grads_other = swap(after(grads_own, rows_other), "expert", 1)
     ahead = line_gather(after(ahead_held, grads_own, rows_other))
     ahead = after(ahead, grads_other)
@@ -148,17 +182,10 @@
             up_grad, up_weights, CONTRACT_LAST
         )
 
-    def forward_slice(gate_slice, up_slice, down_slice):
-        gate_pre = dot(ahead, gate_slice)
-        up_pre = dot(ahead, up_slice)
-        hidden = (jax.nn.silu(gate_pre) * up_pre).astype(jnp.bfloat16)
-        return dot(hidden, down_slice)
-
-    forward_parts = forward_slice(gate_weights, up_weights, down_weights) + forward_slice(
-        partner_gate, partner_up, partner_down
-    )
-    forward_total = line_sum(forward_parts.astype(jnp.bfloat16).reshape(lines, tall, width))
-
+    forward_parts = forward_block(
+        ahead, (gate_weights, up_weights, down_weights), (partner_gate, partner_up, partner_down)
+    )
+    forward_total = line_sum(forward_parts.reshape(lines, tall, width))
     grads_other = after(grads_other, forward_parts)
     other = backward_half(rows_other, grads_other)
     backward_leaving = backward_parts(*other[1:]).astype(jnp.bfloat16)

time: 230 us -> 221 us (0.961)
  waiting for transfers between devices: 42.3 us -> 50.1 us
  starting transfers between devices: 82.5 us -> 75.3 us
  matrix products: 25.8 us -> 18.6 us
  local copies, waits for them, and re-layouts: 8.23 us -> 5.38 us
    dot_general x31 -> x27, matrix products: 25.8 us -> 18.6 us  [dot(): lax.dot_general(left, right, dims, preferred_element_type=jnp.float32)]
    all_to_all x2, waiting for transfers between devices: 9.73 us -> 16.5 us  [line_sum(): lax.all_to_all(values, 'expert', split_axis=0, concat_axis=0, axis_index_...]
    ppermute x12, starting transfers between devices: 61.6 us -> 55.9 us  [swap(): return lax.ppermute(value, axis, pairs)]
    ppermute x12, waiting for transfers between devices: 25.8 us -> 30.1 us  [swap(): return lax.ppermute(value, axis, pairs)]
    ppermute x1, waiting for transfers between devices: 6.75 us -> 3.54 us  [mirror(): return lax.ppermute(value, 'pipe', pairs)]
    ppermute x1, starting transfers between devices: 11.7 us -> 8.59 us  [mirror(): return lax.ppermute(value, 'pipe', pairs)]
    unnamed x43 -> x41, local copies, waits for them, and re-layouts: 5.49 us -> 3.03 us
  transfers between devices with their start and end apart: 15 -> 15, of which waited for: 6 -> 7; matrix products, arithmetic and copies ran while one was open for 12% -> 12% of each run, Pallas kernels for 0% -> 0%
where the time goes in v4:
time: 221 us; the launch traced here: 220 us
  starting transfers between devices  75.3 us (34%)
  blocking collectives  58.8 us (27%)
  waiting for transfers between devices  50.1 us (23%)
  matrix products  18.6 us (8%)
  other arithmetic  9.35 us (4%)
  local copies, waits for them, and re-layouts  5.38 us (2%)
    all_gather x3, blocking collectives, line_gather(): lax.all_gather(value, 'expert', axis_index_groups=line_groups, tiled=True)  58.8 us
    ppermute x12, starting transfers between devices, swap(): return lax.ppermute(value, axis, pairs)  55.9 us
    ppermute x12, waiting for transfers between devices, swap(): return lax.ppermute(value, axis, pairs)  30.1 us
    dot_general x27, matrix products, dot(): lax.dot_general(left, right, dims, preferred_element_type=jnp.float32)  18.6 us
    all_to_all x2, waiting for transfers between devices, line_sum(): lax.all_to_all(values, 'expert', split_axis=0, concat_axis=0, axis_index_...  16.5 us
    all_to_all x2, starting transfers between devices, line_sum(): lax.all_to_all(values, 'expert', split_axis=0, concat_axis=0, axis_index_...  10.7 us
    ppermute x1, starting transfers between devices, mirror(): return lax.ppermute(value, 'pipe', pairs)  8.59 us
  transfers between devices with their start and end apart: 15, of which 7 were waited for; matrix products, arithmetic and copies ran while one was open for 12% of the time, Pallas kernels for 0%

profile of v4, /device:TPU:1, one launch (start us, length us, event | category | flops | bytes accessed | tf_op | source)
XLA Modules:
  0.0 220.5 jit_solution(17050146391769574822)
XLA Ops:
  0.7 5.6 %collective-permute-start.3 = (bf16[3584,128]{1,0:T(8,128)(2,1)}, bf16[3584,128]{1,0:T(8,128)(2,1)S(1)}, u32[]{:S(2)}, u32[]{:S(2)}) collective-permute-start(bf16[3584,128]{1,0:T(8,128)(2,1)} %bitcast.142), channel_id=1, source_target_pairs={{0,1},{1,0},{2,3},{3,2},{4,5},{5,4},{6,7},{7,6},{8,9},{9,8},{10,11... | collective-permute-start | bytes 2752520 | tf_op jit(solution)/shard_map/ppermute | solution.py:15
  10.2 15.4 %collective-permute-start = (bf16[3,8,3584]{2,1,0:T(8,128)(2,1)S(1)}, bf16[3,8,3584]{2,1,0:T(8,128)(2,1)S(1)}, u32[]{:S(2)}, u32[]{:S(2)}) collective-permute-start(bf16[3,8,3584]{2,1,0:T(8,128)(2,1)S(1)} %get-tuple-element.37), channel_id=1, source_target_pairs={{0,16},{1,17},{2,18},{3,19},{4,20},{5,21},{6,22},{7,23},{8,24},{9,... | collective-permute-start | bytes 516104 | tf_op jit(solution)/shard_map/ppermute | solution.py:15
  25.7 4.0 %collective-permute-start.1 = (bf16[3,8,3584]{2,1,0:T(8,128)(2,1)S(1)}, bf16[3,8,3584]{2,1,0:T(8,128)(2,1)S(1)}, u32[]{:S(2)}, u32[]{:S(2)}) collective-permute-start(bf16[3,8,3584]{2,1,0:T(8,128)(2,1)S(1)} %get-tuple-element.36), channel_id=1, source_target_pairs={{0,8},{1,9},{2,10},{3,11},{4,12},{5,13},{6,14},{7,15},{8,0},{9,1},... | collective-permute-start | bytes 516104 | tf_op jit(solution)/shard_map/ppermute | solution.py:15
  29.7 1.9 collective-permute-start.2
  31.6 2.1 collective-permute-start.4
  33.8 4.7 %collective-permute-start.5 = (bf16[128,3584]{1,0:T(8,128)(2,1)S(1)}, bf16[128,3584]{1,0:T(8,128)(2,1)S(1)}, u32[]{:S(2)}, u32[]{:S(2)}) collective-permute-start(bf16[128,3584]{1,0:T(8,128)(2,1)S(1)} %bitcast.144), channel_id=1, source_target_pairs={{0,1},{1,0},{2,3},{3,2},{4,5},{5,4},{6,7},{7,6},{8,9},{9,8},{10,11... | collective-permute-start | bytes 2752520 | tf_op jit(solution)/shard_map/ppermute | solution.py:15
  38.5 14.7 %collective-permute-done.1 = bf16[3,8,3584]{2,1,0:T(8,128)(2,1)S(1)} collective-permute-done((bf16[3,8,3584]{2,1,0:T(8,128)(2,1)S(1)}, bf16[3,8,3584]{2,1,0:T(8,128)(2,1)S(1)}, u32[]{:S(2)}, u32[]{:S(2)}) %collective-permute-start.1) | collective-permute-done | bytes 172064 | tf_op jit(solution)/shard_map/ppermute | solution.py:15
  54.1 20.6 %all_gather.9 = bf16[128,3584]{1,0:T(8,128)(2,1)S(1)} all-gather(bf16[32,3584]{1,0:T(8,128)(2,1)S(1)} %pad_maximum_fusion.3), channel_id=1, replica_groups={{0,2,4,6},{1,3,5,7},{8,10,12,14},{9,11,13,15},{16,18,20,22},{17,19,21,2..., dimensions={0}, use_global_device_ids=true | all-gather | bytes 1146880 | tf_op jit(solution)/shard_map/all_gather | solution.py:132
  74.7 2.2 collective-permute-start.6
  77.0 17.9 %all_gather.10 = bf16[128,3584]{1,0:T(8,128)(2,1)S(1)} all-gather(bf16[32,3584]{1,0:T(8,128)(2,1)S(1)} %pad_maximum_fusion.2), channel_id=1, replica_groups={{0,2,4,6},{1,3,5,7},{8,10,12,14},{9,11,13,15},{16,18,20,22},{17,19,21,2..., dimensions={0}, use_global_device_ids=true | all-gather | bytes 1146880 | tf_op jit(solution)/shard_map/all_gather | solution.py:132
  94.8 2.8 %collective-permute-done.6 = bf16[128,3584]{1,0:T(8,128)(2,1)S(1)} collective-permute-done((bf16[128,3584]{1,0:T(8,128)(2,1)S(1)}, bf16[128,3584]{1,0:T(8,128)(2,1)S(1)}, u32[]{:S(2)}, u32[]{:S(2)}) %collective-permute-start.6) | collective-permute-done | bytes 917536 | tf_op jit(solution)/shard_map/ppermute | solution.py:15
  99.6 20.3 %all_gather.11.x_ref = bf16[128,3584]{1,0:T(8,128)(2,1)S(1)} all-gather(bf16[32,3584]{1,0:T(8,128)(2,1)S(1)} %pad_maximum_fusion.1), channel_id=1, replica_groups={{0,2,4,6},{1,3,5,7},{8,10,12,14},{9,11,13,15},{16,18,20,22},{17,19,21,2..., dimensions={0}, use_global_device_ids=true | all-gather | bytes 1146880 | tf_op jit(solution)/shard_map/all_gather | solution.py:132
  122.5 6.4 %all-to-all-start = ((bf16[4,32,3584]{2,1,0:T(8,128)(2,1)}), bf16[4,32,3584]{2,1,0:T(8,128)(2,1)}, u32[]{:S(2)}, u32[]{:S(2)}) async-start(bf16[4,32,3584]{2,1,0:T(8,128)(2,1)} %bitcast.146), calls=%async_computation | async-start | bytes 1835008 | tf_op jit(solution)/shard_map/all_to_all | solution.py:145
  138.4 12.6 %all-to-all-done = bf16[4,32,3584]{2,1,0:T(8,128)(2,1)} async-done(((bf16[4,32,3584]{2,1,0:T(8,128)(2,1)}), bf16[4,32,3584]{2,1,0:T(8,128)(2,1)}, u32[]{:S(2)}, u32[]{:S(2)}) %all-to-all-start) | async-done | bytes 917536 | tf_op jit(solution)/shard_map/all_to_all | solution.py:145
  152.3 5.1 %collective-permute-done.8 = bf16[128,3584]{1,0:T(8,128)(2,1)} collective-permute-done((bf16[128,3584]{1,0:T(8,128)(2,1)}, bf16[128,3584]{1,0:T(8,128)(2,1)}, u32[]{:S(2)}, u32[]{:S(2)}) %collective-permute-start.8) | collective-permute-done | bytes 917536 | tf_op jit(solution)/shard_map/ppermute | solution.py:15
  157.3 2.3 %add_convert_fusion.1 = bf16[128,3584]{1,0:T(8,128)(2,1)} fusion(f32[128,3584]{1,0:T(8,128)S(1)} %convolution_add_fusion.1, bf16[128,3584]{1,0:T(8,128)(2,1)} %collective-permute-done.8), kind=kLoop, calls=%fused_computation.30 | loop fusion | flops 1376256 | bytes 3670016 | tf_op jit(solution)/shard_map/convert_element_type | solution.py:197
  159.6 4.4 %all-to-all-start.1 = ((bf16[4,32,3584]{2,1,0:T(8,128)(2,1)}), bf16[4,32,3584]{2,1,0:T(8,128)(2,1)}, u32[]{:S(2)}, u32[]{:S(2)}) async-start(bf16[4,32,3584]{2,1,0:T(8,128)(2,1)} %bitcast.147), calls=%async_computation.1 | async-start | bytes 1835008 | tf_op jit(solution)/shard_map/all_to_all | solution.py:145
  168.8 8.6 %collective-permute-start.12 = (bf16[3,1792,128]{2,1,0:T(8,128)(2,1)}, bf16[3,1792,128]{2,1,0:T(8,128)(2,1)}, u32[]{:S(2)}, u32[]{:S(2)}) collective-permute-start(bf16[3,1792,128]{2,1,0:T(8,128)(2,1)} %pad_maximum_fusion), channel_id=1, source_target_pairs={{0,480},{32,448},{64,416},{96,384},{128,352},{160,320},{192,288},{... | collective-permute-start | bytes 4128776 | tf_op jit(solution)/shard_map/ppermute | solution.py:21
  180.7 3.9 %all-to-all-done.1 = bf16[4,32,3584]{2,1,0:T(8,128)(2,1)} async-done(((bf16[4,32,3584]{2,1,0:T(8,128)(2,1)}), bf16[4,32,3584]{2,1,0:T(8,128)(2,1)}, u32[]{:S(2)}, u32[]{:S(2)}) %all-to-all-start.1) | async-done | bytes 917536 | tf_op jit(solution)/shard_map/all_to_all | solution.py:145
  185.9 9.7 %collective-permute-start.9 = (bf16[2,8,3584]{2,1,0:T(8,128)(2,1)S(1)}, bf16[2,8,3584]{2,1,0:T(8,128)(2,1)S(1)}, u32[]{:S(2)}, u32[]{:S(2)}) collective-permute-start(bf16[2,8,3584]{2,1,0:T(8,128)(2,1)S(1)} %get-tuple-element.38), channel_id=1, source_target_pairs={{0,16},{1,17},{2,18},{3,19},{4,20},{5,21},{6,22},{7,23},{8,24},{9,... | collective-permute-start | bytes 344072 | tf_op jit(solution)/shard_map/ppermute | solution.py:15
  197.3 3.0 %collective-permute-start.10 = (bf16[2,8,3584]{2,1,0:T(8,128)(2,1)S(1)}, bf16[2,8,3584]{2,1,0:T(8,128)(2,1)S(1)}, u32[]{:S(2)}, u32[]{:S(2)}) collective-permute-start(bf16[2,8,3584]{2,1,0:T(8,128)(2,1)S(1)} %get-tuple-element.39), channel_id=1, source_target_pairs={{0,8},{1,9},{2,10},{3,11},{4,12},{5,13},{6,14},{7,15},{8,0},{9,1},... | collective-permute-start | bytes 344072 | tf_op jit(solution)/shard_map/ppermute | solution.py:15
  200.3 3.4 %collective-permute-start.11 = (bf16[2,8,3584]{2,1,0:T(8,128)(2,1)S(1)}, bf16[2,8,3584]{2,1,0:T(8,128)(2,1)S(1)}, u32[]{:S(2)}, u32[]{:S(2)}) collective-permute-start(bf16[2,8,3584]{2,1,0:T(8,128)(2,1)S(1)} %get-tuple-element.40), channel_id=1, source_target_pairs={{0,24},{1,25},{2,26},{3,27},{4,28},{5,29},{6,30},{7,31},{8,16},{9,... | collective-permute-start | bytes 344072 | tf_op jit(solution)/shard_map/ppermute | solution.py:15
  203.7 3.5 %collective-permute-done.12 = bf16[3,1792,128]{2,1,0:T(8,128)(2,1)} collective-permute-done((bf16[3,1792,128]{2,1,0:T(8,128)(2,1)}, bf16[3,1792,128]{2,1,0:T(8,128)(2,1)}, u32[]{:S(2)}, u32[]{:S(2)}) %collective-permute-start.12) | collective-permute-done | bytes 1376288 | tf_op jit(solution)/shard_map/ppermute | solution.py:21
  209.0 7.6 %collective-permute-done.10 = bf16[2,8,3584]{2,1,0:T(8,128)(2,1)S(1)} collective-permute-done((bf16[2,8,3584]{2,1,0:T(8,128)(2,1)S(1)}, bf16[2,8,3584]{2,1,0:T(8,128)(2,1)S(1)}, u32[]{:S(2)}, u32[]{:S(2)}) %collective-permute-start.10) | collective-permute-done | bytes 114720 | tf_op jit(solution)/shard_map/ppermute | solution.py:15
  (109 shorter events, 36.6 us)
Async XLA Ops:
  0.6 7.0 %copy-start = (bf16[1,24,3584]{2,1,0:T(8,128)(2,1)S(1)}, bf16[1,24,3584]{2,1,0:T(8,128)(2,1)}, u32[]{:S(2)}) copy-start(bf16[1,24,3584]{2,1,0:T(8,128)(2,1)} %param.13) | copy-start | bytes 516100
  0.6 31.0 %copy-start.1 = (bf16[1,3584,128]{2,1,0:T(8,128)(2,1)S(1)}, bf16[1,3584,128]{2,1,0:T(8,128)(2,1)}, u32[]{:S(2)}) copy-start(bf16[1,3584,128]{2,1,0:T(8,128)(2,1)} %param.18) | copy-start | bytes 2752516
  0.7 33.1 %copy-start.3 = (bf16[1,128,3584]{2,1,0:T(8,128)(2,1)S(1)}, bf16[1,128,3584]{2,1,0:T(8,128)(2,1)}, u32[]{:S(2)}) copy-start(bf16[1,128,3584]{2,1,0:T(8,128)(2,1)} %param.19) | copy-start | bytes 2752516
  0.7 52.5 %collective-permute-start.3 = (bf16[3584,128]{1,0:T(8,128)(2,1)}, bf16[3584,128]{1,0:T(8,128)(2,1)S(1)}, u32[]{:S(2)}, u32[]{:S(2)}) collective-permute-start(bf16[3584,128]{1,0:T(8,128)(2,1)} %bitcast.142), channel_id=1, source_target_pairs={{0,1},{1,0},{2,3},{3,2},{4,5},{5,4},{6,7},{7,6},{8,9},{9,8},{10,11... | collective-permute-start | bytes 2752520 | tf_op jit(solution)/shard_map/ppermute | solution.py:15
  10.2 23.6 %collective-permute-start = (bf16[3,8,3584]{2,1,0:T(8,128)(2,1)S(1)}, bf16[3,8,3584]{2,1,0:T(8,128)(2,1)S(1)}, u32[]{:S(2)}, u32[]{:S(2)}) collective-permute-start(bf16[3,8,3584]{2,1,0:T(8,128)(2,1)S(1)} %get-tuple-element.37), channel_id=1, source_target_pairs={{0,16},{1,17},{2,18},{3,19},{4,20},{5,21},{6,22},{7,23},{8,24},{9,... | collective-permute-start | bytes 516104 | tf_op jit(solution)/shard_map/ppermute | solution.py:15
  25.7 27.5 %collective-permute-start.1 = (bf16[3,8,3584]{2,1,0:T(8,128)(2,1)S(1)}, bf16[3,8,3584]{2,1,0:T(8,128)(2,1)S(1)}, u32[]{:S(2)}, u32[]{:S(2)}) collective-permute-start(bf16[3,8,3584]{2,1,0:T(8,128)(2,1)S(1)} %get-tuple-element.36), channel_id=1, source_target_pairs={{0,8},{1,9},{2,10},{3,11},{4,12},{5,13},{6,14},{7,15},{8,0},{9,1},... | collective-permute-start | bytes 516104 | tf_op jit(solution)/shard_map/ppermute | solution.py:15
  29.7 23.4 %collective-permute-start.2 = (bf16[3,8,3584]{2,1,0:T(8,128)(2,1)S(1)}, bf16[3,8,3584]{2,1,0:T(8,128)(2,1)S(1)}, u32[]{:S(2)}, u32[]{:S(2)}) collective-permute-start(bf16[3,8,3584]{2,1,0:T(8,128)(2,1)S(1)} %get-tuple-element.35), channel_id=1, source_target_pairs={{0,24},{1,25},{2,26},{3,27},{4,28},{5,29},{6,30},{7,31},{8,16},{9,... | collective-permute-start | bytes 516104 | tf_op jit(solution)/shard_map/ppermute | solution.py:15
  31.6 45.3 %collective-permute-start.4 = (bf16[3584,128]{1,0:T(8,128)(2,1)S(1)}, bf16[3584,128]{1,0:T(8,128)(2,1)S(1)}, u32[]{:S(2)}, u32[]{:S(2)}) collective-permute-start(bf16[3584,128]{1,0:T(8,128)(2,1)S(1)} %bitcast.140), channel_id=1, source_target_pairs={{0,1},{1,0},{2,3},{3,2},{4,5},{5,4},{6,7},{7,6},{8,9},{9,8},{10,11... | collective-permute-start | bytes 2752520 | tf_op jit(solution)/shard_map/ppermute | solution.py:15
  33.8 43.1 %collective-permute-start.5 = (bf16[128,3584]{1,0:T(8,128)(2,1)S(1)}, bf16[128,3584]{1,0:T(8,128)(2,1)S(1)}, u32[]{:S(2)}, u32[]{:S(2)}) collective-permute-start(bf16[128,3584]{1,0:T(8,128)(2,1)S(1)} %bitcast.144), channel_id=1, source_target_pairs={{0,1},{1,0},{2,3},{3,2},{4,5},{5,4},{6,7},{7,6},{8,9},{9,8},{10,11... | collective-permute-start | bytes 2752520 | tf_op jit(solution)/shard_map/ppermute | solution.py:15
  74.7 45.2 %copy-start.7 = (bf16[128,3584]{1,0:T(8,128)(2,1)}, bf16[128,3584]{1,0:T(8,128)(2,1)S(1)}, u32[]{:S(2)}) copy-start(bf16[128,3584]{1,0:T(8,128)(2,1)S(1)} %all_gather.9) | copy-start | bytes 2752516
  74.7 45.2 %copy-start.2 = (bf16[1,3584,128]{2,1,0:T(8,128)(2,1)S(1)}, bf16[1,3584,128]{2,1,0:T(8,128)(2,1)}, u32[]{:S(2)}) copy-start(bf16[1,3584,128]{2,1,0:T(8,128)(2,1)} %param.17) | copy-start | bytes 2752516
  74.7 45.2 %copy-start.6 = (bf16[3584,128]{1,0:T(8,128)(2,1)S(1)}, bf16[3584,128]{1,0:T(8,128)(2,1)}, u32[]{:S(2)}) copy-start(bf16[3584,128]{1,0:T(8,128)(2,1)} %copy-done.5) | copy-start | bytes 2752516
  74.7 22.9 %collective-permute-start.6 = (bf16[128,3584]{1,0:T(8,128)(2,1)S(1)}, bf16[128,3584]{1,0:T(8,128)(2,1)S(1)}, u32[]{:S(2)}, u32[]{:S(2)}) collective-permute-start(bf16[128,3584]{1,0:T(8,128)(2,1)S(1)} %all_gather.9), channel_id=1, source_target_pairs={{0,1},{1,0},{2,3},{3,2},{4,5},{5,4},{6,7},{7,6},{8,9},{9,8},{10,11... | collective-permute-start | bytes 2752520 | tf_op jit(solution)/shard_map/ppermute | solution.py:15
  94.8 25.0 %copy-start.13 = (bf16[128,3584]{1,0:T(8,128)(2,1)}, bf16[128,3584]{1,0:T(8,128)(2,1)S(1)}, u32[]{:S(2)}) copy-start(bf16[128,3584]{1,0:T(8,128)(2,1)S(1)} %all_gather.10) | copy-start | bytes 2752516
  97.6 22.3 %copy-start.10 = (bf16[128,3584]{1,0:T(8,128)(2,1)}, bf16[128,3584]{1,0:T(8,128)(2,1)S(1)}, u32[]{:S(2)}) copy-start(bf16[128,3584]{1,0:T(8,128)(2,1)S(1)} %collective-permute-done.6) | copy-start | bytes 2752516
  97.6 22.3 %collective-permute-start.7 = (bf16[128,3584]{1,0:T(8,128)(2,1)S(1)}, bf16[128,3584]{1,0:T(8,128)(2,1)}, u32[]{:S(2)}, u32[]{:S(2)}) collective-permute-start(bf16[128,3584]{1,0:T(8,128)(2,1)S(1)} %all_gather.10), channel_id=1, source_target_pairs={{0,1},{1,0},{2,3},{3,2},{4,5},{5,4},{6,7},{7,6},{8,9},{9,8},{10,11... | collective-permute-start | bytes 2752520 | tf_op jit(solution)/shard_map/ppermute | solution.py:15
  122.5 28.4 %all-to-all-start = ((bf16[4,32,3584]{2,1,0:T(8,128)(2,1)}), bf16[4,32,3584]{2,1,0:T(8,128)(2,1)}, u32[]{:S(2)}, u32[]{:S(2)}) async-start(bf16[4,32,3584]{2,1,0:T(8,128)(2,1)} %bitcast.146), calls=%async_computation | async-start | bytes 1835008 | tf_op jit(solution)/shard_map/all_to_all | solution.py:145
  135.2 22.1 %collective-permute-start.8 = (bf16[128,3584]{1,0:T(8,128)(2,1)}, bf16[128,3584]{1,0:T(8,128)(2,1)}, u32[]{:S(2)}, u32[]{:S(2)}) collective-permute-start(bf16[128,3584]{1,0:T(8,128)(2,1)} %fusion), channel_id=1, source_target_pairs={{0,1},{1,0},{2,3},{3,2},{4,5},{5,4},{6,7},{7,6},{8,9},{9,8},{10,11... | collective-permute-start | bytes 2752520 | tf_op jit(solution)/shard_map/ppermute | solution.py:15
  159.6 24.9 %all-to-all-start.1 = ((bf16[4,32,3584]{2,1,0:T(8,128)(2,1)}), bf16[4,32,3584]{2,1,0:T(8,128)(2,1)}, u32[]{:S(2)}, u32[]{:S(2)}) async-start(bf16[4,32,3584]{2,1,0:T(8,128)(2,1)} %bitcast.147), calls=%async_computation.1 | async-start | bytes 1835008 | tf_op jit(solution)/shard_map/all_to_all | solution.py:145
  168.8 38.5 %collective-permute-start.12 = (bf16[3,1792,128]{2,1,0:T(8,128)(2,1)}, bf16[3,1792,128]{2,1,0:T(8,128)(2,1)}, u32[]{:S(2)}, u32[]{:S(2)}) collective-permute-start(bf16[3,1792,128]{2,1,0:T(8,128)(2,1)} %pad_maximum_fusion), channel_id=1, source_target_pairs={{0,480},{32,448},{64,416},{96,384},{128,352},{160,320},{192,288},{... | collective-permute-start | bytes 4128776 | tf_op jit(solution)/shard_map/ppermute | solution.py:21
  180.3 15.3 %copy-start.16 = (f32[1792,128]{1,0:T(8,128)S(1)}, f32[1792,128]{1,0:T(8,128)}, u32[]{:S(2)}) copy-start(f32[1792,128]{1,0:T(8,128)} %fusion.30) | copy-start | bytes 2752516
  185.9 21.3 %collective-permute-start.9 = (bf16[2,8,3584]{2,1,0:T(8,128)(2,1)S(1)}, bf16[2,8,3584]{2,1,0:T(8,128)(2,1)S(1)}, u32[]{:S(2)}, u32[]{:S(2)}) collective-permute-start(bf16[2,8,3584]{2,1,0:T(8,128)(2,1)S(1)} %get-tuple-element.38), channel_id=1, source_target_pairs={{0,16},{1,17},{2,18},{3,19},{4,20},{5,21},{6,22},{7,23},{8,24},{9,... | collective-permute-start | bytes 344072 | tf_op jit(solution)/shard_map/ppermute | solution.py:15
  197.3 19.3 %collective-permute-start.10 = (bf16[2,8,3584]{2,1,0:T(8,128)(2,1)S(1)}, bf16[2,8,3584]{2,1,0:T(8,128)(2,1)S(1)}, u32[]{:S(2)}, u32[]{:S(2)}) collective-permute-start(bf16[2,8,3584]{2,1,0:T(8,128)(2,1)S(1)} %get-tuple-element.39), channel_id=1, source_target_pairs={{0,8},{1,9},{2,10},{3,11},{4,12},{5,13},{6,14},{7,15},{8,0},{9,1},... | collective-permute-start | bytes 344072 | tf_op jit(solution)/shard_map/ppermute | solution.py:15
  200.3 18.3 %collective-permute-start.11 = (bf16[2,8,3584]{2,1,0:T(8,128)(2,1)S(1)}, bf16[2,8,3584]{2,1,0:T(8,128)(2,1)S(1)}, u32[]{:S(2)}, u32[]{:S(2)}) collective-permute-start(bf16[2,8,3584]{2,1,0:T(8,128)(2,1)S(1)} %get-tuple-element.40), channel_id=1, source_target_pairs={{0,24},{1,25},{2,26},{3,27},{4,28},{5,29},{6,30},{7,31},{8,16},{9,... | collective-permute-start | bytes 344072 | tf_op jit(solution)/shard_map/ppermute | solution.py:15
  (11 other events, 24.4 us)

commit v5 on v4

--- a/solution.py
+++ b/solution.py
@@ -216,19 +216,21 @@
 
     back = give_back(forward_total, backward_total)
     forward_back, backward_back = joined(back, 0), joined(back, 1)
+    outgoing = after(outgoing, back[1])
+    gradients = (retained.astype(jnp.float32) + outgoing.astype(jnp.float32)).astype(jnp.bfloat16)
+    down_result = gradients[2].T
+    backward_back = after(backward_back, down_result)
     forward_result = (
         forward_gates[0][:, None] * dot(forward_slots, forward_back, CONTRACT_FIRST)
     ).astype(jnp.bfloat16)
     backward_result = dot(backward_slots, backward_back, CONTRACT_FIRST).astype(jnp.bfloat16)
 
-    outgoing = after(outgoing, back[1])
-    gradients = (retained.astype(jnp.float32) + outgoing.astype(jnp.float32)).astype(jnp.bfloat16)
     return (
         forward_result[None],
         backward_result[None],
         gradients[0][None],
         gradients[1][None],
-        gradients[2].T[None],
+        down_result[None],
     )
 
 

time: 221 us -> 222 us (level)
  transfers between devices with their start and end apart: 15 -> 15, of which waited for: 7 -> 7; matrix products, arithmetic and copies ran while one was open for 12% -> 13% of each run, Pallas kernels for 0% -> 0%
where the time goes in v5:
time: 222 us; the launch traced here: 221 us
  starting transfers between devices  75.4 us (34%)
  blocking collectives  58.8 us (26%)
  waiting for transfers between devices  48.2 us (22%)
  matrix products  19.4 us (9%)
  other arithmetic  10.6 us (5%)
  local copies, waits for them, and re-layouts  5.76 us (3%)
    all_gather x3, blocking collectives, line_gather(): lax.all_gather(value, 'expert', axis_index_groups=line_groups, tiled=True)  58.8 us
    ppermute x12, starting transfers between devices, swap(): return lax.ppermute(value, axis, pairs)  56 us
    ppermute x12, waiting for transfers between devices, swap(): return lax.ppermute(value, axis, pairs)  29.9 us
    dot_general x27, matrix products, dot(): lax.dot_general(left, right, dims, preferred_element_type=jnp.float32)  19.4 us
    all_to_all x2, waiting for transfers between devices, line_sum(): lax.all_to_all(values, 'expert', split_axis=0, concat_axis=0, axis_index_...  15.7 us
    all_to_all x2, starting transfers between devices, line_sum(): lax.all_to_all(values, 'expert', split_axis=0, concat_axis=0, axis_index_...  10.8 us
    ppermute x1, starting transfers between devices, mirror(): return lax.ppermute(value, 'pipe', pairs)  8.61 us
  transfers between devices with their start and end apart: 15, of which 7 were waited for; matrix products, arithmetic and copies ran while one was open for 13% of the time, Pallas kernels for 0%

profile of v5, /device:TPU:1, one launch (start us, length us, event | category | flops | bytes accessed | tf_op | source)
XLA Modules:
  0.0 221.0 jit_solution(16648364536987770206)
XLA Ops:
  0.7 5.6 %collective-permute-start.3 = (bf16[3584,128]{1,0:T(8,128)(2,1)}, bf16[3584,128]{1,0:T(8,128)(2,1)S(1)}, u32[]{:S(2)}, u32[]{:S(2)}) collective-permute-start(bf16[3584,128]{1,0:T(8,128)(2,1)} %bitcast.143), channel_id=1, source_target_pairs={{0,1},{1,0},{2,3},{3,2},{4,5},{5,4},{6,7},{7,6},{8,9},{9,8},{10,11... | collective-permute-start | bytes 2752520 | tf_op jit(solution)/shard_map/ppermute | solution.py:15
  10.2 15.4 %collective-permute-start = (bf16[3,8,3584]{2,1,0:T(8,128)(2,1)S(1)}, bf16[3,8,3584]{2,1,0:T(8,128)(2,1)S(1)}, u32[]{:S(2)}, u32[]{:S(2)}) collective-permute-start(bf16[3,8,3584]{2,1,0:T(8,128)(2,1)S(1)} %get-tuple-element.39), channel_id=1, source_target_pairs={{0,16},{1,17},{2,18},{3,19},{4,20},{5,21},{6,22},{7,23},{8,24},{9,... | collective-permute-start | bytes 516104 | tf_op jit(solution)/shard_map/ppermute | solution.py:15
  25.7 4.0 %collective-permute-start.1 = (bf16[3,8,3584]{2,1,0:T(8,128)(2,1)S(1)}, bf16[3,8,3584]{2,1,0:T(8,128)(2,1)S(1)}, u32[]{:S(2)}, u32[]{:S(2)}) collective-permute-start(bf16[3,8,3584]{2,1,0:T(8,128)(2,1)S(1)} %get-tuple-element.38), channel_id=1, source_target_pairs={{0,8},{1,9},{2,10},{3,11},{4,12},{5,13},{6,14},{7,15},{8,0},{9,1},... | collective-permute-start | bytes 516104 | tf_op jit(solution)/shard_map/ppermute | solution.py:15
  31.6 2.1 collective-permute-start.4
  33.8 4.7 %collective-permute-start.5 = (bf16[128,3584]{1,0:T(8,128)(2,1)S(1)}, bf16[128,3584]{1,0:T(8,128)(2,1)S(1)}, u32[]{:S(2)}, u32[]{:S(2)}) collective-permute-start(bf16[128,3584]{1,0:T(8,128)(2,1)S(1)} %bitcast.145), channel_id=1, source_target_pairs={{0,1},{1,0},{2,3},{3,2},{4,5},{5,4},{6,7},{7,6},{8,9},{9,8},{10,11... | collective-permute-start | bytes 2752520 | tf_op jit(solution)/shard_map/ppermute | solution.py:15
  38.5 14.7 %collective-permute-done.1 = bf16[3,8,3584]{2,1,0:T(8,128)(2,1)S(1)} collective-permute-done((bf16[3,8,3584]{2,1,0:T(8,128)(2,1)S(1)}, bf16[3,8,3584]{2,1,0:T(8,128)(2,1)S(1)}, u32[]{:S(2)}, u32[]{:S(2)}) %collective-permute-start.1) | collective-permute-done | bytes 172064 | tf_op jit(solution)/shard_map/ppermute | solution.py:15
  54.1 20.6 %all_gather.9 = bf16[128,3584]{1,0:T(8,128)(2,1)S(1)} all-gather(bf16[32,3584]{1,0:T(8,128)(2,1)S(1)} %pad_maximum_fusion.3), channel_id=1, replica_groups={{0,2,4,6},{1,3,5,7},{8,10,12,14},{9,11,13,15},{16,18,20,22},{17,19,21,2..., dimensions={0}, use_global_device_ids=true | all-gather | bytes 1146880 | tf_op jit(solution)/shard_map/all_gather | solution.py:132
  74.7 2.2 collective-permute-start.6
  77.0 17.9 %all_gather.10 = bf16[128,3584]{1,0:T(8,128)(2,1)S(1)} all-gather(bf16[32,3584]{1,0:T(8,128)(2,1)S(1)} %pad_maximum_fusion.2), channel_id=1, replica_groups={{0,2,4,6},{1,3,5,7},{8,10,12,14},{9,11,13,15},{16,18,20,22},{17,19,21,2..., dimensions={0}, use_global_device_ids=true | all-gather | bytes 1146880 | tf_op jit(solution)/shard_map/all_gather | solution.py:132
  94.8 2.8 %collective-permute-done.6 = bf16[128,3584]{1,0:T(8,128)(2,1)S(1)} collective-permute-done((bf16[128,3584]{1,0:T(8,128)(2,1)S(1)}, bf16[128,3584]{1,0:T(8,128)(2,1)S(1)}, u32[]{:S(2)}, u32[]{:S(2)}) %collective-permute-start.6) | collective-permute-done | bytes 917536 | tf_op jit(solution)/shard_map/ppermute | solution.py:15
  99.6 20.3 %all_gather.11.x_ref = bf16[128,3584]{1,0:T(8,128)(2,1)S(1)} all-gather(bf16[32,3584]{1,0:T(8,128)(2,1)S(1)} %pad_maximum_fusion.1), channel_id=1, replica_groups={{0,2,4,6},{1,3,5,7},{8,10,12,14},{9,11,13,15},{16,18,20,22},{17,19,21,2..., dimensions={0}, use_global_device_ids=true | all-gather | bytes 1146880 | tf_op jit(solution)/shard_map/all_gather | solution.py:132
  122.5 6.4 %all-to-all-start = ((bf16[4,32,3584]{2,1,0:T(8,128)(2,1)}), bf16[4,32,3584]{2,1,0:T(8,128)(2,1)}, u32[]{:S(2)}, u32[]{:S(2)}) async-start(bf16[4,32,3584]{2,1,0:T(8,128)(2,1)} %bitcast.147), calls=%async_computation | async-start | bytes 1835008 | tf_op jit(solution)/shard_map/all_to_all | solution.py:145
  138.4 12.6 %all-to-all-done = bf16[4,32,3584]{2,1,0:T(8,128)(2,1)} async-done(((bf16[4,32,3584]{2,1,0:T(8,128)(2,1)}), bf16[4,32,3584]{2,1,0:T(8,128)(2,1)}, u32[]{:S(2)}, u32[]{:S(2)}) %all-to-all-start) | async-done | bytes 917536 | tf_op jit(solution)/shard_map/all_to_all | solution.py:145
  150.9 2.1 convert_reduce_fusion
  153.0 4.3 %collective-permute-done.8 = bf16[128,3584]{1,0:T(8,128)(2,1)} collective-permute-done((bf16[128,3584]{1,0:T(8,128)(2,1)}, bf16[128,3584]{1,0:T(8,128)(2,1)}, u32[]{:S(2)}, u32[]{:S(2)}) %collective-permute-start.8) | collective-permute-done | bytes 917536 | tf_op jit(solution)/shard_map/ppermute | solution.py:15
  157.3 2.3 %add_convert_fusion.1 = bf16[128,3584]{1,0:T(8,128)(2,1)} fusion(f32[128,3584]{1,0:T(8,128)S(1)} %convolution_add_fusion.1, bf16[128,3584]{1,0:T(8,128)(2,1)} %collective-permute-done.8), kind=kLoop, calls=%fused_computation.30 | loop fusion | flops 1376256 | bytes 3670016 | tf_op jit(solution)/shard_map/convert_element_type | solution.py:197
  159.6 4.4 %all-to-all-start.1 = ((bf16[4,32,3584]{2,1,0:T(8,128)(2,1)}), bf16[4,32,3584]{2,1,0:T(8,128)(2,1)S(1)}, u32[]{:S(2)}, u32[]{:S(2)}) async-start(bf16[4,32,3584]{2,1,0:T(8,128)(2,1)} %bitcast.148), calls=%async_computation.1 | async-start | bytes 1835008 | tf_op jit(solution)/shard_map/all_to_all | solution.py:145
  168.7 8.6 %collective-permute-start.12 = (bf16[3,1792,128]{2,1,0:T(8,128)(2,1)}, bf16[3,1792,128]{2,1,0:T(8,128)(2,1)}, u32[]{:S(2)}, u32[]{:S(2)}) collective-permute-start(bf16[3,1792,128]{2,1,0:T(8,128)(2,1)} %pad_maximum_fusion), channel_id=1, source_target_pairs={{0,480},{32,448},{64,416},{96,384},{128,352},{160,320},{192,288},{... | collective-permute-start | bytes 4128776 | tf_op jit(solution)/shard_map/ppermute | solution.py:21
  181.4 3.1 %all-to-all-done.1 = bf16[4,32,3584]{2,1,0:T(8,128)(2,1)S(1)} async-done(((bf16[4,32,3584]{2,1,0:T(8,128)(2,1)}), bf16[4,32,3584]{2,1,0:T(8,128)(2,1)S(1)}, u32[]{:S(2)}, u32[]{:S(2)}) %all-to-all-start.1) | async-done | bytes 917536 | tf_op jit(solution)/shard_map/all_to_all | solution.py:145
  186.4 9.7 %collective-permute-start.9 = (bf16[2,8,3584]{2,1,0:T(8,128)(2,1)S(1)}, bf16[2,8,3584]{2,1,0:T(8,128)(2,1)S(1)}, u32[]{:S(2)}, u32[]{:S(2)}) collective-permute-start(bf16[2,8,3584]{2,1,0:T(8,128)(2,1)S(1)} %get-tuple-element.40), channel_id=1, source_target_pairs={{0,16},{1,17},{2,18},{3,19},{4,20},{5,21},{6,22},{7,23},{8,24},{9,... | collective-permute-start | bytes 344072 | tf_op jit(solution)/shard_map/ppermute | solution.py:15
  198.2 3.0 %collective-permute-start.10 = (bf16[2,8,3584]{2,1,0:T(8,128)(2,1)S(1)}, bf16[2,8,3584]{2,1,0:T(8,128)(2,1)S(1)}, u32[]{:S(2)}, u32[]{:S(2)}) collective-permute-start(bf16[2,8,3584]{2,1,0:T(8,128)(2,1)S(1)} %get-tuple-element.41), channel_id=1, source_target_pairs={{0,8},{1,9},{2,10},{3,11},{4,12},{5,13},{6,14},{7,15},{8,0},{9,1},... | collective-permute-start | bytes 344072 | tf_op jit(solution)/shard_map/ppermute | solution.py:15
  201.2 3.4 %collective-permute-start.11 = (bf16[2,8,3584]{2,1,0:T(8,128)(2,1)S(1)}, bf16[2,8,3584]{2,1,0:T(8,128)(2,1)S(1)}, u32[]{:S(2)}, u32[]{:S(2)}) collective-permute-start(bf16[2,8,3584]{2,1,0:T(8,128)(2,1)S(1)} %get-tuple-element.42), channel_id=1, source_target_pairs={{0,24},{1,25},{2,26},{3,27},{4,28},{5,29},{6,30},{7,31},{8,16},{9,... | collective-permute-start | bytes 344072 | tf_op jit(solution)/shard_map/ppermute | solution.py:15
  204.6 2.6 %collective-permute-done.12 = bf16[3,1792,128]{2,1,0:T(8,128)(2,1)} collective-permute-done((bf16[3,1792,128]{2,1,0:T(8,128)(2,1)}, bf16[3,1792,128]{2,1,0:T(8,128)(2,1)}, u32[]{:S(2)}, u32[]{:S(2)}) %collective-permute-start.12) | collective-permute-done | bytes 1376288 | tf_op jit(solution)/shard_map/ppermute | solution.py:21
  209.0 8.2 %collective-permute-done.10 = bf16[2,8,3584]{2,1,0:T(8,128)(2,1)S(1)} collective-permute-done((bf16[2,8,3584]{2,1,0:T(8,128)(2,1)S(1)}, bf16[2,8,3584]{2,1,0:T(8,128)(2,1)S(1)}, u32[]{:S(2)}, u32[]{:S(2)}) %collective-permute-start.10) | collective-permute-done | bytes 114720 | tf_op jit(solution)/shard_map/ppermute | solution.py:15
  (108 shorter events, 38.9 us)
Async XLA Ops:
  0.6 31.0 %copy-start.1 = (bf16[1,3584,128]{2,1,0:T(8,128)(2,1)S(1)}, bf16[1,3584,128]{2,1,0:T(8,128)(2,1)}, u32[]{:S(2)}) copy-start(bf16[1,3584,128]{2,1,0:T(8,128)(2,1)} %param.18) | copy-start | bytes 2752516
  0.7 33.1 %copy-start.3 = (bf16[1,128,3584]{2,1,0:T(8,128)(2,1)S(1)}, bf16[1,128,3584]{2,1,0:T(8,128)(2,1)}, u32[]{:S(2)}) copy-start(bf16[1,128,3584]{2,1,0:T(8,128)(2,1)} %param.19) | copy-start | bytes 2752516
  0.7 52.5 %collective-permute-start.3 = (bf16[3584,128]{1,0:T(8,128)(2,1)}, bf16[3584,128]{1,0:T(8,128)(2,1)S(1)}, u32[]{:S(2)}, u32[]{:S(2)}) collective-permute-start(bf16[3584,128]{1,0:T(8,128)(2,1)} %bitcast.143), channel_id=1, source_target_pairs={{0,1},{1,0},{2,3},{3,2},{4,5},{5,4},{6,7},{7,6},{8,9},{9,8},{10,11... | collective-permute-start | bytes 2752520 | tf_op jit(solution)/shard_map/ppermute | solution.py:15
  10.2 23.6 %collective-permute-start = (bf16[3,8,3584]{2,1,0:T(8,128)(2,1)S(1)}, bf16[3,8,3584]{2,1,0:T(8,128)(2,1)S(1)}, u32[]{:S(2)}, u32[]{:S(2)}) collective-permute-start(bf16[3,8,3584]{2,1,0:T(8,128)(2,1)S(1)} %get-tuple-element.39), channel_id=1, source_target_pairs={{0,16},{1,17},{2,18},{3,19},{4,20},{5,21},{6,22},{7,23},{8,24},{9,... | collective-permute-start | bytes 516104 | tf_op jit(solution)/shard_map/ppermute | solution.py:15
  25.7 27.5 %collective-permute-start.1 = (bf16[3,8,3584]{2,1,0:T(8,128)(2,1)S(1)}, bf16[3,8,3584]{2,1,0:T(8,128)(2,1)S(1)}, u32[]{:S(2)}, u32[]{:S(2)}) collective-permute-start(bf16[3,8,3584]{2,1,0:T(8,128)(2,1)S(1)} %get-tuple-element.38), channel_id=1, source_target_pairs={{0,8},{1,9},{2,10},{3,11},{4,12},{5,13},{6,14},{7,15},{8,0},{9,1},... | collective-permute-start | bytes 516104 | tf_op jit(solution)/shard_map/ppermute | solution.py:15
  29.7 23.4 %collective-permute-start.2 = (bf16[3,8,3584]{2,1,0:T(8,128)(2,1)S(1)}, bf16[3,8,3584]{2,1,0:T(8,128)(2,1)S(1)}, u32[]{:S(2)}, u32[]{:S(2)}) collective-permute-start(bf16[3,8,3584]{2,1,0:T(8,128)(2,1)S(1)} %get-tuple-element.37), channel_id=1, source_target_pairs={{0,24},{1,25},{2,26},{3,27},{4,28},{5,29},{6,30},{7,31},{8,16},{9,... | collective-permute-start | bytes 516104 | tf_op jit(solution)/shard_map/ppermute | solution.py:15
  31.6 45.3 %collective-permute-start.4 = (bf16[3584,128]{1,0:T(8,128)(2,1)S(1)}, bf16[3584,128]{1,0:T(8,128)(2,1)S(1)}, u32[]{:S(2)}, u32[]{:S(2)}) collective-permute-start(bf16[3584,128]{1,0:T(8,128)(2,1)S(1)} %bitcast.141), channel_id=1, source_target_pairs={{0,1},{1,0},{2,3},{3,2},{4,5},{5,4},{6,7},{7,6},{8,9},{9,8},{10,11... | collective-permute-start | bytes 2752520 | tf_op jit(solution)/shard_map/ppermute | solution.py:15
  33.8 43.1 %collective-permute-start.5 = (bf16[128,3584]{1,0:T(8,128)(2,1)S(1)}, bf16[128,3584]{1,0:T(8,128)(2,1)S(1)}, u32[]{:S(2)}, u32[]{:S(2)}) collective-permute-start(bf16[128,3584]{1,0:T(8,128)(2,1)S(1)} %bitcast.145), channel_id=1, source_target_pairs={{0,1},{1,0},{2,3},{3,2},{4,5},{5,4},{6,7},{7,6},{8,9},{9,8},{10,11... | collective-permute-start | bytes 2752520 | tf_op jit(solution)/shard_map/ppermute | solution.py:15
  74.7 45.2 %copy-start.7 = (bf16[128,3584]{1,0:T(8,128)(2,1)}, bf16[128,3584]{1,0:T(8,128)(2,1)S(1)}, u32[]{:S(2)}) copy-start(bf16[128,3584]{1,0:T(8,128)(2,1)S(1)} %all_gather.9) | copy-start | bytes 2752516
  74.7 45.2 %copy-start.2 = (bf16[1,3584,128]{2,1,0:T(8,128)(2,1)S(1)}, bf16[1,3584,128]{2,1,0:T(8,128)(2,1)}, u32[]{:S(2)}) copy-start(bf16[1,3584,128]{2,1,0:T(8,128)(2,1)} %param.17) | copy-start | bytes 2752516
  74.7 45.2 %copy-start.6 = (bf16[3584,128]{1,0:T(8,128)(2,1)S(1)}, bf16[3584,128]{1,0:T(8,128)(2,1)}, u32[]{:S(2)}) copy-start(bf16[3584,128]{1,0:T(8,128)(2,1)} %copy-done.5) | copy-start | bytes 2752516
  74.7 22.9 %collective-permute-start.6 = (bf16[128,3584]{1,0:T(8,128)(2,1)S(1)}, bf16[128,3584]{1,0:T(8,128)(2,1)S(1)}, u32[]{:S(2)}, u32[]{:S(2)}) collective-permute-start(bf16[128,3584]{1,0:T(8,128)(2,1)S(1)} %all_gather.9), channel_id=1, source_target_pairs={{0,1},{1,0},{2,3},{3,2},{4,5},{5,4},{6,7},{7,6},{8,9},{9,8},{10,11... | collective-permute-start | bytes 2752520 | tf_op jit(solution)/shard_map/ppermute | solution.py:15
  94.8 25.0 %copy-start.13 = (bf16[128,3584]{1,0:T(8,128)(2,1)}, bf16[128,3584]{1,0:T(8,128)(2,1)S(1)}, u32[]{:S(2)}) copy-start(bf16[128,3584]{1,0:T(8,128)(2,1)S(1)} %all_gather.10) | copy-start | bytes 2752516
  97.6 22.3 %copy-start.10 = (bf16[128,3584]{1,0:T(8,128)(2,1)}, bf16[128,3584]{1,0:T(8,128)(2,1)S(1)}, u32[]{:S(2)}) copy-start(bf16[128,3584]{1,0:T(8,128)(2,1)S(1)} %collective-permute-done.6) | copy-start | bytes 2752516
  97.6 22.3 %collective-permute-start.7 = (bf16[128,3584]{1,0:T(8,128)(2,1)S(1)}, bf16[128,3584]{1,0:T(8,128)(2,1)}, u32[]{:S(2)}, u32[]{:S(2)}) collective-permute-start(bf16[128,3584]{1,0:T(8,128)(2,1)S(1)} %all_gather.10), channel_id=1, source_target_pairs={{0,1},{1,0},{2,3},{3,2},{4,5},{5,4},{6,7},{7,6},{8,9},{9,8},{10,11... | collective-permute-start | bytes 2752520 | tf_op jit(solution)/shard_map/ppermute | solution.py:15
  122.5 28.4 %all-to-all-start = ((bf16[4,32,3584]{2,1,0:T(8,128)(2,1)}), bf16[4,32,3584]{2,1,0:T(8,128)(2,1)}, u32[]{:S(2)}, u32[]{:S(2)}) async-start(bf16[4,32,3584]{2,1,0:T(8,128)(2,1)} %bitcast.147), calls=%async_computation | async-start | bytes 1835008 | tf_op jit(solution)/shard_map/all_to_all | solution.py:145
  135.2 22.1 %collective-permute-start.8 = (bf16[128,3584]{1,0:T(8,128)(2,1)}, bf16[128,3584]{1,0:T(8,128)(2,1)}, u32[]{:S(2)}, u32[]{:S(2)}) collective-permute-start(bf16[128,3584]{1,0:T(8,128)(2,1)} %fusion), channel_id=1, source_target_pairs={{0,1},{1,0},{2,3},{3,2},{4,5},{5,4},{6,7},{7,6},{8,9},{9,8},{10,11... | collective-permute-start | bytes 2752520 | tf_op jit(solution)/shard_map/ppermute | solution.py:15
  159.6 25.0 %all-to-all-start.1 = ((bf16[4,32,3584]{2,1,0:T(8,128)(2,1)}), bf16[4,32,3584]{2,1,0:T(8,128)(2,1)S(1)}, u32[]{:S(2)}, u32[]{:S(2)}) async-start(bf16[4,32,3584]{2,1,0:T(8,128)(2,1)} %bitcast.148), calls=%async_computation.1 | async-start | bytes 1835008 | tf_op jit(solution)/shard_map/all_to_all | solution.py:145
  168.7 38.5 %collective-permute-start.12 = (bf16[3,1792,128]{2,1,0:T(8,128)(2,1)}, bf16[3,1792,128]{2,1,0:T(8,128)(2,1)}, u32[]{:S(2)}, u32[]{:S(2)}) collective-permute-start(bf16[3,1792,128]{2,1,0:T(8,128)(2,1)} %pad_maximum_fusion), channel_id=1, source_target_pairs={{0,480},{32,448},{64,416},{96,384},{128,352},{160,320},{192,288},{... | collective-permute-start | bytes 4128776 | tf_op jit(solution)/shard_map/ppermute | solution.py:21
  180.3 15.9 %copy-start.16 = (f32[1792,128]{1,0:T(8,128)S(1)}, f32[1792,128]{1,0:T(8,128)}, u32[]{:S(2)}) copy-start(f32[1792,128]{1,0:T(8,128)} %fusion.30) | copy-start | bytes 2752516
  185.4 21.9 %copy-start.17 = (bf16[1,1792,128]{2,1,0:T(8,128)(2,1)S(1)}, bf16[1,1792,128]{2,1,0:T(8,128)(2,1)}, u32[]{:S(2)}) copy-start(bf16[1,1792,128]{2,1,0:T(8,128)(2,1)} %fusion.15) | copy-start | bytes 1376260
  186.4 20.8 %collective-permute-start.9 = (bf16[2,8,3584]{2,1,0:T(8,128)(2,1)S(1)}, bf16[2,8,3584]{2,1,0:T(8,128)(2,1)S(1)}, u32[]{:S(2)}, u32[]{:S(2)}) collective-permute-start(bf16[2,8,3584]{2,1,0:T(8,128)(2,1)S(1)} %get-tuple-element.40), channel_id=1, source_target_pairs={{0,16},{1,17},{2,18},{3,19},{4,20},{5,21},{6,22},{7,23},{8,24},{9,... | collective-permute-start | bytes 344072 | tf_op jit(solution)/shard_map/ppermute | solution.py:15
  198.2 19.0 %collective-permute-start.10 = (bf16[2,8,3584]{2,1,0:T(8,128)(2,1)S(1)}, bf16[2,8,3584]{2,1,0:T(8,128)(2,1)S(1)}, u32[]{:S(2)}, u32[]{:S(2)}) collective-permute-start(bf16[2,8,3584]{2,1,0:T(8,128)(2,1)S(1)} %get-tuple-element.41), channel_id=1, source_target_pairs={{0,8},{1,9},{2,10},{3,11},{4,12},{5,13},{6,14},{7,15},{8,0},{9,1},... | collective-permute-start | bytes 344072 | tf_op jit(solution)/shard_map/ppermute | solution.py:15
  201.2 17.9 %collective-permute-start.11 = (bf16[2,8,3584]{2,1,0:T(8,128)(2,1)S(1)}, bf16[2,8,3584]{2,1,0:T(8,128)(2,1)S(1)}, u32[]{:S(2)}, u32[]{:S(2)}) collective-permute-start(bf16[2,8,3584]{2,1,0:T(8,128)(2,1)S(1)} %get-tuple-element.42), channel_id=1, source_target_pairs={{0,24},{1,25},{2,26},{3,27},{4,28},{5,29},{6,30},{7,31},{8,16},{9,... | collective-permute-start | bytes 344072 | tf_op jit(solution)/shard_map/ppermute | solution.py:15
  (10 other events, 26.4 us)
